TPU v7x, 128 devices: a whole 4x4x4 slice. The times are simulated.
128 devices in a mesh: row: 8 (over y, x_hi), col: 16 (over x_lo, z, core).
Axes of the slice: x: 4 (x_hi: 2, x_lo: 2; x = x_hi * 2 + x_lo), y: 4, z: 4, core: 2. Of those that a mesh axis runs over, the one named last changes fastest.
Arguments:
- left_matrix: float32 [4096, 4096], P('row', 'col'), may hold values from -6 to 6
- right_matrix: float32 [4096, 4096], P('row', 'col'), may hold values from -0.09375 to 0.09375
Outputs:
- product_matrix: float32 [4096, 4096], P('row', 'col')
All inputs are finite; a program needn't handle non-finite values.
Results may differ from a plain program's by a relative error of at most 0.00019.
Values sent between devices are 32-bit elements; how exact they have to be, the bound alone decides.
No kernel may reach another device: no remote copies, remote signals or barrier semaphores. Data moves between devices by JAX's collectives and lax.ppermute only.
A program may use at most 64 MiB of HBM per device.

v0:
```python
import jax
import jax.numpy as jnp
from jax import lax
from jax.sharding import PartitionSpec as P


def copy_for_each(array, axis):
    devices = lax.axis_size(axis)
    return lax.all_to_all(
        jnp.broadcast_to(array[None], (devices, *array.shape)), axis, 0, 0, tiled=True
    )


def joined_along(pieces, dim):
    lengths = list(pieces.shape[1:])
    lengths[dim] *= pieces.shape[0]
    return jnp.moveaxis(pieces, 0, dim).reshape(lengths)


def collect(array, axis, dim):
    pieces = copy_for_each(array, axis)
    return joined_along(pieces, dim)


def multiply(left_term, right_term):
    return jnp.dot(
        left_term, right_term, precision=lax.Precision.HIGHEST, preferred_element_type=jnp.float32
    )


def body(left_matrix, right_matrix):
    row_panel = lax.all_gather(left_matrix, "col", axis=1, tiled=True)
    col_panel = collect(right_matrix, "row", 0)
    return multiply(row_panel, col_panel)


def solution(mesh):
    placed = (P("row", "col"), P("row", "col"))
    return jax.shard_map(
        body, mesh=mesh, in_specs=placed, out_specs=P("row", "col"), check_vma=False
    )
```

profile of v0, /device:TPU:0, one launch (start us, length us, event | category | flops | bytes accessed | tf_op | source)
XLA Modules:
  0.0 123.2 jit_solution(261679742766452399)
XLA Ops:
  6.5 0.0 all-gather.2.cloned.1.call-start
  6.5 0.7 all-gather.2.cloned.1.call-update
  7.3 1.4 %broadcast_in_dim.2 = f32[8,512,256]{2,1,0:T(8,128)S(1)} broadcast(f32[512,256]{1,0:T(8,128)} %param.3), dimensions={1,2} | broadcast | bytes 4718592 | tf_op jit(solution)/shard_map/broadcast_in_dim | solution.py:10
  8.7 97.2 %all_to_all.5 = f32[8,512,256]{2,1,0:T(8,128)} all-to-all(f32[8,512,256]{2,1,0:T(8,128)S(1)} %broadcast_in_dim.2), channel_id=1, replica_groups=mesh['row'=8,'col'=16] {'row'}, dimensions={0} | all-to-all | bytes 8388608 | tf_op jit(solution)/shard_map/all_to_all | solution.py:9
  105.8 0.0 all-gather.2.cloned.1.call-done
  105.8 10.5 %fusion = f32[512,256]{1,0:T(8,128)} fusion(f32[512,4096]{1,0:T(8,128)} %all-gather.2.cloned.1.call-done, f32[4096,256]{1,0:T(8,128)} %bitcast.3), kind=kOutput, calls=%fused_computation | convolution fusion | flops 6442450944 | bytes 13107200 | tf_op jit(solution)/shard_map/dot_general | solution.py:26
Async XLA Ops:
  6.5 99.3 %all-gather.2.cloned.1.call-start = ((), (), s32[]{:S(2)}) async-start(), calls=%async_computation.1 | async-start | bytes 8912896 | tf_op jit(solution)/shard_map/all_gather | solution.py:32
Sparse Core Ops, SparseCore 0:
  9.0 93.1 all-gather.1
where the time goes:
time: 123 us
  blocking collectives  97.2 us (79%)
  between operations  13.4 us (11%)
  matrix products  10.5 us (9%)
  local copies, waits for them, and re-layouts  1.4 us (1%)
    all_to_all x1, blocking collectives, copy_for_each(): lax.all_to_all(jnp.broadcast_to(array[None], (devices, *array.shape)), ax...  97.2 us
    dot_general x1, matrix products, multiply(): jnp.dot(left_term, right_term, precision=lax.Precision.HIGHEST, preferred...  10.5 us
  transfers between devices with their start and end apart: 1, of which 0 were waited for; matrix products, arithmetic and copies ran while one was open for 1% of the time, Pallas kernels for 0%

commit v1 on v0

v1 whole, which is shorter than its diff:
```python
import jax
import jax.numpy as jnp
from jax import lax
from jax.experimental import pallas as pl
from jax.experimental.pallas import tpu as pltpu
from jax.sharding import PartitionSpec as P


BOTH = ("row", "col")
Y, XH, XL, Z, CORE = 4, 2, 2, 4, 2
F32, BF16 = jnp.float32, jnp.bfloat16


def pairs(move):
    listed = []
    for y in range(Y):
        for x in range(XH * XL):
            for z in range(Z):
                for core in range(CORE):
                    y2, x2, z2, core2 = move(y, x, z, core)
                    y2, x2, z2 = y2 % Y, x2 % (XH * XL), z2 % Z
                    source = ((y * XH + x // XL) * XL + x % XL) * Z + z
                    target = ((y2 * XH + x2 // XL) * XL + x2 % XL) * Z + z2
                    listed.append((source * CORE + core, target * CORE + core2))
    return listed


MOVES = {
    "z+": pairs(lambda y, x, z, c: (y, x, z + 1, c)),
    "z-": pairs(lambda y, x, z, c: (y, x, z - 1, c)),
    "y+": pairs(lambda y, x, z, c: (y + 1, x, z, c)),
    "y-": pairs(lambda y, x, z, c: (y - 1, x, z, c)),
    "lo": pairs(lambda y, x, z, c: (y, x ^ 1, z, c)),
    "hi": pairs(lambda y, x, z, c: (y, x ^ 2, z, c)),
    "core": pairs(lambda y, x, z, c: (y, x, z, 1 - c)),
}


def send(array, move):
    return lax.ppermute(array, BOTH, MOVES[move])


def cut(array, top, rows):
    return array[top : top + rows]


def place():
    row, col = lax.axis_index("row"), lax.axis_index("col")
    y, xh = row >> 1, row & 1
    xl, z, core = col >> 3, (col >> 1) & 3, col & 1
    left = lambda other, turn: ((xl ^ other) * Z) + ((z + turn) & 3)
    right = lambda other, turn: (((y + turn) & 3) * XH) + (xh ^ other)
    return left, right, core


def split(value):
    high = value.astype(BF16)
    return high, (value - high.astype(F32)).astype(BF16)


def mul(left, high, low):
    left_high, left_low = split(left)
    dot = lambda one, two: jnp.dot(one, two, preferred_element_type=F32)
    return dot(left_high, high) + (dot(left_low, high) + dot(left_high, low))


LEFTS = ((0, 0, 0), (1, 0, 0), (0, 3, 0), (0, 1, 0), (0, 2, 0), (0, 2, 1), (1, 3, 0), (1, 1, 0))
RIGHTS = ((0, 0, 0), (0, 3, 0), (0, 1, 0), (0, 2, 0), (0, 2, 1), (1, 0, 0), (1, 0, 1), (1, 3, 0), (1, 1, 0), (1, 3, 1), (1, 1, 1))


def main_kernel(*refs):
    count = len(LEFTS)
    mine, theirs, rights = refs[:count], refs[count : 2 * count], refs[2 * count : 2 * count + len(RIGHTS)]
    total, held_left, held_high, held_low, high, low = refs[2 * count + len(RIGHTS) :]
    left_of, right_of, core = place()
    last = right_of(1, 2)
    spare = left_of(1, 2)
    step = high.shape[1]

    for ref, (other, turn, half) in zip(rights, RIGHTS):
        for part in range(ref.shape[0] // step):
            at = right_of(other, turn) * 2 + half + part
            high[at], low[at] = split(ref[part * step : (part + 1) * step])
    for part in range(2):
        high[last * 2 + part] = jnp.zeros(high.shape[1:], BF16)
        low[last * 2 + part] = jnp.zeros(low.shape[1:], BF16)
    for part in range(2):
        held_high[part] = high[spare * 2 + part]
        held_low[part] = low[spare * 2 + part]

    begun = False
    for refs, side in ((mine, core), (theirs, 1 - core)):
        for ref, (other, turn, half) in zip(refs, LEFTS):
            tile = left_of(other, turn)
            rows = ref.shape[0]
            at = tile * 2 + side
            top = half * rows
            for block in range(rows // step):
                rows_in = pl.ds(block * step, step)
                rows_out = pl.ds(top + block * step, step)
                product = mul(ref[rows_in], high[at], low[at])
                if begun:
                    total[rows_out] += product
                else:
                    total[rows_out] = product

            begun = True

            @pl.when(tile == last)
            def _():
                held_left[side, pl.ds(top, rows)] = ref[...]


def last_kernel(total, held_left, held_high, held_low, a0, a1, s0, s1, b0, b1, b2, b3, out, high, low):
    left_of, right_of, core = place()
    last = right_of(1, 2)
    spare = left_of(1, 2)
    step = high.shape[1]
    for index, ref in enumerate((b0, b1, b2, b3)):
        rows = ref.shape[0]
        at = pl.ds(index % 2 * rows, rows)
        high[index // 2, at], low[index // 2, at] = split(ref[...])

    @pl.when(last == spare)
    def _():
        held_high[...] = high[...]
        held_low[...] = low[...]

    for block, (mine, theirs) in enumerate(((a0, s0), (a1, s1))):
        rows = pl.ds(block * step, step)
        out[rows] = (
            total[rows]
            + mul(mine[...], held_high[core], held_low[core])
            + mul(theirs[...], held_high[1 - core], held_low[1 - core])
        )

    @pl.when(last != spare)
    def _():
        for block in range(2):
            rows = pl.ds(block * step, step)
            out[rows] += mul(held_left[0, rows], high[0], low[0]) + mul(held_left[1, rows], high[1], low[1])


def product(a, b):
    tall, wide = a.shape
    deep, broad = b.shape
    half, quarter, hill = deep // 2, deep // 4, tall // 2
    inside = pl.BlockSpec(memory_space=pltpu.VMEM)

    a_lo = send(a, "lo")
    a_p, a_m = send(a, "z+"), send(a, "z-")
    b_p, b_m = send(b, "y+"), send(b, "y-")
    b_hi = [send(cut(b, 0, half), "hi"), send(cut(b, half, half), "hi")]
    al_p, al_m = send(a_lo, "z+"), send(a_lo, "z-")
    a_pp = send(cut(a_p, 0, hill), "z+")
    a_mm = send(cut(a_m, hill, hill), "z-")
    b_pp = send(cut(b_p, 0, half), "y+")
    b_mm = send(cut(b_m, half, half), "y-")
    bh_p = [send(b_hi[0], "y+"), send(b_hi[1], "y+")]
    bh_m = [send(b_hi[0], "y-"), send(b_hi[1], "y-")]
    al_pp = send(cut(al_p, 0, hill), "z+")
    al_mm = send(cut(al_m, hill, hill), "z-")
    bh_pp = [send(cut(bh_p[0], 0, quarter), "y+"), send(cut(bh_p[1], 0, quarter), "y+")]
    bh_mm = [send(cut(bh_m[0], quarter, quarter), "y-"), send(cut(bh_m[1], quarter, quarter), "y-")]

    lefts = (a, a_lo, a_p, a_m, a_pp, a_mm, al_p, al_m)
    others = tuple(send(piece, "core") for piece in lefts)
    rights = (b, b_p, b_m, b_pp, b_mm, b_hi[0], b_hi[1], bh_p[0], bh_m[0], bh_p[1], bh_m[1])
    step = half
    flops = 6 * tall * deep * XL * Z * broad
    total, held_left, held_high, held_low = pl.pallas_call(
        main_kernel,
        out_shape=(
            jax.ShapeDtypeStruct((tall, broad), F32),
            jax.ShapeDtypeStruct((2, tall, wide), F32),
            jax.ShapeDtypeStruct((2, step, broad), BF16),
            jax.ShapeDtypeStruct((2, step, broad), BF16),
        ),
        in_specs=[inside] * (2 * len(lefts) + len(rights)),
        out_specs=(inside,) * 4,
        scratch_shapes=[pltpu.VMEM((XL * Z * 2, step, broad), BF16)] * 2,
        compiler_params=pltpu.CompilerParams(vmem_limit_bytes=24 << 20),
        cost_estimate=pl.CostEstimate(flops=flops, bytes_accessed=12 << 20, transcendentals=0),
    )(*lefts, *others, *rights)

    last_s = send(al_pp, "core"), send(al_mm, "core")
    return pl.pallas_call(
        last_kernel,
        out_shape=jax.ShapeDtypeStruct((tall, broad), F32),
        in_specs=[inside] * 12,
        out_specs=inside,
        scratch_shapes=[pltpu.VMEM((2, step, broad), BF16)] * 2,
        compiler_params=pltpu.CompilerParams(vmem_limit_bytes=12 << 20),
        cost_estimate=pl.CostEstimate(flops=flops // 4, bytes_accessed=3 << 20, transcendentals=0),
    )(total, held_left, held_high, held_low, al_pp, al_mm, *last_s, bh_pp[0], bh_mm[0], bh_pp[1], bh_mm[1])


def solution(mesh):
    placed = (P("row", "col"), P("row", "col"))
    return jax.shard_map(product, mesh=mesh, in_specs=placed, out_specs=P("row", "col"), check_vma=False)
```

time: 123 us -> 94.7 us (0.77); the launches traced: 123 us -> 93.4 us
  blocking collectives: 97.2 us -> 0 us
  waiting for transfers between devices: 0.71 us -> 44.4 us
  starting transfers between devices: 0.01 us -> 40.5 us
  between operations: 13.4 us -> 0.16 us
  matrix products: 10.5 us -> 0 us
  Pallas kernels: 0 us -> 7.19 us
    all_to_all x1 -> x0, blocking collectives: 97.2 us -> none  [copy_for_each(): lax.all_to_all(jnp.broadcast_to(array[None], (devices, *array.shape)), ax...]
    ppermute x0 -> x33, waiting for transfers between devices: none -> 44.4 us  [send(): return lax.ppermute(array, BOTH, MOVES[move])]
    ppermute x0 -> x33, starting transfers between devices: none -> 40.5 us  [send(): return lax.ppermute(array, BOTH, MOVES[move])]
    dot_general x1 -> x0, matrix products: 10.5 us -> none  [multiply(): jnp.dot(left_term, right_term, precision=lax.Precision.HIGHEST, preferred...]
    pallas_call x0 -> x2, Pallas kernels: none -> 7.19 us  [the longest x1 5.17 us: product(): pl.pallas_call(main_kernel, out_shape=(jax.ShapeDtypeStruct((tall, broad)...]
    broadcast_in_dim x1 -> x0, local copies, waits for them, and re-layouts: 1.4 us -> none  [copy_for_each(): jnp.broadcast_to(array[None], (devices, *array.shape))]
  transfers between devices with their start and end apart: 1 -> 33, of which waited for: 0 -> 12; matrix products, arithmetic and copies ran while one was open for 1% -> 1% of each run, Pallas kernels for 0% -> 6%
where the time goes in v1:
time: 94.7 us; the launch traced here: 93.4 us
  waiting for transfers between devices  44.4 us (47%)
  starting transfers between devices  40.5 us (43%)
  Pallas kernels  7.19 us (8%)
  local copies, waits for them, and re-layouts  1.22 us (1%)
    ppermute x33, waiting for transfers between devices, send(): return lax.ppermute(array, BOTH, MOVES[move])  44.4 us
    ppermute x33, starting transfers between devices, send(): return lax.ppermute(array, BOTH, MOVES[move])  40.5 us
    pallas_call x1, Pallas kernels, product(): pl.pallas_call(main_kernel, out_shape=(jax.ShapeDtypeStruct((tall, broad)...  5.17 us
    pallas_call x1, Pallas kernels, product(): pl.pallas_call(last_kernel, out_shape=jax.ShapeDtypeStruct((tall, broad),...  2.03 us
  transfers between devices with their start and end apart: 33, of which 12 were waited for; matrix products, arithmetic and copies ran while one was open for 1% of the time, Pallas kernels for 6%

profile of v1, /device:TPU:0, one launch (start us, length us, event | category | flops | bytes accessed | tf_op | source)
XLA Modules:
  0.0 93.4 jit_solution(8838812733713243000)
XLA Ops:
  0.0 1.6 %collective-permute-start = (f32[512,256]{1,0:T(8,128)}, f32[512,256]{1,0:T(8,128)S(1)}, u32[]{:S(2)}, u32[]{:S(2)}) collective-permute-start(f32[512,256]{1,0:T(8,128)} %refs_0_.1), channel_id=1, source_target_pairs={{0,8},{1,9},{2,10},{3,11},{4,12},{5,13},{6,14},{7,15},{8,0},{9,1},... | collective-permute-start | bytes 1572872 | tf_op jit(solution)/shard_map/ppermute | solution.py:40
  1.6 1.1 %fusion = (f32[256,256]{1,0:T(8,128)S(1)}, f32[256,256]{1,0:T(8,128)S(1)}) fusion(f32[512,256]{1,0:T(8,128)} %refs_16_.1), kind=kLoop, calls=%fused_computation | loop fusion | bytes 1048576 | tf_op jit(solution)/shard_map/slice | solution.py:44
  2.7 2.8 %collective-permute-start.19 = (f32[256,256]{1,0:T(8,128)S(1)}, f32[256,256]{1,0:T(8,128)S(1)}, u32[]{:S(2)}, u32[]{:S(2)}) collective-permute-start(f32[256,256]{1,0:T(8,128)S(1)} %get-tuple-element.14), channel_id=1, source_target_pairs={{0,16},{1,17},{2,18},{3,19},{4,20},{5,21},{6,22},{7,23},{8,24},{9,... | collective-permute-start | bytes 786440 | tf_op jit(solution)/shard_map/ppermute | solution.py:40
  5.5 0.8 collective-permute-start.20
  6.3 16.6 %collective-permute-done.19.refs_21_ = f32[256,256]{1,0:T(8,128)S(1)} collective-permute-done((f32[256,256]{1,0:T(8,128)S(1)}, f32[256,256]{1,0:T(8,128)S(1)}, u32[]{:S(2)}, u32[]{:S(2)}) %collective-permute-start.19) | collective-permute-done | bytes 262176 | tf_op jit(solution)/shard_map/ppermute | solution.py:40
  22.9 1.6 %collective-permute-start.21 = (f32[256,256]{1,0:T(8,128)S(1)}, f32[256,256]{1,0:T(8,128)S(1)}, u32[]{:S(2)}, u32[]{:S(2)}) collective-permute-start(f32[256,256]{1,0:T(8,128)S(1)} %collective-permute-done.19.refs_21_), channel_id=1, source_target_pairs={{0,32},{1,33},{2,34},{3,35},{4,36},{5,37},{6,38},{7,39},{8,40},{9,... | collective-permute-start | bytes 786440 | tf_op jit(solution)/shard_map/ppermute | solution.py:40
  24.5 1.7 %collective-permute-start.22 = (f32[256,256]{1,0:T(8,128)S(1)}, f32[256,256]{1,0:T(8,128)S(1)}, u32[]{:S(2)}, u32[]{:S(2)}) collective-permute-start(f32[256,256]{1,0:T(8,128)S(1)} %collective-permute-done.19.refs_21_), channel_id=1, source_target_pairs={{0,96},{1,97},{2,98},{3,99},{4,100},{5,101},{6,102},{7,103},{8,104... | collective-permute-start | bytes 786440 | tf_op jit(solution)/shard_map/ppermute | solution.py:40
  26.2 1.9 %collective-permute-start.1 = (f32[512,256]{1,0:T(8,128)S(1)}, f32[512,256]{1,0:T(8,128)S(1)}, u32[]{:S(2)}, u32[]{:S(2)}) collective-permute-start(f32[512,256]{1,0:T(8,128)S(1)} %copy-done.1), channel_id=1, source_target_pairs={{0,2},{1,3},{2,4},{3,5},{4,6},{5,7},{6,0},{7,1},{8,10},{9,11},{10,... | collective-permute-start | bytes 1572872 | tf_op jit(solution)/shard_map/ppermute | solution.py:40
  28.1 0.9 collective-permute-start.23
  29.0 4.0 %collective-permute-start.2 = (f32[512,256]{1,0:T(8,128)S(1)}, f32[512,256]{1,0:T(8,128)S(1)}, u32[]{:S(2)}, u32[]{:S(2)}) collective-permute-start(f32[512,256]{1,0:T(8,128)S(1)} %copy-done.1), channel_id=1, source_target_pairs={{0,6},{1,7},{2,0},{3,1},{4,2},{5,3},{6,4},{7,5},{8,14},{9,15},{10,... | collective-permute-start | bytes 1572872 | tf_op jit(solution)/shard_map/ppermute | solution.py:40
  33.0 1.6 %collective-permute-start.15 = (f32[512,256]{1,0:T(8,128)S(1)}, f32[512,256]{1,0:T(8,128)S(1)}, u32[]{:S(2)}, u32[]{:S(2)}) collective-permute-start(f32[512,256]{1,0:T(8,128)S(1)} %copy-done), channel_id=1, source_target_pairs={{0,32},{1,33},{2,34},{3,35},{4,36},{5,37},{6,38},{7,39},{8,40},{9,... | collective-permute-start | bytes 1572872 | tf_op jit(solution)/shard_map/ppermute | solution.py:40
  34.6 1.7 %collective-permute-start.16 = (f32[512,256]{1,0:T(8,128)S(1)}, f32[512,256]{1,0:T(8,128)S(1)}, u32[]{:S(2)}, u32[]{:S(2)}) collective-permute-start(f32[512,256]{1,0:T(8,128)S(1)} %copy-done), channel_id=1, source_target_pairs={{0,96},{1,97},{2,98},{3,99},{4,100},{5,101},{6,102},{7,103},{8,104... | collective-permute-start | bytes 1572872 | tf_op jit(solution)/shard_map/ppermute | solution.py:40
  36.3 0.7 collective-permute-done.23.refs_25_
  37.0 2.6 %collective-permute-done.1.refs_2_ = f32[512,256]{1,0:T(8,128)S(1)} collective-permute-done((f32[512,256]{1,0:T(8,128)S(1)}, f32[512,256]{1,0:T(8,128)S(1)}, u32[]{:S(2)}, u32[]{:S(2)}) %collective-permute-start.1) | collective-permute-done | bytes 524320 | tf_op jit(solution)/shard_map/ppermute | solution.py:40
  39.6 1.7 %collective-permute-start.24 = (f32[256,256]{1,0:T(8,128)S(1)}, f32[256,256]{1,0:T(8,128)S(1)}, u32[]{:S(2)}, u32[]{:S(2)}) collective-permute-start(f32[256,256]{1,0:T(8,128)S(1)} %collective-permute-done.20.refs_22_), channel_id=1, source_target_pairs={{0,96},{1,97},{2,98},{3,99},{4,100},{5,101},{6,102},{7,103},{8,104... | collective-permute-start | bytes 786440 | tf_op jit(solution)/shard_map/ppermute | solution.py:40
  41.4 1.7 %collective-permute-done.2.refs_3_ = f32[512,256]{1,0:T(8,128)S(1)} collective-permute-done((f32[512,256]{1,0:T(8,128)S(1)}, f32[512,256]{1,0:T(8,128)S(1)}, u32[]{:S(2)}, u32[]{:S(2)}) %collective-permute-start.2) | collective-permute-done | bytes 524320 | tf_op jit(solution)/shard_map/ppermute | solution.py:40
  43.6 3.7 %collective-permute-done.15.refs_17_ = f32[512,256]{1,0:T(8,128)S(1)} collective-permute-done((f32[512,256]{1,0:T(8,128)S(1)}, f32[512,256]{1,0:T(8,128)S(1)}, u32[]{:S(2)}, u32[]{:S(2)}) %collective-permute-start.15) | collective-permute-done | bytes 524320 | tf_op jit(solution)/shard_map/ppermute | solution.py:40
  47.4 1.9 %collective-permute-start.5 = (f32[512,256]{1,0:T(8,128)S(1)}, f32[512,256]{1,0:T(8,128)S(1)}, u32[]{:S(2)}, u32[]{:S(2)}) collective-permute-start(f32[512,256]{1,0:T(8,128)S(1)} %collective-permute-done.refs_1_), channel_id=1, source_target_pairs={{0,2},{1,3},{2,4},{3,5},{4,6},{5,7},{6,0},{7,1},{8,10},{9,11},{10,... | collective-permute-start | bytes 1572872 | tf_op jit(solution)/shard_map/ppermute | solution.py:40
  49.4 1.3 %collective-permute-start.29 = (f32[128,256]{1,0:T(8,128)S(1)}, f32[128,256]{1,0:T(8,128)S(1)}, u32[]{:S(2)}, u32[]{:S(2)}) collective-permute-start(f32[128,256]{1,0:T(8,128)S(1)} %slice.54), channel_id=1, source_target_pairs={{0,32},{1,33},{2,34},{3,35},{4,36},{5,37},{6,38},{7,39},{8,40},{9,... | collective-permute-start | bytes 393224 | tf_op jit(solution)/shard_map/ppermute | solution.py:40
  50.8 1.4 %collective-permute-done.24.refs_26_ = f32[256,256]{1,0:T(8,128)S(1)} collective-permute-done((f32[256,256]{1,0:T(8,128)S(1)}, f32[256,256]{1,0:T(8,128)S(1)}, u32[]{:S(2)}, u32[]{:S(2)}) %collective-permute-start.24) | collective-permute-done | bytes 262176 | tf_op jit(solution)/shard_map/ppermute | solution.py:40
  52.6 1.4 %collective-permute-start.4 = (f32[256,256]{1,0:T(8,128)S(1)}, f32[256,256]{1,0:T(8,128)S(1)}, u32[]{:S(2)}, u32[]{:S(2)}) collective-permute-start(f32[256,256]{1,0:T(8,128)S(1)} %slice.49), channel_id=1, source_target_pairs={{0,6},{1,7},{2,0},{3,1},{4,2},{5,3},{6,4},{7,5},{8,14},{9,15},{10,... | collective-permute-start | bytes 786440 | tf_op jit(solution)/shard_map/ppermute | solution.py:40
  54.1 1.5 %collective-permute-done.29.b0 = f32[128,256]{1,0:T(8,128)S(1)} collective-permute-done((f32[128,256]{1,0:T(8,128)S(1)}, f32[128,256]{1,0:T(8,128)S(1)}, u32[]{:S(2)}, u32[]{:S(2)}) %collective-permute-start.29) | collective-permute-done | bytes 131104 | tf_op jit(solution)/shard_map/ppermute | solution.py:40
  55.8 3.1 %collective-permute-start.18 = (f32[256,256]{1,0:T(8,128)S(1)}, f32[256,256]{1,0:T(8,128)S(1)}, u32[]{:S(2)}, u32[]{:S(2)}) collective-permute-start(f32[256,256]{1,0:T(8,128)S(1)} %slice.51), channel_id=1, source_target_pairs={{0,96},{1,97},{2,98},{3,99},{4,100},{5,101},{6,102},{7,103},{8,104... | collective-permute-start | bytes 786440 | tf_op jit(solution)/shard_map/ppermute | solution.py:40
  58.8 10.1 %collective-permute-done.4.refs_5_ = f32[256,256]{1,0:T(8,128)S(1)} collective-permute-done((f32[256,256]{1,0:T(8,128)S(1)}, f32[256,256]{1,0:T(8,128)S(1)}, u32[]{:S(2)}, u32[]{:S(2)}) %collective-permute-start.4) | collective-permute-done | bytes 262176 | tf_op jit(solution)/shard_map/ppermute | solution.py:40
  70.1 1.9 %collective-permute-done.11.refs_12_ = f32[256,256]{1,0:T(8,128)S(1)} collective-permute-done((f32[256,256]{1,0:T(8,128)S(1)}, f32[256,256]{1,0:T(8,128)S(1)}, u32[]{:S(2)}, u32[]{:S(2)}) %collective-permute-start.11) | collective-permute-done | bytes 262176 | tf_op jit(solution)/shard_map/ppermute | solution.py:40
  72.8 3.0 %collective-permute-start.26 = (f32[256,256]{1,0:T(8,128)S(1)}, f32[256,256]{1,0:T(8,128)S(1)}, u32[]{:S(2)}, u32[]{:S(2)}) collective-permute-start(f32[256,256]{1,0:T(8,128)S(1)} %slice.53), channel_id=1, source_target_pairs={{0,6},{1,7},{2,0},{3,1},{4,2},{5,3},{6,4},{7,5},{8,14},{9,15},{10,... | collective-permute-start | bytes 786440 | tf_op jit(solution)/shard_map/ppermute | solution.py:40
  75.9 2.9 %collective-permute-start.30 = (f32[128,256]{1,0:T(8,128)S(1)}, f32[128,256]{1,0:T(8,128)S(1)}, u32[]{:S(2)}, u32[]{:S(2)}) collective-permute-start(f32[128,256]{1,0:T(8,128)S(1)} %slice.55), channel_id=1, source_target_pairs={{0,96},{1,97},{2,98},{3,99},{4,100},{5,101},{6,102},{7,103},{8,104... | collective-permute-start | bytes 393224 | tf_op jit(solution)/shard_map/ppermute | solution.py:40
  78.9 3.6 %collective-permute-done.25.a0 = f32[256,256]{1,0:T(8,128)S(1)} collective-permute-done((f32[256,256]{1,0:T(8,128)S(1)}, f32[256,256]{1,0:T(8,128)S(1)}, u32[]{:S(2)}, u32[]{:S(2)}) %collective-permute-start.25) | collective-permute-done | bytes 262176 | tf_op jit(solution)/shard_map/ppermute | solution.py:40
  82.4 1.3 %collective-permute-start.31 = (f32[128,256]{1,0:T(8,128)S(1)}, f32[128,256]{1,0:T(8,128)S(1)}, u32[]{:S(2)}, u32[]{:S(2)}) collective-permute-start(f32[128,256]{1,0:T(8,128)S(1)} %slice.56), channel_id=1, source_target_pairs={{0,32},{1,33},{2,34},{3,35},{4,36},{5,37},{6,38},{7,39},{8,40},{9,... | collective-permute-start | bytes 393224 | tf_op jit(solution)/shard_map/ppermute | solution.py:40
  83.7 2.0 %collective-permute-start.32 = (f32[128,256]{1,0:T(8,128)S(1)}, f32[128,256]{1,0:T(8,128)S(1)}, u32[]{:S(2)}, u32[]{:S(2)}) collective-permute-start(f32[128,256]{1,0:T(8,128)S(1)} %slice.57), channel_id=1, source_target_pairs={{0,96},{1,97},{2,98},{3,99},{4,100},{5,101},{6,102},{7,103},{8,104... | collective-permute-start | bytes 393224 | tf_op jit(solution)/shard_map/ppermute | solution.py:40
  86.2 5.2 %shard_map.28 = (f32[512,256]{1,0:T(8,128)S(1)}, f32[2,512,256]{2,1,0:T(8,128)S(1)}, bf16[2,256,256]{2,1,0:T(8,128)(2,1)S(1)}, bf16[2,256,256]{2,1,0:T(8,128)(2,1)S(1)}) custom-call(f32[512,256]{1,0:T(8,128)S(1)} %copy-done.1, f32[512,256]{1,0:T(8,128)S(1)} %collective-permute-done.refs_1_, f32[512,256]{1,0:T(8,128)S(1)} %collective-permute-done.1.refs_2_, ...), custom_call_target="tpu_custom_call" | custom-call | flops 3221225472 | bytes 12582912 | tf_op jit(solution)/shard_map/pallas_call | solution.py:171
  91.4 2.0 %shard_map.29 = f32[512,256]{1,0:T(8,128)} custom-call(f32[512,256]{1,0:T(8,128)S(1)} %get-tuple-element.9.total, f32[2,512,256]{2,1,0:T(8,128)S(1)} %get-tuple-element.10.held_left, bf16[2,256,256]{2,1,0:T(8,128)(2,1)S(1)} %get-tuple-element.11.held_high, bf16[2,256,256]{2,1,0:T(8,128)(2,1)S(1)} %get-tuple-element.12.held_low, ...), custom_call_target="tpu_custom_call" | custom-call | flops 805306368 | bytes 3145728 | tf_op jit(solution)/shard_map/pallas_call | solution.py:187
  (51 shorter events, 3.8 us)
Async XLA Ops:
  0.0 29.0 %collective-permute-start = (f32[512,256]{1,0:T(8,128)}, f32[512,256]{1,0:T(8,128)S(1)}, u32[]{:S(2)}, u32[]{:S(2)}) collective-permute-start(f32[512,256]{1,0:T(8,128)} %refs_0_.1), channel_id=1, source_target_pairs={{0,8},{1,9},{2,10},{3,11},{4,12},{5,13},{6,14},{7,15},{8,0},{9,1},... | collective-permute-start | bytes 1572872 | tf_op jit(solution)/shard_map/ppermute | solution.py:40
  2.7 20.3 %collective-permute-start.19 = (f32[256,256]{1,0:T(8,128)S(1)}, f32[256,256]{1,0:T(8,128)S(1)}, u32[]{:S(2)}, u32[]{:S(2)}) collective-permute-start(f32[256,256]{1,0:T(8,128)S(1)} %get-tuple-element.14), channel_id=1, source_target_pairs={{0,16},{1,17},{2,18},{3,19},{4,20},{5,21},{6,22},{7,23},{8,24},{9,... | collective-permute-start | bytes 786440 | tf_op jit(solution)/shard_map/ppermute | solution.py:40
  5.5 22.6 %collective-permute-start.20 = (f32[256,256]{1,0:T(8,128)S(1)}, f32[256,256]{1,0:T(8,128)S(1)}, u32[]{:S(2)}, u32[]{:S(2)}) collective-permute-start(f32[256,256]{1,0:T(8,128)S(1)} %get-tuple-element.13), channel_id=1, source_target_pairs={{0,16},{1,17},{2,18},{3,19},{4,20},{5,21},{6,22},{7,23},{8,24},{9,... | collective-permute-start | bytes 786440 | tf_op jit(solution)/shard_map/ppermute | solution.py:40
  22.9 10.1 %collective-permute-start.21 = (f32[256,256]{1,0:T(8,128)S(1)}, f32[256,256]{1,0:T(8,128)S(1)}, u32[]{:S(2)}, u32[]{:S(2)}) collective-permute-start(f32[256,256]{1,0:T(8,128)S(1)} %collective-permute-done.19.refs_21_), channel_id=1, source_target_pairs={{0,32},{1,33},{2,34},{3,35},{4,36},{5,37},{6,38},{7,39},{8,40},{9,... | collective-permute-start | bytes 786440 | tf_op jit(solution)/shard_map/ppermute | solution.py:40
  24.5 10.1 %collective-permute-start.22 = (f32[256,256]{1,0:T(8,128)S(1)}, f32[256,256]{1,0:T(8,128)S(1)}, u32[]{:S(2)}, u32[]{:S(2)}) collective-permute-start(f32[256,256]{1,0:T(8,128)S(1)} %collective-permute-done.19.refs_21_), channel_id=1, source_target_pairs={{0,96},{1,97},{2,98},{3,99},{4,100},{5,101},{6,102},{7,103},{8,104... | collective-permute-start | bytes 786440 | tf_op jit(solution)/shard_map/ppermute | solution.py:40
  26.2 13.5 %collective-permute-start.1 = (f32[512,256]{1,0:T(8,128)S(1)}, f32[512,256]{1,0:T(8,128)S(1)}, u32[]{:S(2)}, u32[]{:S(2)}) collective-permute-start(f32[512,256]{1,0:T(8,128)S(1)} %copy-done.1), channel_id=1, source_target_pairs={{0,2},{1,3},{2,4},{3,5},{4,6},{5,7},{6,0},{7,1},{8,10},{9,11},{10,... | collective-permute-start | bytes 1572872 | tf_op jit(solution)/shard_map/ppermute | solution.py:40
  28.1 8.9 %collective-permute-start.23 = (f32[256,256]{1,0:T(8,128)S(1)}, f32[256,256]{1,0:T(8,128)S(1)}, u32[]{:S(2)}, u32[]{:S(2)}) collective-permute-start(f32[256,256]{1,0:T(8,128)S(1)} %collective-permute-done.20.refs_22_), channel_id=1, source_target_pairs={{0,32},{1,33},{2,34},{3,35},{4,36},{5,37},{6,38},{7,39},{8,40},{9,... | collective-permute-start | bytes 786440 | tf_op jit(solution)/shard_map/ppermute | solution.py:40
  29.0 14.1 %collective-permute-start.2 = (f32[512,256]{1,0:T(8,128)S(1)}, f32[512,256]{1,0:T(8,128)S(1)}, u32[]{:S(2)}, u32[]{:S(2)}) collective-permute-start(f32[512,256]{1,0:T(8,128)S(1)} %copy-done.1), channel_id=1, source_target_pairs={{0,6},{1,7},{2,0},{3,1},{4,2},{5,3},{6,4},{7,5},{8,14},{9,15},{10,... | collective-permute-start | bytes 1572872 | tf_op jit(solution)/shard_map/ppermute | solution.py:40
  33.0 14.3 %collective-permute-start.15 = (f32[512,256]{1,0:T(8,128)S(1)}, f32[512,256]{1,0:T(8,128)S(1)}, u32[]{:S(2)}, u32[]{:S(2)}) collective-permute-start(f32[512,256]{1,0:T(8,128)S(1)} %copy-done), channel_id=1, source_target_pairs={{0,32},{1,33},{2,34},{3,35},{4,36},{5,37},{6,38},{7,39},{8,40},{9,... | collective-permute-start | bytes 1572872 | tf_op jit(solution)/shard_map/ppermute | solution.py:40
  34.6 14.8 %collective-permute-start.16 = (f32[512,256]{1,0:T(8,128)S(1)}, f32[512,256]{1,0:T(8,128)S(1)}, u32[]{:S(2)}, u32[]{:S(2)}) collective-permute-start(f32[512,256]{1,0:T(8,128)S(1)} %copy-done), channel_id=1, source_target_pairs={{0,96},{1,97},{2,98},{3,99},{4,100},{5,101},{6,102},{7,103},{8,104... | collective-permute-start | bytes 1572872 | tf_op jit(solution)/shard_map/ppermute | solution.py:40
  37.0 15.6 %collective-permute-start.7 = (f32[512,256]{1,0:T(8,128)S(1)}, f32[512,256]{1,0:T(8,128)S(1)}, u32[]{:S(2)}, u32[]{:S(2)}) collective-permute-start(f32[512,256]{1,0:T(8,128)S(1)} %copy-done.1), channel_id=1, source_target_pairs={{0,1},{1,0},{2,3},{3,2},{4,5},{5,4},{6,7},{7,6},{8,9},{9,8},{10,11... | collective-permute-start | bytes 1572872 | tf_op jit(solution)/shard_map/ppermute | solution.py:40
  39.6 12.6 %collective-permute-start.24 = (f32[256,256]{1,0:T(8,128)S(1)}, f32[256,256]{1,0:T(8,128)S(1)}, u32[]{:S(2)}, u32[]{:S(2)}) collective-permute-start(f32[256,256]{1,0:T(8,128)S(1)} %collective-permute-done.20.refs_22_), channel_id=1, source_target_pairs={{0,96},{1,97},{2,98},{3,99},{4,100},{5,101},{6,102},{7,103},{8,104... | collective-permute-start | bytes 786440 | tf_op jit(solution)/shard_map/ppermute | solution.py:40
  43.1 12.7 %collective-permute-start.3 = (f32[256,256]{1,0:T(8,128)S(1)}, f32[256,256]{1,0:T(8,128)S(1)}, u32[]{:S(2)}, u32[]{:S(2)}) collective-permute-start(f32[256,256]{1,0:T(8,128)S(1)} %slice.48), channel_id=1, source_target_pairs={{0,2},{1,3},{2,4},{3,5},{4,6},{5,7},{6,0},{7,1},{8,10},{9,11},{10,... | collective-permute-start | bytes 786440 | tf_op jit(solution)/shard_map/ppermute | solution.py:40
  47.4 22.2 %collective-permute-start.5 = (f32[512,256]{1,0:T(8,128)S(1)}, f32[512,256]{1,0:T(8,128)S(1)}, u32[]{:S(2)}, u32[]{:S(2)}) collective-permute-start(f32[512,256]{1,0:T(8,128)S(1)} %collective-permute-done.refs_1_), channel_id=1, source_target_pairs={{0,2},{1,3},{2,4},{3,5},{4,6},{5,7},{6,0},{7,1},{8,10},{9,11},{10,... | collective-permute-start | bytes 1572872 | tf_op jit(solution)/shard_map/ppermute | solution.py:40
  49.4 6.2 %collective-permute-start.29 = (f32[128,256]{1,0:T(8,128)S(1)}, f32[128,256]{1,0:T(8,128)S(1)}, u32[]{:S(2)}, u32[]{:S(2)}) collective-permute-start(f32[128,256]{1,0:T(8,128)S(1)} %slice.54), channel_id=1, source_target_pairs={{0,32},{1,33},{2,34},{3,35},{4,36},{5,37},{6,38},{7,39},{8,40},{9,... | collective-permute-start | bytes 393224 | tf_op jit(solution)/shard_map/ppermute | solution.py:40
  52.2 17.8 %collective-permute-start.6 = (f32[512,256]{1,0:T(8,128)S(1)}, f32[512,256]{1,0:T(8,128)S(1)}, u32[]{:S(2)}, u32[]{:S(2)}) collective-permute-start(f32[512,256]{1,0:T(8,128)S(1)} %collective-permute-done.refs_1_), channel_id=1, source_target_pairs={{0,6},{1,7},{2,0},{3,1},{4,2},{5,3},{6,4},{7,5},{8,14},{9,15},{10,... | collective-permute-start | bytes 1572872 | tf_op jit(solution)/shard_map/ppermute | solution.py:40
  52.6 16.3 %collective-permute-start.4 = (f32[256,256]{1,0:T(8,128)S(1)}, f32[256,256]{1,0:T(8,128)S(1)}, u32[]{:S(2)}, u32[]{:S(2)}) collective-permute-start(f32[256,256]{1,0:T(8,128)S(1)} %slice.49), channel_id=1, source_target_pairs={{0,6},{1,7},{2,0},{3,1},{4,2},{5,3},{6,4},{7,5},{8,14},{9,15},{10,... | collective-permute-start | bytes 786440 | tf_op jit(solution)/shard_map/ppermute | solution.py:40
  55.6 13.4 %collective-permute-start.17 = (f32[256,256]{1,0:T(8,128)S(1)}, f32[256,256]{1,0:T(8,128)S(1)}, u32[]{:S(2)}, u32[]{:S(2)}) collective-permute-start(f32[256,256]{1,0:T(8,128)S(1)} %slice.50), channel_id=1, source_target_pairs={{0,32},{1,33},{2,34},{3,35},{4,36},{5,37},{6,38},{7,39},{8,40},{9,... | collective-permute-start | bytes 786440 | tf_op jit(solution)/shard_map/ppermute | solution.py:40
  55.8 13.7 %collective-permute-start.18 = (f32[256,256]{1,0:T(8,128)S(1)}, f32[256,256]{1,0:T(8,128)S(1)}, u32[]{:S(2)}, u32[]{:S(2)}) collective-permute-start(f32[256,256]{1,0:T(8,128)S(1)} %slice.51), channel_id=1, source_target_pairs={{0,96},{1,97},{2,98},{3,99},{4,100},{5,101},{6,102},{7,103},{8,104... | collective-permute-start | bytes 786440 | tf_op jit(solution)/shard_map/ppermute | solution.py:40
  68.9 3.6 %collective-permute-start.8 = (f32[512,256]{1,0:T(8,128)S(1)}, f32[512,256]{1,0:T(8,128)S(1)}, u32[]{:S(2)}, u32[]{:S(2)}) collective-permute-start(f32[512,256]{1,0:T(8,128)S(1)} %collective-permute-done.refs_1_), channel_id=1, source_target_pairs={{0,1},{1,0},{2,3},{3,2},{4,5},{5,4},{6,7},{7,6},{8,9},{9,8},{10,11... | collective-permute-start | bytes 1572872 | tf_op jit(solution)/shard_map/ppermute | solution.py:40
  69.0 3.9 %collective-permute-start.10 = (f32[512,256]{1,0:T(8,128)S(1)}, f32[512,256]{1,0:T(8,128)S(1)}, u32[]{:S(2)}, u32[]{:S(2)}) collective-permute-start(f32[512,256]{1,0:T(8,128)S(1)} %collective-permute-done.2.refs_3_), channel_id=1, source_target_pairs={{0,1},{1,0},{2,3},{3,2},{4,5},{5,4},{6,7},{7,6},{8,9},{9,8},{10,11... | collective-permute-start | bytes 1572872 | tf_op jit(solution)/shard_map/ppermute | solution.py:40
  69.6 2.8 %collective-permute-start.12 = (f32[256,256]{1,0:T(8,128)S(1)}, f32[256,256]{1,0:T(8,128)S(1)}, u32[]{:S(2)}, u32[]{:S(2)}) collective-permute-start(f32[256,256]{1,0:T(8,128)S(1)} %collective-permute-done.4.refs_5_), channel_id=1, source_target_pairs={{0,1},{1,0},{2,3},{3,2},{4,5},{5,4},{6,7},{7,6},{8,9},{9,8},{10,11... | collective-permute-start | bytes 786440 | tf_op jit(solution)/shard_map/ppermute | solution.py:40
  70.0 5.9 %collective-permute-start.9 = (f32[512,256]{1,0:T(8,128)S(1)}, f32[512,256]{1,0:T(8,128)S(1)}, u32[]{:S(2)}, u32[]{:S(2)}) collective-permute-start(f32[512,256]{1,0:T(8,128)S(1)} %collective-permute-done.1.refs_2_), channel_id=1, source_target_pairs={{0,1},{1,0},{2,3},{3,2},{4,5},{5,4},{6,7},{7,6},{8,9},{9,8},{10,11... | collective-permute-start | bytes 1572872 | tf_op jit(solution)/shard_map/ppermute | solution.py:40
  72.0 13.7 %collective-permute-start.13 = (f32[512,256]{1,0:T(8,128)S(1)}, f32[512,256]{1,0:T(8,128)S(1)}, u32[]{:S(2)}, u32[]{:S(2)}) collective-permute-start(f32[512,256]{1,0:T(8,128)S(1)} %collective-permute-done.5.refs_6_), channel_id=1, source_target_pairs={{0,1},{1,0},{2,3},{3,2},{4,5},{5,4},{6,7},{7,6},{8,9},{9,8},{10,11... | collective-permute-start | bytes 1572872 | tf_op jit(solution)/shard_map/ppermute | solution.py:40
  72.4 13.3 %collective-permute-start.14 = (f32[512,256]{1,0:T(8,128)S(1)}, f32[512,256]{1,0:T(8,128)S(1)}, u32[]{:S(2)}, u32[]{:S(2)}) collective-permute-start(f32[512,256]{1,0:T(8,128)S(1)} %collective-permute-done.6.refs_7_), channel_id=1, source_target_pairs={{0,1},{1,0},{2,3},{3,2},{4,5},{5,4},{6,7},{7,6},{8,9},{9,8},{10,11... | collective-permute-start | bytes 1572872 | tf_op jit(solution)/shard_map/ppermute | solution.py:40
  72.6 9.9 %collective-permute-start.25 = (f32[256,256]{1,0:T(8,128)S(1)}, f32[256,256]{1,0:T(8,128)S(1)}, u32[]{:S(2)}, u32[]{:S(2)}) collective-permute-start(f32[256,256]{1,0:T(8,128)S(1)} %slice.52), channel_id=1, source_target_pairs={{0,2},{1,3},{2,4},{3,5},{4,6},{5,7},{6,0},{7,1},{8,10},{9,11},{10,... | collective-permute-start | bytes 786440 | tf_op jit(solution)/shard_map/ppermute | solution.py:40
  72.8 10.9 %collective-permute-start.26 = (f32[256,256]{1,0:T(8,128)S(1)}, f32[256,256]{1,0:T(8,128)S(1)}, u32[]{:S(2)}, u32[]{:S(2)}) collective-permute-start(f32[256,256]{1,0:T(8,128)S(1)} %slice.53), channel_id=1, source_target_pairs={{0,6},{1,7},{2,0},{3,1},{4,2},{5,3},{6,4},{7,5},{8,14},{9,15},{10,... | collective-permute-start | bytes 786440 | tf_op jit(solution)/shard_map/ppermute | solution.py:40
  75.9 15.4 %collective-permute-start.30 = (f32[128,256]{1,0:T(8,128)S(1)}, f32[128,256]{1,0:T(8,128)S(1)}, u32[]{:S(2)}, u32[]{:S(2)}) collective-permute-start(f32[128,256]{1,0:T(8,128)S(1)} %slice.55), channel_id=1, source_target_pairs={{0,96},{1,97},{2,98},{3,99},{4,100},{5,101},{6,102},{7,103},{8,104... | collective-permute-start | bytes 393224 | tf_op jit(solution)/shard_map/ppermute | solution.py:40
  82.4 8.9 %collective-permute-start.31 = (f32[128,256]{1,0:T(8,128)S(1)}, f32[128,256]{1,0:T(8,128)S(1)}, u32[]{:S(2)}, u32[]{:S(2)}) collective-permute-start(f32[128,256]{1,0:T(8,128)S(1)} %slice.56), channel_id=1, source_target_pairs={{0,32},{1,33},{2,34},{3,35},{4,36},{5,37},{6,38},{7,39},{8,40},{9,... | collective-permute-start | bytes 393224 | tf_op jit(solution)/shard_map/ppermute | solution.py:40
  83.7 7.7 %collective-permute-start.32 = (f32[128,256]{1,0:T(8,128)S(1)}, f32[128,256]{1,0:T(8,128)S(1)}, u32[]{:S(2)}, u32[]{:S(2)}) collective-permute-start(f32[128,256]{1,0:T(8,128)S(1)} %slice.57), channel_id=1, source_target_pairs={{0,96},{1,97},{2,98},{3,99},{4,100},{5,101},{6,102},{7,103},{8,104... | collective-permute-start | bytes 393224 | tf_op jit(solution)/shard_map/ppermute | solution.py:40
  85.7 5.7 %collective-permute-start.27 = (f32[256,256]{1,0:T(8,128)S(1)}, f32[256,256]{1,0:T(8,128)S(1)}, u32[]{:S(2)}, u32[]{:S(2)}) collective-permute-start(f32[256,256]{1,0:T(8,128)S(1)} %collective-permute-done.25.a0), channel_id=1, source_target_pairs={{0,1},{1,0},{2,3},{3,2},{4,5},{5,4},{6,7},{7,6},{8,9},{9,8},{10,11... | collective-permute-start | bytes 786440 | tf_op jit(solution)/shard_map/ppermute | solution.py:40
  85.7 5.7 %collective-permute-start.28 = (f32[256,256]{1,0:T(8,128)S(1)}, f32[256,256]{1,0:T(8,128)S(1)}, u32[]{:S(2)}, u32[]{:S(2)}) collective-permute-start(f32[256,256]{1,0:T(8,128)S(1)} %collective-permute-done.26.a1), channel_id=1, source_target_pairs={{0,1},{1,0},{2,3},{3,2},{4,5},{5,4},{6,7},{7,6},{8,9},{9,8},{10,11... | collective-permute-start | bytes 786440 | tf_op jit(solution)/shard_map/ppermute | solution.py:40
  (3 other events, 61.7 us)

commit v2 on v1

v2 whole, which is shorter than its diff:
```python
import jax
import jax.numpy as jnp
from jax import lax
from jax.experimental import pallas as pl
from jax.experimental.pallas import tpu as pltpu
from jax.sharding import PartitionSpec as P


BOTH = ("row", "col")
Y, XH, XL, Z, CORE = 4, 2, 2, 4, 2
F32, BF16 = jnp.float32, jnp.bfloat16


def pairs(move):
    listed = []
    for y in range(Y):
        for x in range(XH * XL):
            for z in range(Z):
                for core in range(CORE):
                    y2, x2, z2, core2 = move(y, x, z, core)
                    y2, x2, z2 = y2 % Y, x2 % (XH * XL), z2 % Z
                    source = ((y * XH + x // XL) * XL + x % XL) * Z + z
                    target = ((y2 * XH + x2 // XL) * XL + x2 % XL) * Z + z2
                    listed.append((source * CORE + core, target * CORE + core2))
    return listed


MOVES = {
    "z+": pairs(lambda y, x, z, c: (y, x, z + 1, 1 - c)),
    "z-": pairs(lambda y, x, z, c: (y, x, z - 1, 1 - c)),
    "y+": pairs(lambda y, x, z, c: (y + 1, x, z, c)),
    "y-": pairs(lambda y, x, z, c: (y - 1, x, z, c)),
    "lo": pairs(lambda y, x, z, c: (y, x ^ 1, z, 1 - c)),
    "hi": pairs(lambda y, x, z, c: (y, x ^ 2, z, c)),
    "core": pairs(lambda y, x, z, c: (y, x, z, 1 - c)),
}


def send(array, move):
    return lax.ppermute(array, BOTH, MOVES[move])


def cut(array, top, rows):
    return array[top : top + rows]


def place():
    row, col = lax.axis_index("row"), lax.axis_index("col")
    y, xh = row >> 1, row & 1
    xl, z, core = col >> 3, (col >> 1) & 3, col & 1
    left = lambda other, turn: ((xl ^ other) * Z) + ((z + turn) & 3)
    right = lambda other, turn: (((y + turn) & 3) * XH) + (xh ^ other)
    return left, right, core


def split(value):
    high = value.astype(BF16)
    return high, (value - high.astype(F32)).astype(BF16)


def mul(*terms):
    lefts, rights = [], []
    for left, high, low in terms:
        left_high, left_low = split(left)
        lefts += [left_high, left_low, left_high]
        rights += [high, high, low]
    return jnp.dot(jnp.concatenate(lefts, axis=1), jnp.concatenate(rights), preferred_element_type=F32)


LEFTS = ((0, 0, 0), (1, 0, 0), (0, 3, 0), (0, 1, 0), (0, 2, 0), (0, 2, 1), (1, 3, 0), (1, 1, 0))
ROWS, FAR = 64, 256
RIGHTS = (
    (0, 0, 0), (0, 3, 0), (0, 1, 0), (0, 2, 0), (0, 2, FAR), (1, 0, 0), (1, 0, 256),
    (1, 3, 0), (1, 1, 0), (1, 3, 256), (1, 1, 256),
)
SOON, HELD = 4, 7


def store_right(refs, places, right_of, high, low):
    step = high.shape[1]
    for ref, (other, turn, top) in zip(refs, places):
        for part in range(0, ref.shape[0], ROWS):
            at, rows = right_of(other, turn) * 2 + (top + part) // step, pl.ds((top + part) % step, ROWS)
            high[at, rows], low[at, rows] = split(ref[part : part + ROWS])


def add(total, mine, theirs, place_of, left_of, core, high, low):
    other, turn, half = place_of
    tile = left_of(other, turn)
    rows, step = mine.shape[0], high.shape[1]
    side = (core + other + turn) & 1
    at, beside = tile * 2 + side, tile * 2 + 1 - side
    for block in range(rows // step):
        rows_in = pl.ds(block * step, step)
        rows_out = pl.ds(half * rows + block * step, step)
        total[rows_out] += mul((mine[rows_in], high[at], low[at]), (theirs[rows_in], high[beside], low[beside]))


def is_soon(tile, right_of):
    return ((tile & 1) == (right_of(0, 0) & 1)) | (tile == right_of(1, 0))


def soon_kernel(*refs):
    mine, theirs, rights = refs[:SOON], refs[SOON : 2 * SOON], refs[2 * SOON : 2 * SOON + HELD]
    total, high, low = refs[2 * SOON + HELD :]
    left_of, right_of, core = place()
    store_right(rights, RIGHTS[:HELD], right_of, high, low)
    total[...] = jnp.zeros_like(total)
    for mine_ref, their_ref, where in zip(mine, theirs, LEFTS):

        @pl.when(is_soon(left_of(*where[:2]), right_of))
        def _():
            add(total, mine_ref, their_ref, where, left_of, core, high, low)


def main_kernel(*refs):
    count, late = len(LEFTS), len(RIGHTS) - HELD
    mine, theirs, rights = refs[:count], refs[count : 2 * count], refs[2 * count : 2 * count + late]
    _, _, _, total, high, low, held_left, held_high, held_low = refs[2 * count + late :]
    left_of, right_of, core = place()
    last = right_of(1, 2)
    spare = left_of(1, 2)

    store_right(rights, RIGHTS[HELD:], right_of, high, low)
    for part in range(2):
        high[last * 2 + part] = jnp.zeros(high.shape[1:], BF16)
        low[last * 2 + part] = jnp.zeros(low.shape[1:], BF16)

    @pl.when(last == spare)
    def _():
        held_left[...] = jnp.zeros_like(held_left)

    for part in range(2):
        held_high[part] = high[spare * 2 + part]
        held_low[part] = low[spare * 2 + part]

    for index, (mine_ref, their_ref, where) in enumerate(zip(mine, theirs, LEFTS)):
        other, turn, half = where
        tile = left_of(other, turn)
        rows = mine_ref.shape[0]
        if index < SOON:

            @pl.when(jnp.logical_not(is_soon(tile, right_of)))
            def _():
                add(total, mine_ref, their_ref, where, left_of, core, high, low)

        else:
            add(total, mine_ref, their_ref, where, left_of, core, high, low)

        @pl.when(tile == last)
        def _():
            side = (core + other + turn) & 1
            held_left[side, pl.ds(half * rows, rows)] = mine_ref[...]
            held_left[1 - side, pl.ds(half * rows, rows)] = their_ref[...]


def last_kernel(total, held_left, held_high, held_low, a0, a1, s0, s1, b0, b1, out, high, low, done, sems):
    left_of, right_of, core = place()
    last = right_of(1, 2)
    spare = left_of(1, 2)
    step = high.shape[1]
    for index, ref in enumerate((b0, b1)):
        high[index], low[index] = split(ref[...])

    @pl.when(last == spare)
    def _():
        held_high[...] = high[...]
        held_low[...] = low[...]

    side = 1 - core
    copies = []
    for block, (mine, theirs) in enumerate(((a0, s0), (a1, s1))):
        rows = pl.ds(block * step, step)
        done[rows] = total[rows] + mul(
            (mine[...], held_high[side], held_low[side]),
            (theirs[...], held_high[1 - side], held_low[1 - side]),
            (held_left[0, rows], high[0], low[0]),
            (held_left[1, rows], high[1], low[1]),
        )
        copies.append(pltpu.make_async_copy(done.at[rows], out.at[rows], sems.at[block]))
        copies[-1].start()
    for copy in copies:
        copy.wait()


def product(a, b):
    tall, wide = a.shape
    deep, broad = b.shape
    half, hill = deep // 2, tall // 2
    inside = pl.BlockSpec(memory_space=pltpu.VMEM)

    a_lo = send(a, "lo")
    a_p, a_m = send(a, "z+"), send(a, "z-")
    b_p, b_m = send(b, "y+"), send(b, "y-")
    b_hi = [send(cut(b, 0, half), "hi"), send(cut(b, half, half), "hi")]
    al_p, al_m = send(a_lo, "z+"), send(a_lo, "z-")
    a_pp = send(cut(a_p, 0, hill), "z+")
    a_mm = send(cut(a_m, hill, hill), "z-")
    b_pp = send(cut(b_p, 0, FAR), "y+")
    b_mm = send(cut(b_m, FAR, deep - FAR), "y-")
    bh_p = [send(b_hi[0], "y+"), send(b_hi[1], "y+")]
    bh_m = [send(b_hi[0], "y-"), send(b_hi[1], "y-")]
    al_pp = send(cut(al_p, 0, hill), "z+")
    al_mm = send(cut(al_m, hill, hill), "z-")
    far_b = send(bh_p[0], "y+"), send(bh_m[1], "y-")

    lefts = (a, a_lo, a_p, a_m, a_pp, a_mm, al_p, al_m)
    others = tuple(send(piece, "core") for piece in lefts)
    rights = (b, b_p, b_m, b_pp, b_mm, b_hi[0], b_hi[1], bh_p[0], bh_m[0], bh_p[1], bh_m[1])
    step = half
    flops = 6 * tall * deep * XL * Z * broad
    shape = jax.ShapeDtypeStruct
    whole, panel = shape((tall, broad), F32), shape((XL * Z * 2, step, broad), BF16)

    def cost(part):
        return pl.CostEstimate(flops=flops * part // 8, bytes_accessed=part << 20, transcendentals=0)

    soon = (*lefts[:SOON], *others[:SOON], *rights[:HELD])
    total, high, low = pl.pallas_call(
        soon_kernel,
        out_shape=(whole, panel, panel),
        in_specs=[inside] * len(soon),
        out_specs=(inside,) * 3,
        compiler_params=pltpu.CompilerParams(vmem_limit_bytes=16 << 20),
        cost_estimate=cost(2),
    )(*soon)
    later = (*lefts, *others, *rights[HELD:])
    total, _, _, held_left, held_high, held_low = pl.pallas_call(
        main_kernel,
        out_shape=(
            whole, panel, panel,
            shape((2, tall, wide), F32),
            shape((2, step, broad), BF16),
            shape((2, step, broad), BF16),
        ),
        in_specs=[inside] * (len(later) + 3),
        out_specs=(inside,) * 6,
        input_output_aliases={len(later) + index: index for index in range(3)},
        compiler_params=pltpu.CompilerParams(vmem_limit_bytes=16 << 20),
        cost_estimate=cost(5),
    )(*later, total, high, low)

    last_s = send(al_pp, "core"), send(al_mm, "core")
    return pl.pallas_call(
        last_kernel,
        out_shape=jax.ShapeDtypeStruct((tall, broad), F32),
        in_specs=[inside] * 10,
        out_specs=pl.BlockSpec(memory_space=pl.ANY),
        scratch_shapes=[pltpu.VMEM((2, step, broad), BF16)] * 2
        + [pltpu.VMEM((tall, broad), F32), pltpu.SemaphoreType.DMA((2,))],
        compiler_params=pltpu.CompilerParams(vmem_limit_bytes=12 << 20),
        cost_estimate=cost(2),
    )(total, held_left, held_high, held_low, al_pp, al_mm, *last_s, *far_b)


def solution(mesh):
    placed = (P("row", "col"), P("row", "col"))
    return jax.shard_map(product, mesh=mesh, in_specs=placed, out_specs=P("row", "col"), check_vma=False)
```

time: 94.7 us -> 97.6 us (1.031)
  waiting for transfers between devices: 44.4 us -> 47.3 us
    ppermute x33 -> x31, waiting for transfers between devices: 44.4 us -> 47.3 us  [send(): return lax.ppermute(array, BOTH, MOVES[move])]
    ppermute x33 -> x31, starting transfers between devices: 40.5 us -> 41.1 us  [send(): return lax.ppermute(array, BOTH, MOVES[move])]
    pallas_call x1 -> x2, Pallas kernels: 5.17 us -> 5.08 us  [the longest x1 2.82 us: product(): pl.pallas_call(main_kernel, out_shape=(whole, panel, panel, shape((2, tal...]
  transfers between devices with their start and end apart: 33 -> 31, of which waited for: 12 -> 10; matrix products, arithmetic and copies ran while one was open for 1% -> 1% of each run, Pallas kernels for 6% -> 5%
where the time goes in v2:
time: 97.6 us; the launch traced here: 96.9 us
  waiting for transfers between devices  47.3 us (48%)
  starting transfers between devices  41.1 us (42%)
  Pallas kernels  6.96 us (7%)
  local copies, waits for them, and re-layouts  1.18 us (1%)
    ppermute x31, waiting for transfers between devices, send(): return lax.ppermute(array, BOTH, MOVES[move])  47.3 us
    ppermute x31, starting transfers between devices, send(): return lax.ppermute(array, BOTH, MOVES[move])  41.1 us
    pallas_call x1, Pallas kernels, product(): pl.pallas_call(main_kernel, out_shape=(whole, panel, panel, shape((2, tal...  2.82 us
    pallas_call x1, Pallas kernels, product(): pl.pallas_call(soon_kernel, out_shape=(whole, panel, panel), in_specs=[in...  2.26 us
  transfers between devices with their start and end apart: 31, of which 10 were waited for; matrix products, arithmetic and copies ran while one was open for 1% of the time, Pallas kernels for 5%

profile of v2, /device:TPU:0, one launch (start us, length us, event | category | flops | bytes accessed | tf_op | source)
XLA Modules:
  0.0 96.9 jit_solution(17232929928119644942)
XLA Ops:
  0.0 1.0 %collective-permute-start = (f32[512,256]{1,0:T(8,128)}, f32[512,256]{1,0:T(8,128)S(1)}, u32[]{:S(2)}, u32[]{:S(2)}) collective-permute-start(f32[512,256]{1,0:T(8,128)} %refs_0_.3), channel_id=1, source_target_pairs={{0,9},{1,8},{2,11},{3,10},{4,13},{5,12},{6,15},{7,14},{8,1},{9,0},... | collective-permute-start | bytes 1572872 | tf_op jit(solution)/shard_map/ppermute | solution.py:40
  1.0 1.1 %fusion = (f32[256,256]{1,0:T(8,128)S(1)}, f32[256,256]{1,0:T(8,128)S(1)}) fusion(f32[512,256]{1,0:T(8,128)} %refs_8_.1), kind=kLoop, calls=%fused_computation | loop fusion | bytes 1048576 | tf_op jit(solution)/shard_map/slice | solution.py:44
  2.1 2.8 %collective-permute-start.15 = (f32[256,256]{1,0:T(8,128)S(1)}, f32[256,256]{1,0:T(8,128)S(1)}, u32[]{:S(2)}, u32[]{:S(2)}) collective-permute-start(f32[256,256]{1,0:T(8,128)S(1)} %get-tuple-element.20), channel_id=1, source_target_pairs={{0,16},{1,17},{2,18},{3,19},{4,20},{5,21},{6,22},{7,23},{8,24},{9,... | collective-permute-start | bytes 786440 | tf_op jit(solution)/shard_map/ppermute | solution.py:40
  4.9 0.8 collective-permute-start.18
  5.7 3.8 %collective-permute-start.2 = (f32[512,256]{1,0:T(8,128)}, f32[512,256]{1,0:T(8,128)S(1)}, u32[]{:S(2)}, u32[]{:S(2)}) collective-permute-start(f32[512,256]{1,0:T(8,128)} %refs_0_.3), channel_id=1, source_target_pairs={{0,7},{1,6},{2,1},{3,0},{4,3},{5,2},{6,5},{7,4},{8,15},{9,14},{10,... | collective-permute-start | bytes 1572872 | tf_op jit(solution)/shard_map/ppermute | solution.py:40
  9.5 12.9 %collective-permute-done.15.refs_13_ = f32[256,256]{1,0:T(8,128)S(1)} collective-permute-done((f32[256,256]{1,0:T(8,128)S(1)}, f32[256,256]{1,0:T(8,128)S(1)}, u32[]{:S(2)}, u32[]{:S(2)}) %collective-permute-start.15) | collective-permute-done | bytes 262176 | tf_op jit(solution)/shard_map/ppermute | solution.py:40
  22.4 1.6 %collective-permute-start.21 = (f32[512,256]{1,0:T(8,128)}, f32[512,256]{1,0:T(8,128)S(1)}, u32[]{:S(2)}, u32[]{:S(2)}) collective-permute-start(f32[512,256]{1,0:T(8,128)} %refs_8_.1), channel_id=1, source_target_pairs={{0,32},{1,33},{2,34},{3,35},{4,36},{5,37},{6,38},{7,39},{8,40},{9,... | collective-permute-start | bytes 1572872 | tf_op jit(solution)/shard_map/ppermute | solution.py:40
  24.0 4.0 %collective-permute-done.18.refs_14_ = f32[256,256]{1,0:T(8,128)S(1)} collective-permute-done((f32[256,256]{1,0:T(8,128)S(1)}, f32[256,256]{1,0:T(8,128)S(1)}, u32[]{:S(2)}, u32[]{:S(2)}) %collective-permute-start.18) | collective-permute-done | bytes 262176 | tf_op jit(solution)/shard_map/ppermute | solution.py:40
  28.0 3.0 %collective-permute-start.22 = (f32[512,256]{1,0:T(8,128)}, f32[512,256]{1,0:T(8,128)S(1)}, u32[]{:S(2)}, u32[]{:S(2)}) collective-permute-start(f32[512,256]{1,0:T(8,128)} %refs_8_.1), channel_id=1, source_target_pairs={{0,96},{1,97},{2,98},{3,99},{4,100},{5,101},{6,102},{7,103},{8,104... | collective-permute-start | bytes 1572872 | tf_op jit(solution)/shard_map/ppermute | solution.py:40
  31.1 3.2 %collective-permute-start.20 = (f32[256,256]{1,0:T(8,128)S(1)}, f32[256,256]{1,0:T(8,128)S(1)}, u32[]{:S(2)}, u32[]{:S(2)}) collective-permute-start(f32[256,256]{1,0:T(8,128)S(1)} %collective-permute-done.18.refs_14_), channel_id=1, source_target_pairs={{0,96},{1,97},{2,98},{3,99},{4,100},{5,101},{6,102},{7,103},{8,104... | collective-permute-start | bytes 786440 | tf_op jit(solution)/shard_map/ppermute | solution.py:40
  34.3 4.3 %collective-permute-done.21.refs_9_ = f32[512,256]{1,0:T(8,128)S(1)} collective-permute-done((f32[512,256]{1,0:T(8,128)}, f32[512,256]{1,0:T(8,128)S(1)}, u32[]{:S(2)}, u32[]{:S(2)}) %collective-permute-start.21) | collective-permute-done | bytes 524320 | tf_op jit(solution)/shard_map/ppermute | solution.py:40
  38.6 1.8 %collective-permute-start.17 = (f32[256,256]{1,0:T(8,128)S(1)}, f32[256,256]{1,0:T(8,128)S(1)}, u32[]{:S(2)}, u32[]{:S(2)}) collective-permute-start(f32[256,256]{1,0:T(8,128)S(1)} %collective-permute-done.15.refs_13_), channel_id=1, source_target_pairs={{0,96},{1,97},{2,98},{3,99},{4,100},{5,101},{6,102},{7,103},{8,104... | collective-permute-start | bytes 786440 | tf_op jit(solution)/shard_map/ppermute | solution.py:40
  40.4 3.2 %collective-permute-done.22.refs_10_ = f32[512,256]{1,0:T(8,128)S(1)} collective-permute-done((f32[512,256]{1,0:T(8,128)}, f32[512,256]{1,0:T(8,128)S(1)}, u32[]{:S(2)}, u32[]{:S(2)}) %collective-permute-start.22) | collective-permute-done | bytes 524320 | tf_op jit(solution)/shard_map/ppermute | solution.py:40
  43.6 0.9 collective-permute-start.19
  44.6 1.6 %collective-permute-start.23 = (f32[256,256]{1,0:T(8,128)S(1)}, f32[256,256]{1,0:T(8,128)S(1)}, u32[]{:S(2)}, u32[]{:S(2)}) collective-permute-start(f32[256,256]{1,0:T(8,128)S(1)} %slice.34), channel_id=1, source_target_pairs={{0,32},{1,33},{2,34},{3,35},{4,36},{5,37},{6,38},{7,39},{8,40},{9,... | collective-permute-start | bytes 786440 | tf_op jit(solution)/shard_map/ppermute | solution.py:40
  46.3 1.7 %collective-permute-start.24 = (f32[256,256]{1,0:T(8,128)S(1)}, f32[256,256]{1,0:T(8,128)S(1)}, u32[]{:S(2)}, u32[]{:S(2)}) collective-permute-start(f32[256,256]{1,0:T(8,128)S(1)} %slice.35), channel_id=1, source_target_pairs={{0,96},{1,97},{2,98},{3,99},{4,100},{5,101},{6,102},{7,103},{8,104... | collective-permute-start | bytes 786440 | tf_op jit(solution)/shard_map/ppermute | solution.py:40
  48.1 1.1 %collective-permute-done.20.refs_19_ = f32[256,256]{1,0:T(8,128)S(1)} collective-permute-done((f32[256,256]{1,0:T(8,128)S(1)}, f32[256,256]{1,0:T(8,128)S(1)}, u32[]{:S(2)}, u32[]{:S(2)}) %collective-permute-start.20) | collective-permute-done | bytes 262176 | tf_op jit(solution)/shard_map/ppermute | solution.py:40
  49.1 5.6 %collective-permute-done.17.refs_17_ = f32[256,256]{1,0:T(8,128)S(1)} collective-permute-done((f32[256,256]{1,0:T(8,128)S(1)}, f32[256,256]{1,0:T(8,128)S(1)}, u32[]{:S(2)}, u32[]{:S(2)}) %collective-permute-start.17) | collective-permute-done | bytes 262176 | tf_op jit(solution)/shard_map/ppermute | solution.py:40
  54.8 2.0 %collective-permute-start.4 = (f32[256,256]{1,0:T(8,128)S(1)}, f32[256,256]{1,0:T(8,128)S(1)}, u32[]{:S(2)}, u32[]{:S(2)}) collective-permute-start(f32[256,256]{1,0:T(8,128)S(1)} %slice.33), channel_id=1, source_target_pairs={{0,7},{1,6},{2,1},{3,0},{4,3},{5,2},{6,5},{7,4},{8,15},{9,14},{10,... | collective-permute-start | bytes 786440 | tf_op jit(solution)/shard_map/ppermute | solution.py:40
  56.8 2.1 %collective-permute-start.8 = (f32[512,256]{1,0:T(8,128)S(1)}, f32[512,256]{1,0:T(8,128)S(1)}, u32[]{:S(2)}, u32[]{:S(2)}) collective-permute-start(f32[512,256]{1,0:T(8,128)S(1)} %collective-permute-done.refs_1_), channel_id=1, source_target_pairs={{0,1},{1,0},{2,3},{3,2},{4,5},{5,4},{6,7},{7,6},{8,9},{9,8},{10,11... | collective-permute-start | bytes 1572872 | tf_op jit(solution)/shard_map/ppermute | solution.py:40
  59.5 2.9 %collective-permute-start.6 = (f32[512,256]{1,0:T(8,128)S(1)}, f32[512,256]{1,0:T(8,128)S(1)}, u32[]{:S(2)}, u32[]{:S(2)}) collective-permute-start(f32[512,256]{1,0:T(8,128)S(1)} %collective-permute-done.refs_1_), channel_id=1, source_target_pairs={{0,7},{1,6},{2,1},{3,0},{4,3},{5,2},{6,5},{7,4},{8,15},{9,14},{10,... | collective-permute-start | bytes 1572872 | tf_op jit(solution)/shard_map/ppermute | solution.py:40
  62.4 1.3 %collective-permute-start.10 = (f32[512,256]{1,0:T(8,128)S(1)}, f32[512,256]{1,0:T(8,128)S(1)}, u32[]{:S(2)}, u32[]{:S(2)}) collective-permute-start(f32[512,256]{1,0:T(8,128)S(1)} %collective-permute-done.2.refs_3_), channel_id=1, source_target_pairs={{0,1},{1,0},{2,3},{3,2},{4,5},{5,4},{6,7},{7,6},{8,9},{9,8},{10,11... | collective-permute-start | bytes 1572872 | tf_op jit(solution)/shard_map/ppermute | solution.py:40
  64.2 9.9 %collective-permute-done.5.refs_6_ = f32[512,256]{1,0:T(8,128)S(1)} collective-permute-done((f32[512,256]{1,0:T(8,128)S(1)}, f32[512,256]{1,0:T(8,128)S(1)}, u32[]{:S(2)}, u32[]{:S(2)}) %collective-permute-start.5) | collective-permute-done | bytes 524320 | tf_op jit(solution)/shard_map/ppermute | solution.py:40
  74.2 0.6 collective-permute-start.14
  75.0 1.6 %collective-permute-start.25 = (f32[256,256]{1,0:T(8,128)S(1)}, f32[256,256]{1,0:T(8,128)S(1)}, u32[]{:S(2)}, u32[]{:S(2)}) collective-permute-start(f32[256,256]{1,0:T(8,128)S(1)} %slice.36), channel_id=1, source_target_pairs={{0,3},{1,2},{2,5},{3,4},{4,7},{5,6},{6,1},{7,0},{8,11},{9,10},{10,... | collective-permute-start | bytes 786440 | tf_op jit(solution)/shard_map/ppermute | solution.py:40
  76.6 2.2 %collective-permute-start.26 = (f32[256,256]{1,0:T(8,128)S(1)}, f32[256,256]{1,0:T(8,128)S(1)}, u32[]{:S(2)}, u32[]{:S(2)}) collective-permute-start(f32[256,256]{1,0:T(8,128)S(1)} %slice.37), channel_id=1, source_target_pairs={{0,7},{1,6},{2,1},{3,0},{4,3},{5,2},{6,5},{7,4},{8,15},{9,14},{10,... | collective-permute-start | bytes 786440 | tf_op jit(solution)/shard_map/ppermute | solution.py:40
  78.8 1.0 %collective-permute-start.29 = (f32[256,256]{1,0:T(8,128)S(1)}, f32[256,256]{1,0:T(8,128)S(1)}, u32[]{:S(2)}, u32[]{:S(2)}) collective-permute-start(f32[256,256]{1,0:T(8,128)S(1)} %collective-permute-done.16.refs_16_), channel_id=1, source_target_pairs={{0,32},{1,33},{2,34},{3,35},{4,36},{5,37},{6,38},{7,39},{8,40},{9,... | collective-permute-start | bytes 786440 | tf_op jit(solution)/shard_map/ppermute | solution.py:40
  79.9 5.1 %collective-permute-done.25.a0 = f32[256,256]{1,0:T(8,128)S(1)} collective-permute-done((f32[256,256]{1,0:T(8,128)S(1)}, f32[256,256]{1,0:T(8,128)S(1)}, u32[]{:S(2)}, u32[]{:S(2)}) %collective-permute-start.25) | collective-permute-done | bytes 262176 | tf_op jit(solution)/shard_map/ppermute | solution.py:40
  85.0 3.7 %collective-permute-start.30 = (f32[256,256]{1,0:T(8,128)S(1)}, f32[256,256]{1,0:T(8,128)S(1)}, u32[]{:S(2)}, u32[]{:S(2)}) collective-permute-start(f32[256,256]{1,0:T(8,128)S(1)} %collective-permute-done.20.refs_19_), channel_id=1, source_target_pairs={{0,96},{1,97},{2,98},{3,99},{4,100},{5,101},{6,102},{7,103},{8,104... | collective-permute-start | bytes 786440 | tf_op jit(solution)/shard_map/ppermute | solution.py:40
  89.2 2.3 %shard_map.28 = (f32[512,256]{1,0:T(8,128)S(1)}, bf16[16,256,256]{2,1,0:T(8,128)(2,1)S(1)}, bf16[16,256,256]{2,1,0:T(8,128)(2,1)S(1)}) custom-call(f32[512,256]{1,0:T(8,128)S(1)} %copy-done, f32[512,256]{1,0:T(8,128)S(1)} %collective-permute-done.refs_1_, f32[512,256]{1,0:T(8,128)S(1)} %collective-permute-done.1.refs_2_, ...), custom_call_target="tpu_custom_call" | custom-call | flops 805306368 | bytes 2097152 | tf_op jit(solution)/shard_map/pallas_call | solution.py:219
  91.5 2.8 %shard_map.29 = (f32[512,256]{1,0:T(8,128)S(1)}, bf16[16,256,256]{2,1,0:T(8,128)(2,1)S(1)}, bf16[16,256,256]{2,1,0:T(8,128)(2,1)S(1)}, f32[2,512,256]{2,1,0:T(8,...) custom-call(f32[512,256]{1,0:T(8,128)S(1)} %copy-done, ...), custom_call_target="tpu_custom_call", output_to_operand_aliasing={{0}: (20, {}), {1}: (21, {}), {2}: (22, {})} | custom-call | flops 2013265920 | bytes 5242880 | tf_op jit(solution)/shard_map/pallas_call | solution.py:228
  94.9 1.9 %shard_map.30 = f32[512,256]{1,0:T(8,128)} custom-call(f32[512,256]{1,0:T(8,128)S(1)} %get-tuple-element.15.total, f32[2,512,256]{2,1,0:T(8,128)S(1)} %get-tuple-element.16.held_left, bf16[2,256,256]{2,1,0:T(8,128)(2,1)S(1)} %get-tuple-element.17.held_high, bf16[2,256,256]{2,1,0:T(8,128)(2,1)S(1)} %get-tuple-element.18.held_low, ...), custom_call_target="tpu_custom_call" | custom-call | flops 805306368 | bytes 2097152 | tf_op jit(solution)/shard_map/pallas_call | solution.py:244
  (44 shorter events, 2.6 us)
Async XLA Ops:
  0.0 89.2 %copy-start.1 = (f32[512,256]{1,0:T(8,128)S(1)}, f32[512,256]{1,0:T(8,128)}, u32[]{:S(2)}) copy-start(f32[512,256]{1,0:T(8,128)} %refs_8_.1) | copy-start | bytes 1572868
  0.0 31.0 %collective-permute-start = (f32[512,256]{1,0:T(8,128)}, f32[512,256]{1,0:T(8,128)S(1)}, u32[]{:S(2)}, u32[]{:S(2)}) collective-permute-start(f32[512,256]{1,0:T(8,128)} %refs_0_.3), channel_id=1, source_target_pairs={{0,9},{1,8},{2,11},{3,10},{4,13},{5,12},{6,15},{7,14},{8,1},{9,0},... | collective-permute-start | bytes 1572872 | tf_op jit(solution)/shard_map/ppermute | solution.py:40
  2.1 20.3 %collective-permute-start.15 = (f32[256,256]{1,0:T(8,128)S(1)}, f32[256,256]{1,0:T(8,128)S(1)}, u32[]{:S(2)}, u32[]{:S(2)}) collective-permute-start(f32[256,256]{1,0:T(8,128)S(1)} %get-tuple-element.20), channel_id=1, source_target_pairs={{0,16},{1,17},{2,18},{3,19},{4,20},{5,21},{6,22},{7,23},{8,24},{9,... | collective-permute-start | bytes 786440 | tf_op jit(solution)/shard_map/ppermute | solution.py:40
  4.9 23.1 %collective-permute-start.18 = (f32[256,256]{1,0:T(8,128)S(1)}, f32[256,256]{1,0:T(8,128)S(1)}, u32[]{:S(2)}, u32[]{:S(2)}) collective-permute-start(f32[256,256]{1,0:T(8,128)S(1)} %get-tuple-element.19), channel_id=1, source_target_pairs={{0,16},{1,17},{2,18},{3,19},{4,20},{5,21},{6,22},{7,23},{8,24},{9,... | collective-permute-start | bytes 786440 | tf_op jit(solution)/shard_map/ppermute | solution.py:40
  5.7 25.3 %collective-permute-start.2 = (f32[512,256]{1,0:T(8,128)}, f32[512,256]{1,0:T(8,128)S(1)}, u32[]{:S(2)}, u32[]{:S(2)}) collective-permute-start(f32[512,256]{1,0:T(8,128)} %refs_0_.3), channel_id=1, source_target_pairs={{0,7},{1,6},{2,1},{3,0},{4,3},{5,2},{6,5},{7,4},{8,15},{9,14},{10,... | collective-permute-start | bytes 1572872 | tf_op jit(solution)/shard_map/ppermute | solution.py:40
  9.5 21.6 %collective-permute-start.1 = (f32[512,256]{1,0:T(8,128)}, f32[512,256]{1,0:T(8,128)S(1)}, u32[]{:S(2)}, u32[]{:S(2)}) collective-permute-start(f32[512,256]{1,0:T(8,128)} %refs_0_.3), channel_id=1, source_target_pairs={{0,3},{1,2},{2,5},{3,4},{4,7},{5,6},{6,1},{7,0},{8,11},{9,10},{10,... | collective-permute-start | bytes 1572872 | tf_op jit(solution)/shard_map/ppermute | solution.py:40
  22.4 16.2 %collective-permute-start.21 = (f32[512,256]{1,0:T(8,128)}, f32[512,256]{1,0:T(8,128)S(1)}, u32[]{:S(2)}, u32[]{:S(2)}) collective-permute-start(f32[512,256]{1,0:T(8,128)} %refs_8_.1), channel_id=1, source_target_pairs={{0,32},{1,33},{2,34},{3,35},{4,36},{5,37},{6,38},{7,39},{8,40},{9,... | collective-permute-start | bytes 1572872 | tf_op jit(solution)/shard_map/ppermute | solution.py:40
  28.0 15.6 %collective-permute-start.22 = (f32[512,256]{1,0:T(8,128)}, f32[512,256]{1,0:T(8,128)S(1)}, u32[]{:S(2)}, u32[]{:S(2)}) collective-permute-start(f32[512,256]{1,0:T(8,128)} %refs_8_.1), channel_id=1, source_target_pairs={{0,96},{1,97},{2,98},{3,99},{4,100},{5,101},{6,102},{7,103},{8,104... | collective-permute-start | bytes 1572872 | tf_op jit(solution)/shard_map/ppermute | solution.py:40
  31.0 13.6 %collective-permute-start.7 = (f32[512,256]{1,0:T(8,128)}, f32[512,256]{1,0:T(8,128)S(1)}, u32[]{:S(2)}, u32[]{:S(2)}) collective-permute-start(f32[512,256]{1,0:T(8,128)} %refs_0_.3), channel_id=1, source_target_pairs={{0,1},{1,0},{2,3},{3,2},{4,5},{5,4},{6,7},{7,6},{8,9},{9,8},{10,11... | collective-permute-start | bytes 1572872 | tf_op jit(solution)/shard_map/ppermute | solution.py:40
  31.0 15.3 %collective-permute-start.16 = (f32[256,256]{1,0:T(8,128)S(1)}, f32[256,256]{1,0:T(8,128)S(1)}, u32[]{:S(2)}, u32[]{:S(2)}) collective-permute-start(f32[256,256]{1,0:T(8,128)S(1)} %collective-permute-done.15.refs_13_), channel_id=1, source_target_pairs={{0,32},{1,33},{2,34},{3,35},{4,36},{5,37},{6,38},{7,39},{8,40},{9,... | collective-permute-start | bytes 786440 | tf_op jit(solution)/shard_map/ppermute | solution.py:40
  31.1 18.0 %collective-permute-start.20 = (f32[256,256]{1,0:T(8,128)S(1)}, f32[256,256]{1,0:T(8,128)S(1)}, u32[]{:S(2)}, u32[]{:S(2)}) collective-permute-start(f32[256,256]{1,0:T(8,128)S(1)} %collective-permute-done.18.refs_14_), channel_id=1, source_target_pairs={{0,96},{1,97},{2,98},{3,99},{4,100},{5,101},{6,102},{7,103},{8,104... | collective-permute-start | bytes 786440 | tf_op jit(solution)/shard_map/ppermute | solution.py:40
  38.6 16.2 %collective-permute-start.17 = (f32[256,256]{1,0:T(8,128)S(1)}, f32[256,256]{1,0:T(8,128)S(1)}, u32[]{:S(2)}, u32[]{:S(2)}) collective-permute-start(f32[256,256]{1,0:T(8,128)S(1)} %collective-permute-done.15.refs_13_), channel_id=1, source_target_pairs={{0,96},{1,97},{2,98},{3,99},{4,100},{5,101},{6,102},{7,103},{8,104... | collective-permute-start | bytes 786440 | tf_op jit(solution)/shard_map/ppermute | solution.py:40
  43.6 13.2 %collective-permute-start.19 = (f32[256,256]{1,0:T(8,128)S(1)}, f32[256,256]{1,0:T(8,128)S(1)}, u32[]{:S(2)}, u32[]{:S(2)}) collective-permute-start(f32[256,256]{1,0:T(8,128)S(1)} %collective-permute-done.18.refs_14_), channel_id=1, source_target_pairs={{0,32},{1,33},{2,34},{3,35},{4,36},{5,37},{6,38},{7,39},{8,40},{9,... | collective-permute-start | bytes 786440 | tf_op jit(solution)/shard_map/ppermute | solution.py:40
  44.6 14.3 %collective-permute-start.23 = (f32[256,256]{1,0:T(8,128)S(1)}, f32[256,256]{1,0:T(8,128)S(1)}, u32[]{:S(2)}, u32[]{:S(2)}) collective-permute-start(f32[256,256]{1,0:T(8,128)S(1)} %slice.34), channel_id=1, source_target_pairs={{0,32},{1,33},{2,34},{3,35},{4,36},{5,37},{6,38},{7,39},{8,40},{9,... | collective-permute-start | bytes 786440 | tf_op jit(solution)/shard_map/ppermute | solution.py:40
  46.3 13.2 %collective-permute-start.24 = (f32[256,256]{1,0:T(8,128)S(1)}, f32[256,256]{1,0:T(8,128)S(1)}, u32[]{:S(2)}, u32[]{:S(2)}) collective-permute-start(f32[256,256]{1,0:T(8,128)S(1)} %slice.35), channel_id=1, source_target_pairs={{0,96},{1,97},{2,98},{3,99},{4,100},{5,101},{6,102},{7,103},{8,104... | collective-permute-start | bytes 786440 | tf_op jit(solution)/shard_map/ppermute | solution.py:40
  49.1 13.3 %collective-permute-start.3 = (f32[256,256]{1,0:T(8,128)S(1)}, f32[256,256]{1,0:T(8,128)S(1)}, u32[]{:S(2)}, u32[]{:S(2)}) collective-permute-start(f32[256,256]{1,0:T(8,128)S(1)} %slice.32), channel_id=1, source_target_pairs={{0,3},{1,2},{2,5},{3,4},{4,7},{5,6},{6,1},{7,0},{8,11},{9,10},{10,... | collective-permute-start | bytes 786440 | tf_op jit(solution)/shard_map/ppermute | solution.py:40
  54.8 8.9 %collective-permute-start.4 = (f32[256,256]{1,0:T(8,128)S(1)}, f32[256,256]{1,0:T(8,128)S(1)}, u32[]{:S(2)}, u32[]{:S(2)}) collective-permute-start(f32[256,256]{1,0:T(8,128)S(1)} %slice.33), channel_id=1, source_target_pairs={{0,7},{1,6},{2,1},{3,0},{4,3},{5,2},{6,5},{7,4},{8,15},{9,14},{10,... | collective-permute-start | bytes 786440 | tf_op jit(solution)/shard_map/ppermute | solution.py:40
  56.8 7.2 %collective-permute-start.8 = (f32[512,256]{1,0:T(8,128)S(1)}, f32[512,256]{1,0:T(8,128)S(1)}, u32[]{:S(2)}, u32[]{:S(2)}) collective-permute-start(f32[512,256]{1,0:T(8,128)S(1)} %collective-permute-done.refs_1_), channel_id=1, source_target_pairs={{0,1},{1,0},{2,3},{3,2},{4,5},{5,4},{6,7},{7,6},{8,9},{9,8},{10,11... | collective-permute-start | bytes 1572872 | tf_op jit(solution)/shard_map/ppermute | solution.py:40
  58.9 15.2 %collective-permute-start.5 = (f32[512,256]{1,0:T(8,128)S(1)}, f32[512,256]{1,0:T(8,128)S(1)}, u32[]{:S(2)}, u32[]{:S(2)}) collective-permute-start(f32[512,256]{1,0:T(8,128)S(1)} %collective-permute-done.refs_1_), channel_id=1, source_target_pairs={{0,3},{1,2},{2,5},{3,4},{4,7},{5,6},{6,1},{7,0},{8,11},{9,10},{10,... | collective-permute-start | bytes 1572872 | tf_op jit(solution)/shard_map/ppermute | solution.py:40
  59.5 14.7 %collective-permute-start.6 = (f32[512,256]{1,0:T(8,128)S(1)}, f32[512,256]{1,0:T(8,128)S(1)}, u32[]{:S(2)}, u32[]{:S(2)}) collective-permute-start(f32[512,256]{1,0:T(8,128)S(1)} %collective-permute-done.refs_1_), channel_id=1, source_target_pairs={{0,7},{1,6},{2,1},{3,0},{4,3},{5,2},{6,5},{7,4},{8,15},{9,14},{10,... | collective-permute-start | bytes 1572872 | tf_op jit(solution)/shard_map/ppermute | solution.py:40
  62.4 12.5 %collective-permute-start.10 = (f32[512,256]{1,0:T(8,128)S(1)}, f32[512,256]{1,0:T(8,128)S(1)}, u32[]{:S(2)}, u32[]{:S(2)}) collective-permute-start(f32[512,256]{1,0:T(8,128)S(1)} %collective-permute-done.2.refs_3_), channel_id=1, source_target_pairs={{0,1},{1,0},{2,3},{3,2},{4,5},{5,4},{6,7},{7,6},{8,9},{9,8},{10,11... | collective-permute-start | bytes 1572872 | tf_op jit(solution)/shard_map/ppermute | solution.py:40
  63.7 11.3 %collective-permute-start.9 = (f32[512,256]{1,0:T(8,128)S(1)}, f32[512,256]{1,0:T(8,128)S(1)}, u32[]{:S(2)}, u32[]{:S(2)}) collective-permute-start(f32[512,256]{1,0:T(8,128)S(1)} %collective-permute-done.1.refs_2_), channel_id=1, source_target_pairs={{0,1},{1,0},{2,3},{3,2},{4,5},{5,4},{6,7},{7,6},{8,9},{9,8},{10,11... | collective-permute-start | bytes 1572872 | tf_op jit(solution)/shard_map/ppermute | solution.py:40
  63.9 12.6 %collective-permute-start.11 = (f32[256,256]{1,0:T(8,128)S(1)}, f32[256,256]{1,0:T(8,128)S(1)}, u32[]{:S(2)}, u32[]{:S(2)}) collective-permute-start(f32[256,256]{1,0:T(8,128)S(1)} %collective-permute-done.3.refs_4_), channel_id=1, source_target_pairs={{0,1},{1,0},{2,3},{3,2},{4,5},{5,4},{6,7},{7,6},{8,9},{9,8},{10,11... | collective-permute-start | bytes 786440 | tf_op jit(solution)/shard_map/ppermute | solution.py:40
  74.1 14.8 %collective-permute-start.13 = (f32[512,256]{1,0:T(8,128)S(1)}, f32[512,256]{1,0:T(8,128)S(1)}, u32[]{:S(2)}, u32[]{:S(2)}) collective-permute-start(f32[512,256]{1,0:T(8,128)S(1)} %collective-permute-done.5.refs_6_), channel_id=1, source_target_pairs={{0,1},{1,0},{2,3},{3,2},{4,5},{5,4},{6,7},{7,6},{8,9},{9,8},{10,11... | collective-permute-start | bytes 1572872 | tf_op jit(solution)/shard_map/ppermute | solution.py:40
  74.2 17.3 %collective-permute-start.14 = (f32[512,256]{1,0:T(8,128)S(1)}, f32[512,256]{1,0:T(8,128)S(1)}, u32[]{:S(2)}, u32[]{:S(2)}) collective-permute-start(f32[512,256]{1,0:T(8,128)S(1)} %collective-permute-done.6.refs_7_), channel_id=1, source_target_pairs={{0,1},{1,0},{2,3},{3,2},{4,5},{5,4},{6,7},{7,6},{8,9},{9,8},{10,11... | collective-permute-start | bytes 1572872 | tf_op jit(solution)/shard_map/ppermute | solution.py:40
  74.9 4.0 %collective-permute-start.12 = (f32[256,256]{1,0:T(8,128)S(1)}, f32[256,256]{1,0:T(8,128)S(1)}, u32[]{:S(2)}, u32[]{:S(2)}) collective-permute-start(f32[256,256]{1,0:T(8,128)S(1)} %collective-permute-done.4.refs_5_), channel_id=1, source_target_pairs={{0,1},{1,0},{2,3},{3,2},{4,5},{5,4},{6,7},{7,6},{8,9},{9,8},{10,11... | collective-permute-start | bytes 786440 | tf_op jit(solution)/shard_map/ppermute | solution.py:40
  75.0 10.0 %collective-permute-start.25 = (f32[256,256]{1,0:T(8,128)S(1)}, f32[256,256]{1,0:T(8,128)S(1)}, u32[]{:S(2)}, u32[]{:S(2)}) collective-permute-start(f32[256,256]{1,0:T(8,128)S(1)} %slice.36), channel_id=1, source_target_pairs={{0,3},{1,2},{2,5},{3,4},{4,7},{5,6},{6,1},{7,0},{8,11},{9,10},{10,... | collective-permute-start | bytes 786440 | tf_op jit(solution)/shard_map/ppermute | solution.py:40
  76.6 12.1 %collective-permute-start.26 = (f32[256,256]{1,0:T(8,128)S(1)}, f32[256,256]{1,0:T(8,128)S(1)}, u32[]{:S(2)}, u32[]{:S(2)}) collective-permute-start(f32[256,256]{1,0:T(8,128)S(1)} %slice.37), channel_id=1, source_target_pairs={{0,7},{1,6},{2,1},{3,0},{4,3},{5,2},{6,5},{7,4},{8,15},{9,14},{10,... | collective-permute-start | bytes 786440 | tf_op jit(solution)/shard_map/ppermute | solution.py:40
  78.8 15.5 %collective-permute-start.29 = (f32[256,256]{1,0:T(8,128)S(1)}, f32[256,256]{1,0:T(8,128)S(1)}, u32[]{:S(2)}, u32[]{:S(2)}) collective-permute-start(f32[256,256]{1,0:T(8,128)S(1)} %collective-permute-done.16.refs_16_), channel_id=1, source_target_pairs={{0,32},{1,33},{2,34},{3,35},{4,36},{5,37},{6,38},{7,39},{8,40},{9,... | collective-permute-start | bytes 786440 | tf_op jit(solution)/shard_map/ppermute | solution.py:40
  85.0 9.8 %collective-permute-start.30 = (f32[256,256]{1,0:T(8,128)S(1)}, f32[256,256]{1,0:T(8,128)S(1)}, u32[]{:S(2)}, u32[]{:S(2)}) collective-permute-start(f32[256,256]{1,0:T(8,128)S(1)} %collective-permute-done.20.refs_19_), channel_id=1, source_target_pairs={{0,96},{1,97},{2,98},{3,99},{4,100},{5,101},{6,102},{7,103},{8,104... | collective-permute-start | bytes 786440 | tf_op jit(solution)/shard_map/ppermute | solution.py:40
  88.7 6.2 %collective-permute-start.27 = (f32[256,256]{1,0:T(8,128)S(1)}, f32[256,256]{1,0:T(8,128)S(1)}, u32[]{:S(2)}, u32[]{:S(2)}) collective-permute-start(f32[256,256]{1,0:T(8,128)S(1)} %collective-permute-done.25.a0), channel_id=1, source_target_pairs={{0,1},{1,0},{2,3},{3,2},{4,5},{5,4},{6,7},{7,6},{8,9},{9,8},{10,11... | collective-permute-start | bytes 786440 | tf_op jit(solution)/shard_map/ppermute | solution.py:40
  88.9 6.0 %collective-permute-start.28 = (f32[256,256]{1,0:T(8,128)S(1)}, f32[256,256]{1,0:T(8,128)S(1)}, u32[]{:S(2)}, u32[]{:S(2)}) collective-permute-start(f32[256,256]{1,0:T(8,128)S(1)} %collective-permute-done.26.a1), channel_id=1, source_target_pairs={{0,1},{1,0},{2,3},{3,2},{4,5},{5,4},{6,7},{7,6},{8,9},{9,8},{10,11... | collective-permute-start | bytes 786440 | tf_op jit(solution)/shard_map/ppermute | solution.py:40
  (1 other events, 89.2 us)

commit v3 on v2

--- a/solution.py
+++ b/solution.py
@@ -138,13 +138,12 @@
         other, turn, half = where
         tile = left_of(other, turn)
         rows = mine_ref.shape[0]
+        open_still = tile != last
         if index < SOON:
-
-            @pl.when(jnp.logical_not(is_soon(tile, right_of)))
-            def _():
-                add(total, mine_ref, their_ref, where, left_of, core, high, low)
-
-        else:
+            open_still &= jnp.logical_not(is_soon(tile, right_of))
+
+        @pl.when(open_still)
+        def _():
             add(total, mine_ref, their_ref, where, left_of, core, high, low)
 
         @pl.when(tile == last)

time: 97.6 us -> 97.6 us (level)
  no operation moved by 1% of the time
where the time goes in v3:
time: 97.6 us; the launch traced here: 96.9 us
  waiting for transfers between devices  47.9 us (49%)
  starting transfers between devices  41.1 us (42%)
  Pallas kernels  6.41 us (7%)
  local copies, waits for them, and re-layouts  1.18 us (1%)
    ppermute x31, waiting for transfers between devices, send(): return lax.ppermute(array, BOTH, MOVES[move])  47.9 us
    ppermute x31, starting transfers between devices, send(): return lax.ppermute(array, BOTH, MOVES[move])  41.1 us
    pallas_call x1, Pallas kernels, product(): pl.pallas_call(main_kernel, out_shape=(whole, panel, panel, shape((2, tal...  2.27 us
    pallas_call x1, Pallas kernels, product(): pl.pallas_call(soon_kernel, out_shape=(whole, panel, panel), in_specs=[in...  2.26 us
  transfers between devices with their start and end apart: 31, of which 10 were waited for; matrix products, arithmetic and copies ran while one was open for 1% of the time, Pallas kernels for 5%

profile of v3, /device:TPU:0, one launch (start us, length us, event | category | flops | bytes accessed | tf_op | source)
XLA Modules:
  0.0 96.9 jit_solution(13299358567478989782)
XLA Ops:
  0.0 1.0 %collective-permute-start = (f32[512,256]{1,0:T(8,128)}, f32[512,256]{1,0:T(8,128)S(1)}, u32[]{:S(2)}, u32[]{:S(2)}) collective-permute-start(f32[512,256]{1,0:T(8,128)} %refs_0_.3), channel_id=1, source_target_pairs={{0,9},{1,8},{2,11},{3,10},{4,13},{5,12},{6,15},{7,14},{8,1},{9,0},... | collective-permute-start | bytes 1572872 | tf_op jit(solution)/shard_map/ppermute | solution.py:40
  1.0 1.1 %fusion = (f32[256,256]{1,0:T(8,128)S(1)}, f32[256,256]{1,0:T(8,128)S(1)}) fusion(f32[512,256]{1,0:T(8,128)} %refs_8_.1), kind=kLoop, calls=%fused_computation | loop fusion | bytes 1048576 | tf_op jit(solution)/shard_map/slice | solution.py:44
  2.1 2.8 %collective-permute-start.15 = (f32[256,256]{1,0:T(8,128)S(1)}, f32[256,256]{1,0:T(8,128)S(1)}, u32[]{:S(2)}, u32[]{:S(2)}) collective-permute-start(f32[256,256]{1,0:T(8,128)S(1)} %get-tuple-element.20), channel_id=1, source_target_pairs={{0,16},{1,17},{2,18},{3,19},{4,20},{5,21},{6,22},{7,23},{8,24},{9,... | collective-permute-start | bytes 786440 | tf_op jit(solution)/shard_map/ppermute | solution.py:40
  4.9 0.8 collective-permute-start.18
  5.7 3.8 %collective-permute-start.2 = (f32[512,256]{1,0:T(8,128)}, f32[512,256]{1,0:T(8,128)S(1)}, u32[]{:S(2)}, u32[]{:S(2)}) collective-permute-start(f32[512,256]{1,0:T(8,128)} %refs_0_.3), channel_id=1, source_target_pairs={{0,7},{1,6},{2,1},{3,0},{4,3},{5,2},{6,5},{7,4},{8,15},{9,14},{10,... | collective-permute-start | bytes 1572872 | tf_op jit(solution)/shard_map/ppermute | solution.py:40
  9.5 12.9 %collective-permute-done.15.refs_13_ = f32[256,256]{1,0:T(8,128)S(1)} collective-permute-done((f32[256,256]{1,0:T(8,128)S(1)}, f32[256,256]{1,0:T(8,128)S(1)}, u32[]{:S(2)}, u32[]{:S(2)}) %collective-permute-start.15) | collective-permute-done | bytes 262176 | tf_op jit(solution)/shard_map/ppermute | solution.py:40
  22.4 1.6 %collective-permute-start.21 = (f32[512,256]{1,0:T(8,128)}, f32[512,256]{1,0:T(8,128)S(1)}, u32[]{:S(2)}, u32[]{:S(2)}) collective-permute-start(f32[512,256]{1,0:T(8,128)} %refs_8_.1), channel_id=1, source_target_pairs={{0,32},{1,33},{2,34},{3,35},{4,36},{5,37},{6,38},{7,39},{8,40},{9,... | collective-permute-start | bytes 1572872 | tf_op jit(solution)/shard_map/ppermute | solution.py:40
  24.0 4.0 %collective-permute-done.18.refs_14_ = f32[256,256]{1,0:T(8,128)S(1)} collective-permute-done((f32[256,256]{1,0:T(8,128)S(1)}, f32[256,256]{1,0:T(8,128)S(1)}, u32[]{:S(2)}, u32[]{:S(2)}) %collective-permute-start.18) | collective-permute-done | bytes 262176 | tf_op jit(solution)/shard_map/ppermute | solution.py:40
  28.0 3.0 %collective-permute-start.22 = (f32[512,256]{1,0:T(8,128)}, f32[512,256]{1,0:T(8,128)S(1)}, u32[]{:S(2)}, u32[]{:S(2)}) collective-permute-start(f32[512,256]{1,0:T(8,128)} %refs_8_.1), channel_id=1, source_target_pairs={{0,96},{1,97},{2,98},{3,99},{4,100},{5,101},{6,102},{7,103},{8,104... | collective-permute-start | bytes 1572872 | tf_op jit(solution)/shard_map/ppermute | solution.py:40
  31.1 3.2 %collective-permute-start.20 = (f32[256,256]{1,0:T(8,128)S(1)}, f32[256,256]{1,0:T(8,128)S(1)}, u32[]{:S(2)}, u32[]{:S(2)}) collective-permute-start(f32[256,256]{1,0:T(8,128)S(1)} %collective-permute-done.18.refs_14_), channel_id=1, source_target_pairs={{0,96},{1,97},{2,98},{3,99},{4,100},{5,101},{6,102},{7,103},{8,104... | collective-permute-start | bytes 786440 | tf_op jit(solution)/shard_map/ppermute | solution.py:40
  34.3 4.3 %collective-permute-done.21.refs_9_ = f32[512,256]{1,0:T(8,128)S(1)} collective-permute-done((f32[512,256]{1,0:T(8,128)}, f32[512,256]{1,0:T(8,128)S(1)}, u32[]{:S(2)}, u32[]{:S(2)}) %collective-permute-start.21) | collective-permute-done | bytes 524320 | tf_op jit(solution)/shard_map/ppermute | solution.py:40
  38.6 1.8 %collective-permute-start.17 = (f32[256,256]{1,0:T(8,128)S(1)}, f32[256,256]{1,0:T(8,128)S(1)}, u32[]{:S(2)}, u32[]{:S(2)}) collective-permute-start(f32[256,256]{1,0:T(8,128)S(1)} %collective-permute-done.15.refs_13_), channel_id=1, source_target_pairs={{0,96},{1,97},{2,98},{3,99},{4,100},{5,101},{6,102},{7,103},{8,104... | collective-permute-start | bytes 786440 | tf_op jit(solution)/shard_map/ppermute | solution.py:40
  40.4 3.2 %collective-permute-done.22.refs_10_ = f32[512,256]{1,0:T(8,128)S(1)} collective-permute-done((f32[512,256]{1,0:T(8,128)}, f32[512,256]{1,0:T(8,128)S(1)}, u32[]{:S(2)}, u32[]{:S(2)}) %collective-permute-start.22) | collective-permute-done | bytes 524320 | tf_op jit(solution)/shard_map/ppermute | solution.py:40
  43.6 0.9 collective-permute-start.19
  44.6 1.6 %collective-permute-start.23 = (f32[256,256]{1,0:T(8,128)S(1)}, f32[256,256]{1,0:T(8,128)S(1)}, u32[]{:S(2)}, u32[]{:S(2)}) collective-permute-start(f32[256,256]{1,0:T(8,128)S(1)} %slice.34), channel_id=1, source_target_pairs={{0,32},{1,33},{2,34},{3,35},{4,36},{5,37},{6,38},{7,39},{8,40},{9,... | collective-permute-start | bytes 786440 | tf_op jit(solution)/shard_map/ppermute | solution.py:40
  46.3 1.7 %collective-permute-start.24 = (f32[256,256]{1,0:T(8,128)S(1)}, f32[256,256]{1,0:T(8,128)S(1)}, u32[]{:S(2)}, u32[]{:S(2)}) collective-permute-start(f32[256,256]{1,0:T(8,128)S(1)} %slice.35), channel_id=1, source_target_pairs={{0,96},{1,97},{2,98},{3,99},{4,100},{5,101},{6,102},{7,103},{8,104... | collective-permute-start | bytes 786440 | tf_op jit(solution)/shard_map/ppermute | solution.py:40
  48.1 1.1 %collective-permute-done.20.refs_19_ = f32[256,256]{1,0:T(8,128)S(1)} collective-permute-done((f32[256,256]{1,0:T(8,128)S(1)}, f32[256,256]{1,0:T(8,128)S(1)}, u32[]{:S(2)}, u32[]{:S(2)}) %collective-permute-start.20) | collective-permute-done | bytes 262176 | tf_op jit(solution)/shard_map/ppermute | solution.py:40
  49.1 5.6 %collective-permute-done.17.refs_17_ = f32[256,256]{1,0:T(8,128)S(1)} collective-permute-done((f32[256,256]{1,0:T(8,128)S(1)}, f32[256,256]{1,0:T(8,128)S(1)}, u32[]{:S(2)}, u32[]{:S(2)}) %collective-permute-start.17) | collective-permute-done | bytes 262176 | tf_op jit(solution)/shard_map/ppermute | solution.py:40
  54.8 2.0 %collective-permute-start.4 = (f32[256,256]{1,0:T(8,128)S(1)}, f32[256,256]{1,0:T(8,128)S(1)}, u32[]{:S(2)}, u32[]{:S(2)}) collective-permute-start(f32[256,256]{1,0:T(8,128)S(1)} %slice.33), channel_id=1, source_target_pairs={{0,7},{1,6},{2,1},{3,0},{4,3},{5,2},{6,5},{7,4},{8,15},{9,14},{10,... | collective-permute-start | bytes 786440 | tf_op jit(solution)/shard_map/ppermute | solution.py:40
  56.8 2.1 %collective-permute-start.8 = (f32[512,256]{1,0:T(8,128)S(1)}, f32[512,256]{1,0:T(8,128)S(1)}, u32[]{:S(2)}, u32[]{:S(2)}) collective-permute-start(f32[512,256]{1,0:T(8,128)S(1)} %collective-permute-done.refs_1_), channel_id=1, source_target_pairs={{0,1},{1,0},{2,3},{3,2},{4,5},{5,4},{6,7},{7,6},{8,9},{9,8},{10,11... | collective-permute-start | bytes 1572872 | tf_op jit(solution)/shard_map/ppermute | solution.py:40
  59.5 2.9 %collective-permute-start.6 = (f32[512,256]{1,0:T(8,128)S(1)}, f32[512,256]{1,0:T(8,128)S(1)}, u32[]{:S(2)}, u32[]{:S(2)}) collective-permute-start(f32[512,256]{1,0:T(8,128)S(1)} %collective-permute-done.refs_1_), channel_id=1, source_target_pairs={{0,7},{1,6},{2,1},{3,0},{4,3},{5,2},{6,5},{7,4},{8,15},{9,14},{10,... | collective-permute-start | bytes 1572872 | tf_op jit(solution)/shard_map/ppermute | solution.py:40
  62.4 1.3 %collective-permute-start.10 = (f32[512,256]{1,0:T(8,128)S(1)}, f32[512,256]{1,0:T(8,128)S(1)}, u32[]{:S(2)}, u32[]{:S(2)}) collective-permute-start(f32[512,256]{1,0:T(8,128)S(1)} %collective-permute-done.2.refs_3_), channel_id=1, source_target_pairs={{0,1},{1,0},{2,3},{3,2},{4,5},{5,4},{6,7},{7,6},{8,9},{9,8},{10,11... | collective-permute-start | bytes 1572872 | tf_op jit(solution)/shard_map/ppermute | solution.py:40
  64.2 9.9 %collective-permute-done.5.refs_6_ = f32[512,256]{1,0:T(8,128)S(1)} collective-permute-done((f32[512,256]{1,0:T(8,128)S(1)}, f32[512,256]{1,0:T(8,128)S(1)}, u32[]{:S(2)}, u32[]{:S(2)}) %collective-permute-start.5) | collective-permute-done | bytes 524320 | tf_op jit(solution)/shard_map/ppermute | solution.py:40
  75.0 1.6 %collective-permute-start.25 = (f32[256,256]{1,0:T(8,128)S(1)}, f32[256,256]{1,0:T(8,128)S(1)}, u32[]{:S(2)}, u32[]{:S(2)}) collective-permute-start(f32[256,256]{1,0:T(8,128)S(1)} %slice.36), channel_id=1, source_target_pairs={{0,3},{1,2},{2,5},{3,4},{4,7},{5,6},{6,1},{7,0},{8,11},{9,10},{10,... | collective-permute-start | bytes 786440 | tf_op jit(solution)/shard_map/ppermute | solution.py:40
  76.6 2.2 %collective-permute-start.26 = (f32[256,256]{1,0:T(8,128)S(1)}, f32[256,256]{1,0:T(8,128)S(1)}, u32[]{:S(2)}, u32[]{:S(2)}) collective-permute-start(f32[256,256]{1,0:T(8,128)S(1)} %slice.37), channel_id=1, source_target_pairs={{0,7},{1,6},{2,1},{3,0},{4,3},{5,2},{6,5},{7,4},{8,15},{9,14},{10,... | collective-permute-start | bytes 786440 | tf_op jit(solution)/shard_map/ppermute | solution.py:40
  78.8 1.0 %collective-permute-start.29 = (f32[256,256]{1,0:T(8,128)S(1)}, f32[256,256]{1,0:T(8,128)S(1)}, u32[]{:S(2)}, u32[]{:S(2)}) collective-permute-start(f32[256,256]{1,0:T(8,128)S(1)} %collective-permute-done.16.refs_16_), channel_id=1, source_target_pairs={{0,32},{1,33},{2,34},{3,35},{4,36},{5,37},{6,38},{7,39},{8,40},{9,... | collective-permute-start | bytes 786440 | tf_op jit(solution)/shard_map/ppermute | solution.py:40
  79.9 5.1 %collective-permute-done.25.a0 = f32[256,256]{1,0:T(8,128)S(1)} collective-permute-done((f32[256,256]{1,0:T(8,128)S(1)}, f32[256,256]{1,0:T(8,128)S(1)}, u32[]{:S(2)}, u32[]{:S(2)}) %collective-permute-start.25) | collective-permute-done | bytes 262176 | tf_op jit(solution)/shard_map/ppermute | solution.py:40
  85.0 3.7 %collective-permute-start.30 = (f32[256,256]{1,0:T(8,128)S(1)}, f32[256,256]{1,0:T(8,128)S(1)}, u32[]{:S(2)}, u32[]{:S(2)}) collective-permute-start(f32[256,256]{1,0:T(8,128)S(1)} %collective-permute-done.20.refs_19_), channel_id=1, source_target_pairs={{0,96},{1,97},{2,98},{3,99},{4,100},{5,101},{6,102},{7,103},{8,104... | collective-permute-start | bytes 786440 | tf_op jit(solution)/shard_map/ppermute | solution.py:40
  89.2 2.3 %shard_map.28 = (f32[512,256]{1,0:T(8,128)S(1)}, bf16[16,256,256]{2,1,0:T(8,128)(2,1)S(1)}, bf16[16,256,256]{2,1,0:T(8,128)(2,1)S(1)}) custom-call(f32[512,256]{1,0:T(8,128)S(1)} %copy-done, f32[512,256]{1,0:T(8,128)S(1)} %collective-permute-done.refs_1_, f32[512,256]{1,0:T(8,128)S(1)} %collective-permute-done.1.refs_2_, ...), custom_call_target="tpu_custom_call" | custom-call | flops 805306368 | bytes 2097152 | tf_op jit(solution)/shard_map/pallas_call | solution.py:218
  91.5 2.3 %shard_map.29 = (f32[512,256]{1,0:T(8,128)S(1)}, bf16[16,256,256]{2,1,0:T(8,128)(2,1)S(1)}, bf16[16,256,256]{2,1,0:T(8,128)(2,1)S(1)}, f32[2,512,256]{2,1,0:T(8,...) custom-call(f32[512,256]{1,0:T(8,128)S(1)} %copy-done, ...), custom_call_target="tpu_custom_call", output_to_operand_aliasing={{0}: (20, {}), {1}: (21, {}), {2}: (22, {})} | custom-call | flops 2013265920 | bytes 5242880 | tf_op jit(solution)/shard_map/pallas_call | solution.py:227
  93.8 1.1 %collective-permute-done.30.b1 = f32[256,256]{1,0:T(8,128)S(1)} collective-permute-done((f32[256,256]{1,0:T(8,128)S(1)}, f32[256,256]{1,0:T(8,128)S(1)}, u32[]{:S(2)}, u32[]{:S(2)}) %collective-permute-start.30) | collective-permute-done | bytes 262176 | tf_op jit(solution)/shard_map/ppermute | solution.py:40
  94.9 1.9 %shard_map.30 = f32[512,256]{1,0:T(8,128)} custom-call(f32[512,256]{1,0:T(8,128)S(1)} %get-tuple-element.15.total, f32[2,512,256]{2,1,0:T(8,128)S(1)} %get-tuple-element.16.held_left, bf16[2,256,256]{2,1,0:T(8,128)(2,1)S(1)} %get-tuple-element.17.held_high, bf16[2,256,256]{2,1,0:T(8,128)(2,1)S(1)} %get-tuple-element.18.held_low, ...), custom_call_target="tpu_custom_call" | custom-call | flops 805306368 | bytes 2097152 | tf_op jit(solution)/shard_map/pallas_call | solution.py:243
  (44 shorter events, 2.7 us)
Async XLA Ops:
  0.0 89.2 %copy-start.1 = (f32[512,256]{1,0:T(8,128)S(1)}, f32[512,256]{1,0:T(8,128)}, u32[]{:S(2)}) copy-start(f32[512,256]{1,0:T(8,128)} %refs_8_.1) | copy-start | bytes 1572868
  0.0 31.0 %collective-permute-start = (f32[512,256]{1,0:T(8,128)}, f32[512,256]{1,0:T(8,128)S(1)}, u32[]{:S(2)}, u32[]{:S(2)}) collective-permute-start(f32[512,256]{1,0:T(8,128)} %refs_0_.3), channel_id=1, source_target_pairs={{0,9},{1,8},{2,11},{3,10},{4,13},{5,12},{6,15},{7,14},{8,1},{9,0},... | collective-permute-start | bytes 1572872 | tf_op jit(solution)/shard_map/ppermute | solution.py:40
  2.1 20.3 %collective-permute-start.15 = (f32[256,256]{1,0:T(8,128)S(1)}, f32[256,256]{1,0:T(8,128)S(1)}, u32[]{:S(2)}, u32[]{:S(2)}) collective-permute-start(f32[256,256]{1,0:T(8,128)S(1)} %get-tuple-element.20), channel_id=1, source_target_pairs={{0,16},{1,17},{2,18},{3,19},{4,20},{5,21},{6,22},{7,23},{8,24},{9,... | collective-permute-start | bytes 786440 | tf_op jit(solution)/shard_map/ppermute | solution.py:40
  4.9 23.1 %collective-permute-start.18 = (f32[256,256]{1,0:T(8,128)S(1)}, f32[256,256]{1,0:T(8,128)S(1)}, u32[]{:S(2)}, u32[]{:S(2)}) collective-permute-start(f32[256,256]{1,0:T(8,128)S(1)} %get-tuple-element.19), channel_id=1, source_target_pairs={{0,16},{1,17},{2,18},{3,19},{4,20},{5,21},{6,22},{7,23},{8,24},{9,... | collective-permute-start | bytes 786440 | tf_op jit(solution)/shard_map/ppermute | solution.py:40
  5.7 25.3 %collective-permute-start.2 = (f32[512,256]{1,0:T(8,128)}, f32[512,256]{1,0:T(8,128)S(1)}, u32[]{:S(2)}, u32[]{:S(2)}) collective-permute-start(f32[512,256]{1,0:T(8,128)} %refs_0_.3), channel_id=1, source_target_pairs={{0,7},{1,6},{2,1},{3,0},{4,3},{5,2},{6,5},{7,4},{8,15},{9,14},{10,... | collective-permute-start | bytes 1572872 | tf_op jit(solution)/shard_map/ppermute | solution.py:40
  9.5 21.6 %collective-permute-start.1 = (f32[512,256]{1,0:T(8,128)}, f32[512,256]{1,0:T(8,128)S(1)}, u32[]{:S(2)}, u32[]{:S(2)}) collective-permute-start(f32[512,256]{1,0:T(8,128)} %refs_0_.3), channel_id=1, source_target_pairs={{0,3},{1,2},{2,5},{3,4},{4,7},{5,6},{6,1},{7,0},{8,11},{9,10},{10,... | collective-permute-start | bytes 1572872 | tf_op jit(solution)/shard_map/ppermute | solution.py:40
  22.4 16.2 %collective-permute-start.21 = (f32[512,256]{1,0:T(8,128)}, f32[512,256]{1,0:T(8,128)S(1)}, u32[]{:S(2)}, u32[]{:S(2)}) collective-permute-start(f32[512,256]{1,0:T(8,128)} %refs_8_.1), channel_id=1, source_target_pairs={{0,32},{1,33},{2,34},{3,35},{4,36},{5,37},{6,38},{7,39},{8,40},{9,... | collective-permute-start | bytes 1572872 | tf_op jit(solution)/shard_map/ppermute | solution.py:40
  28.0 15.6 %collective-permute-start.22 = (f32[512,256]{1,0:T(8,128)}, f32[512,256]{1,0:T(8,128)S(1)}, u32[]{:S(2)}, u32[]{:S(2)}) collective-permute-start(f32[512,256]{1,0:T(8,128)} %refs_8_.1), channel_id=1, source_target_pairs={{0,96},{1,97},{2,98},{3,99},{4,100},{5,101},{6,102},{7,103},{8,104... | collective-permute-start | bytes 1572872 | tf_op jit(solution)/shard_map/ppermute | solution.py:40
  31.0 13.6 %collective-permute-start.7 = (f32[512,256]{1,0:T(8,128)}, f32[512,256]{1,0:T(8,128)S(1)}, u32[]{:S(2)}, u32[]{:S(2)}) collective-permute-start(f32[512,256]{1,0:T(8,128)} %refs_0_.3), channel_id=1, source_target_pairs={{0,1},{1,0},{2,3},{3,2},{4,5},{5,4},{6,7},{7,6},{8,9},{9,8},{10,11... | collective-permute-start | bytes 1572872 | tf_op jit(solution)/shard_map/ppermute | solution.py:40
  31.0 15.3 %collective-permute-start.16 = (f32[256,256]{1,0:T(8,128)S(1)}, f32[256,256]{1,0:T(8,128)S(1)}, u32[]{:S(2)}, u32[]{:S(2)}) collective-permute-start(f32[256,256]{1,0:T(8,128)S(1)} %collective-permute-done.15.refs_13_), channel_id=1, source_target_pairs={{0,32},{1,33},{2,34},{3,35},{4,36},{5,37},{6,38},{7,39},{8,40},{9,... | collective-permute-start | bytes 786440 | tf_op jit(solution)/shard_map/ppermute | solution.py:40
  31.1 18.0 %collective-permute-start.20 = (f32[256,256]{1,0:T(8,128)S(1)}, f32[256,256]{1,0:T(8,128)S(1)}, u32[]{:S(2)}, u32[]{:S(2)}) collective-permute-start(f32[256,256]{1,0:T(8,128)S(1)} %collective-permute-done.18.refs_14_), channel_id=1, source_target_pairs={{0,96},{1,97},{2,98},{3,99},{4,100},{5,101},{6,102},{7,103},{8,104... | collective-permute-start | bytes 786440 | tf_op jit(solution)/shard_map/ppermute | solution.py:40
  38.6 16.2 %collective-permute-start.17 = (f32[256,256]{1,0:T(8,128)S(1)}, f32[256,256]{1,0:T(8,128)S(1)}, u32[]{:S(2)}, u32[]{:S(2)}) collective-permute-start(f32[256,256]{1,0:T(8,128)S(1)} %collective-permute-done.15.refs_13_), channel_id=1, source_target_pairs={{0,96},{1,97},{2,98},{3,99},{4,100},{5,101},{6,102},{7,103},{8,104... | collective-permute-start | bytes 786440 | tf_op jit(solution)/shard_map/ppermute | solution.py:40
  43.6 13.2 %collective-permute-start.19 = (f32[256,256]{1,0:T(8,128)S(1)}, f32[256,256]{1,0:T(8,128)S(1)}, u32[]{:S(2)}, u32[]{:S(2)}) collective-permute-start(f32[256,256]{1,0:T(8,128)S(1)} %collective-permute-done.18.refs_14_), channel_id=1, source_target_pairs={{0,32},{1,33},{2,34},{3,35},{4,36},{5,37},{6,38},{7,39},{8,40},{9,... | collective-permute-start | bytes 786440 | tf_op jit(solution)/shard_map/ppermute | solution.py:40
  44.6 14.3 %collective-permute-start.23 = (f32[256,256]{1,0:T(8,128)S(1)}, f32[256,256]{1,0:T(8,128)S(1)}, u32[]{:S(2)}, u32[]{:S(2)}) collective-permute-start(f32[256,256]{1,0:T(8,128)S(1)} %slice.34), channel_id=1, source_target_pairs={{0,32},{1,33},{2,34},{3,35},{4,36},{5,37},{6,38},{7,39},{8,40},{9,... | collective-permute-start | bytes 786440 | tf_op jit(solution)/shard_map/ppermute | solution.py:40
  46.3 13.2 %collective-permute-start.24 = (f32[256,256]{1,0:T(8,128)S(1)}, f32[256,256]{1,0:T(8,128)S(1)}, u32[]{:S(2)}, u32[]{:S(2)}) collective-permute-start(f32[256,256]{1,0:T(8,128)S(1)} %slice.35), channel_id=1, source_target_pairs={{0,96},{1,97},{2,98},{3,99},{4,100},{5,101},{6,102},{7,103},{8,104... | collective-permute-start | bytes 786440 | tf_op jit(solution)/shard_map/ppermute | solution.py:40
  49.1 13.3 %collective-permute-start.3 = (f32[256,256]{1,0:T(8,128)S(1)}, f32[256,256]{1,0:T(8,128)S(1)}, u32[]{:S(2)}, u32[]{:S(2)}) collective-permute-start(f32[256,256]{1,0:T(8,128)S(1)} %slice.32), channel_id=1, source_target_pairs={{0,3},{1,2},{2,5},{3,4},{4,7},{5,6},{6,1},{7,0},{8,11},{9,10},{10,... | collective-permute-start | bytes 786440 | tf_op jit(solution)/shard_map/ppermute | solution.py:40
  54.8 8.9 %collective-permute-start.4 = (f32[256,256]{1,0:T(8,128)S(1)}, f32[256,256]{1,0:T(8,128)S(1)}, u32[]{:S(2)}, u32[]{:S(2)}) collective-permute-start(f32[256,256]{1,0:T(8,128)S(1)} %slice.33), channel_id=1, source_target_pairs={{0,7},{1,6},{2,1},{3,0},{4,3},{5,2},{6,5},{7,4},{8,15},{9,14},{10,... | collective-permute-start | bytes 786440 | tf_op jit(solution)/shard_map/ppermute | solution.py:40
  56.8 7.2 %collective-permute-start.8 = (f32[512,256]{1,0:T(8,128)S(1)}, f32[512,256]{1,0:T(8,128)S(1)}, u32[]{:S(2)}, u32[]{:S(2)}) collective-permute-start(f32[512,256]{1,0:T(8,128)S(1)} %collective-permute-done.refs_1_), channel_id=1, source_target_pairs={{0,1},{1,0},{2,3},{3,2},{4,5},{5,4},{6,7},{7,6},{8,9},{9,8},{10,11... | collective-permute-start | bytes 1572872 | tf_op jit(solution)/shard_map/ppermute | solution.py:40
  58.9 15.2 %collective-permute-start.5 = (f32[512,256]{1,0:T(8,128)S(1)}, f32[512,256]{1,0:T(8,128)S(1)}, u32[]{:S(2)}, u32[]{:S(2)}) collective-permute-start(f32[512,256]{1,0:T(8,128)S(1)} %collective-permute-done.refs_1_), channel_id=1, source_target_pairs={{0,3},{1,2},{2,5},{3,4},{4,7},{5,6},{6,1},{7,0},{8,11},{9,10},{10,... | collective-permute-start | bytes 1572872 | tf_op jit(solution)/shard_map/ppermute | solution.py:40
  59.5 14.7 %collective-permute-start.6 = (f32[512,256]{1,0:T(8,128)S(1)}, f32[512,256]{1,0:T(8,128)S(1)}, u32[]{:S(2)}, u32[]{:S(2)}) collective-permute-start(f32[512,256]{1,0:T(8,128)S(1)} %collective-permute-done.refs_1_), channel_id=1, source_target_pairs={{0,7},{1,6},{2,1},{3,0},{4,3},{5,2},{6,5},{7,4},{8,15},{9,14},{10,... | collective-permute-start | bytes 1572872 | tf_op jit(solution)/shard_map/ppermute | solution.py:40
  62.4 12.5 %collective-permute-start.10 = (f32[512,256]{1,0:T(8,128)S(1)}, f32[512,256]{1,0:T(8,128)S(1)}, u32[]{:S(2)}, u32[]{:S(2)}) collective-permute-start(f32[512,256]{1,0:T(8,128)S(1)} %collective-permute-done.2.refs_3_), channel_id=1, source_target_pairs={{0,1},{1,0},{2,3},{3,2},{4,5},{5,4},{6,7},{7,6},{8,9},{9,8},{10,11... | collective-permute-start | bytes 1572872 | tf_op jit(solution)/shard_map/ppermute | solution.py:40
  63.7 11.3 %collective-permute-start.9 = (f32[512,256]{1,0:T(8,128)S(1)}, f32[512,256]{1,0:T(8,128)S(1)}, u32[]{:S(2)}, u32[]{:S(2)}) collective-permute-start(f32[512,256]{1,0:T(8,128)S(1)} %collective-permute-done.1.refs_2_), channel_id=1, source_target_pairs={{0,1},{1,0},{2,3},{3,2},{4,5},{5,4},{6,7},{7,6},{8,9},{9,8},{10,11... | collective-permute-start | bytes 1572872 | tf_op jit(solution)/shard_map/ppermute | solution.py:40
  63.9 12.6 %collective-permute-start.11 = (f32[256,256]{1,0:T(8,128)S(1)}, f32[256,256]{1,0:T(8,128)S(1)}, u32[]{:S(2)}, u32[]{:S(2)}) collective-permute-start(f32[256,256]{1,0:T(8,128)S(1)} %collective-permute-done.3.refs_4_), channel_id=1, source_target_pairs={{0,1},{1,0},{2,3},{3,2},{4,5},{5,4},{6,7},{7,6},{8,9},{9,8},{10,11... | collective-permute-start | bytes 786440 | tf_op jit(solution)/shard_map/ppermute | solution.py:40
  74.1 14.8 %collective-permute-start.13 = (f32[512,256]{1,0:T(8,128)S(1)}, f32[512,256]{1,0:T(8,128)S(1)}, u32[]{:S(2)}, u32[]{:S(2)}) collective-permute-start(f32[512,256]{1,0:T(8,128)S(1)} %collective-permute-done.5.refs_6_), channel_id=1, source_target_pairs={{0,1},{1,0},{2,3},{3,2},{4,5},{5,4},{6,7},{7,6},{8,9},{9,8},{10,11... | collective-permute-start | bytes 1572872 | tf_op jit(solution)/shard_map/ppermute | solution.py:40
  74.2 17.3 %collective-permute-start.14 = (f32[512,256]{1,0:T(8,128)S(1)}, f32[512,256]{1,0:T(8,128)S(1)}, u32[]{:S(2)}, u32[]{:S(2)}) collective-permute-start(f32[512,256]{1,0:T(8,128)S(1)} %collective-permute-done.6.refs_7_), channel_id=1, source_target_pairs={{0,1},{1,0},{2,3},{3,2},{4,5},{5,4},{6,7},{7,6},{8,9},{9,8},{10,11... | collective-permute-start | bytes 1572872 | tf_op jit(solution)/shard_map/ppermute | solution.py:40
  74.9 4.0 %collective-permute-start.12 = (f32[256,256]{1,0:T(8,128)S(1)}, f32[256,256]{1,0:T(8,128)S(1)}, u32[]{:S(2)}, u32[]{:S(2)}) collective-permute-start(f32[256,256]{1,0:T(8,128)S(1)} %collective-permute-done.4.refs_5_), channel_id=1, source_target_pairs={{0,1},{1,0},{2,3},{3,2},{4,5},{5,4},{6,7},{7,6},{8,9},{9,8},{10,11... | collective-permute-start | bytes 786440 | tf_op jit(solution)/shard_map/ppermute | solution.py:40
  75.0 10.0 %collective-permute-start.25 = (f32[256,256]{1,0:T(8,128)S(1)}, f32[256,256]{1,0:T(8,128)S(1)}, u32[]{:S(2)}, u32[]{:S(2)}) collective-permute-start(f32[256,256]{1,0:T(8,128)S(1)} %slice.36), channel_id=1, source_target_pairs={{0,3},{1,2},{2,5},{3,4},{4,7},{5,6},{6,1},{7,0},{8,11},{9,10},{10,... | collective-permute-start | bytes 786440 | tf_op jit(solution)/shard_map/ppermute | solution.py:40
  76.6 12.1 %collective-permute-start.26 = (f32[256,256]{1,0:T(8,128)S(1)}, f32[256,256]{1,0:T(8,128)S(1)}, u32[]{:S(2)}, u32[]{:S(2)}) collective-permute-start(f32[256,256]{1,0:T(8,128)S(1)} %slice.37), channel_id=1, source_target_pairs={{0,7},{1,6},{2,1},{3,0},{4,3},{5,2},{6,5},{7,4},{8,15},{9,14},{10,... | collective-permute-start | bytes 786440 | tf_op jit(solution)/shard_map/ppermute | solution.py:40
  78.8 14.9 %collective-permute-start.29 = (f32[256,256]{1,0:T(8,128)S(1)}, f32[256,256]{1,0:T(8,128)S(1)}, u32[]{:S(2)}, u32[]{:S(2)}) collective-permute-start(f32[256,256]{1,0:T(8,128)S(1)} %collective-permute-done.16.refs_16_), channel_id=1, source_target_pairs={{0,32},{1,33},{2,34},{3,35},{4,36},{5,37},{6,38},{7,39},{8,40},{9,... | collective-permute-start | bytes 786440 | tf_op jit(solution)/shard_map/ppermute | solution.py:40
  85.0 9.8 %collective-permute-start.30 = (f32[256,256]{1,0:T(8,128)S(1)}, f32[256,256]{1,0:T(8,128)S(1)}, u32[]{:S(2)}, u32[]{:S(2)}) collective-permute-start(f32[256,256]{1,0:T(8,128)S(1)} %collective-permute-done.20.refs_19_), channel_id=1, source_target_pairs={{0,96},{1,97},{2,98},{3,99},{4,100},{5,101},{6,102},{7,103},{8,104... | collective-permute-start | bytes 786440 | tf_op jit(solution)/shard_map/ppermute | solution.py:40
  88.7 6.2 %collective-permute-start.27 = (f32[256,256]{1,0:T(8,128)S(1)}, f32[256,256]{1,0:T(8,128)S(1)}, u32[]{:S(2)}, u32[]{:S(2)}) collective-permute-start(f32[256,256]{1,0:T(8,128)S(1)} %collective-permute-done.25.a0), channel_id=1, source_target_pairs={{0,1},{1,0},{2,3},{3,2},{4,5},{5,4},{6,7},{7,6},{8,9},{9,8},{10,11... | collective-permute-start | bytes 786440 | tf_op jit(solution)/shard_map/ppermute | solution.py:40
  88.9 6.0 %collective-permute-start.28 = (f32[256,256]{1,0:T(8,128)S(1)}, f32[256,256]{1,0:T(8,128)S(1)}, u32[]{:S(2)}, u32[]{:S(2)}) collective-permute-start(f32[256,256]{1,0:T(8,128)S(1)} %collective-permute-done.26.a1), channel_id=1, source_target_pairs={{0,1},{1,0},{2,3},{3,2},{4,5},{5,4},{6,7},{7,6},{8,9},{9,8},{10,11... | collective-permute-start | bytes 786440 | tf_op jit(solution)/shard_map/ppermute | solution.py:40
  (1 other events, 89.2 us)

commit v4 on v3

--- a/solution.py
+++ b/solution.py
@@ -44,6 +44,10 @@
     return array[top : top + rows]
 
 
+def cat(*arrays):
+    return jnp.concatenate(arrays)
+
+
 def place():
     row, col = lax.axis_index("row"), lax.axis_index("col")
     y, xh = row >> 1, row & 1
@@ -67,7 +71,7 @@
     return jnp.dot(jnp.concatenate(lefts, axis=1), jnp.concatenate(rights), preferred_element_type=F32)
 
 
-LEFTS = ((0, 0, 0), (1, 0, 0), (0, 3, 0), (0, 1, 0), (0, 2, 0), (0, 2, 1), (1, 3, 0), (1, 1, 0))
+LEFTS = ((0, 0), (1, 0), (0, 3), (0, 1), (0, 2), (1, 3), (1, 1))
 ROWS, FAR = 64, 256
 RIGHTS = (
     (0, 0, 0), (0, 3, 0), (0, 1, 0), (0, 2, 0), (0, 2, FAR), (1, 0, 0), (1, 0, 256),
@@ -85,38 +89,45 @@
 
 
 def add(total, mine, theirs, place_of, left_of, core, high, low):
-    other, turn, half = place_of
+    other, turn = place_of
     tile = left_of(other, turn)
     rows, step = mine.shape[0], high.shape[1]
     side = (core + other + turn) & 1
     at, beside = tile * 2 + side, tile * 2 + 1 - side
     for block in range(rows // step):
         rows_in = pl.ds(block * step, step)
-        rows_out = pl.ds(half * rows + block * step, step)
-        total[rows_out] += mul((mine[rows_in], high[at], low[at]), (theirs[rows_in], high[beside], low[beside]))
+        total[rows_in] += mul((mine[rows_in], high[at], low[at]), (theirs[rows_in], high[beside], low[beside]))
 
 
 def is_soon(tile, right_of):
     return ((tile & 1) == (right_of(0, 0) & 1)) | (tile == right_of(1, 0))
 
 
+def parts(ref, count):
+    rows = ref.shape[0] // count
+    return tuple(ref.at[pl.ds(index * rows, rows)] for index in range(count))
+
+
 def soon_kernel(*refs):
-    mine, theirs, rights = refs[:SOON], refs[SOON : 2 * SOON], refs[2 * SOON : 2 * SOON + HELD]
-    total, high, low = refs[2 * SOON + HELD :]
+    mine, rights = refs[:SOON], refs[SOON + 2 : SOON + 2 + HELD]
+    theirs = (refs[SOON], *parts(refs[SOON + 1], SOON - 1))
+    total, high, low = refs[SOON + 2 + HELD :]
     left_of, right_of, core = place()
     store_right(rights, RIGHTS[:HELD], right_of, high, low)
     total[...] = jnp.zeros_like(total)
     for mine_ref, their_ref, where in zip(mine, theirs, LEFTS):
 
-        @pl.when(is_soon(left_of(*where[:2]), right_of))
+        @pl.when(is_soon(left_of(*where), right_of))
         def _():
             add(total, mine_ref, their_ref, where, left_of, core, high, low)
 
 
 def main_kernel(*refs):
     count, late = len(LEFTS), len(RIGHTS) - HELD
-    mine, theirs, rights = refs[:count], refs[count : 2 * count], refs[2 * count : 2 * count + late]
-    _, _, _, total, high, low, held_left, held_high, held_low = refs[2 * count + late :]
+    mine, rights = refs[:count], refs[count + 4 : count + 4 + late]
+    own, one, far, two = refs[count : count + 4]
+    theirs = (own, *parts(one, SOON - 1), far, *parts(two, 2))
+    _, _, _, total, high, low, held_left, held_high, held_low = refs[count + 4 + late :]
     left_of, right_of, core = place()
     last = right_of(1, 2)
     spare = left_of(1, 2)
@@ -135,9 +146,8 @@
         held_low[part] = low[spare * 2 + part]
 
     for index, (mine_ref, their_ref, where) in enumerate(zip(mine, theirs, LEFTS)):
-        other, turn, half = where
+        other, turn = where
         tile = left_of(other, turn)
-        rows = mine_ref.shape[0]
         open_still = tile != last
         if index < SOON:
             open_still &= jnp.logical_not(is_soon(tile, right_of))
@@ -149,11 +159,11 @@
         @pl.when(tile == last)
         def _():
             side = (core + other + turn) & 1
-            held_left[side, pl.ds(half * rows, rows)] = mine_ref[...]
-            held_left[1 - side, pl.ds(half * rows, rows)] = their_ref[...]
-
-
-def last_kernel(total, held_left, held_high, held_low, a0, a1, s0, s1, b0, b1, out, high, low, done, sems):
+            held_left[side] = mine_ref[...]
+            held_left[1 - side] = their_ref[...]
+
+
+def last_kernel(total, held_left, held_high, held_low, mine, theirs, b0, b1, out, high, low, done, sems):
     left_of, right_of, core = place()
     last = right_of(1, 2)
     spare = left_of(1, 2)
@@ -168,11 +178,11 @@
 
     side = 1 - core
     copies = []
-    for block, (mine, theirs) in enumerate(((a0, s0), (a1, s1))):
+    for block in range(mine.shape[0] // step):
         rows = pl.ds(block * step, step)
         done[rows] = total[rows] + mul(
-            (mine[...], held_high[side], held_low[side]),
-            (theirs[...], held_high[1 - side], held_low[1 - side]),
+            (mine[rows], held_high[side], held_low[side]),
+            (theirs[rows], held_high[1 - side], held_low[1 - side]),
             (held_left[0, rows], high[0], low[0]),
             (held_left[1, rows], high[1], low[1]),
         )
@@ -203,8 +213,12 @@
     al_mm = send(cut(al_m, hill, hill), "z-")
     far_b = send(bh_p[0], "y+"), send(bh_m[1], "y-")
 
-    lefts = (a, a_lo, a_p, a_m, a_pp, a_mm, al_p, al_m)
-    others = tuple(send(piece, "core") for piece in lefts)
+    a_far = cat(a_pp, a_mm)
+    lefts = (a, a_lo, a_p, a_m, a_far, al_p, al_m)
+    own = send(a, "core")
+    one = send(cat(a_lo, a_p, a_m), "core")
+    two = send(cat(al_p, al_m), "core")
+    far = send(a_far, "core")
     rights = (b, b_p, b_m, b_pp, b_mm, b_hi[0], b_hi[1], bh_p[0], bh_m[0], bh_p[1], bh_m[1])
     step = half
     flops = 6 * tall * deep * XL * Z * broad
@@ -214,7 +228,7 @@
     def cost(part):
         return pl.CostEstimate(flops=flops * part // 8, bytes_accessed=part << 20, transcendentals=0)
 
-    soon = (*lefts[:SOON], *others[:SOON], *rights[:HELD])
+    soon = (*lefts[:SOON], own, one, *rights[:HELD])
     total, high, low = pl.pallas_call(
         soon_kernel,
         out_shape=(whole, panel, panel),
@@ -223,7 +237,7 @@
         compiler_params=pltpu.CompilerParams(vmem_limit_bytes=16 << 20),
         cost_estimate=cost(2),
     )(*soon)
-    later = (*lefts, *others, *rights[HELD:])
+    later = (*lefts, own, one, far, two, *rights[HELD:])
     total, _, _, held_left, held_high, held_low = pl.pallas_call(
         main_kernel,
         out_shape=(
@@ -239,17 +253,18 @@
         cost_estimate=cost(5),
     )(*later, total, high, low)
 
-    last_s = send(al_pp, "core"), send(al_mm, "core")
+    last_a = cat(al_pp, al_mm)
+    last_s = send(last_a, "core")
     return pl.pallas_call(
         last_kernel,
         out_shape=jax.ShapeDtypeStruct((tall, broad), F32),
-        in_specs=[inside] * 10,
+        in_specs=[inside] * 8,
         out_specs=pl.BlockSpec(memory_space=pl.ANY),
         scratch_shapes=[pltpu.VMEM((2, step, broad), BF16)] * 2
         + [pltpu.VMEM((tall, broad), F32), pltpu.SemaphoreType.DMA((2,))],
         compiler_params=pltpu.CompilerParams(vmem_limit_bytes=12 << 20),
         cost_estimate=cost(2),
-    )(total, held_left, held_high, held_low, al_pp, al_mm, *last_s, *far_b)
+    )(total, held_left, held_high, held_low, last_a, last_s, *far_b)
 
 
 def solution(mesh):

time: 97.6 us -> 93.8 us (0.961)
  starting transfers between devices: 41.1 us -> 37.5 us
    ppermute x31 -> x26, starting transfers between devices: 41.1 us -> 37.5 us  [send(): return lax.ppermute(array, BOTH, MOVES[move])]
    ppermute x31 -> x26, waiting for transfers between devices: 47.9 us -> 48.2 us  [send(): return lax.ppermute(array, BOTH, MOVES[move])]
  transfers between devices with their start and end apart: 31 -> 26, of which waited for: 10 -> 14; matrix products, arithmetic and copies ran while one was open for 1% -> 2% of each run, Pallas kernels for 5% -> 5%
where the time goes in v4:
time: 93.8 us; the launch traced here: 93.6 us
  waiting for transfers between devices  48.2 us (51%)
  starting transfers between devices  37.5 us (40%)
  Pallas kernels  6.23 us (7%)
  local copies, waits for them, and re-layouts  1.26 us (1%)
    ppermute x26, waiting for transfers between devices, send(): return lax.ppermute(array, BOTH, MOVES[move])  48.2 us
    ppermute x26, starting transfers between devices, send(): return lax.ppermute(array, BOTH, MOVES[move])  37.5 us
    pallas_call x1, Pallas kernels, product(): pl.pallas_call(main_kernel, out_shape=(whole, panel, panel, shape((2, tal...  2.25 us
    pallas_call x1, Pallas kernels, product(): pl.pallas_call(soon_kernel, out_shape=(whole, panel, panel), in_specs=[in...  2.09 us
    pallas_call x1, Pallas kernels, product(): pl.pallas_call(last_kernel, out_shape=jax.ShapeDtypeStruct((tall, broad),...  1.88 us
  transfers between devices with their start and end apart: 26, of which 14 were waited for; matrix products, arithmetic and copies ran while one was open for 2% of the time, Pallas kernels for 5%

profile of v4, /device:TPU:0, one launch (start us, length us, event | category | flops | bytes accessed | tf_op | source)
XLA Modules:
  0.0 93.6 jit_solution(14449698142686665842)
XLA Ops:
  1.0 2.2 %collective-permute-start.1 = (f32[512,256]{1,0:T(8,128)}, f32[512,256]{1,0:T(8,128)S(1)}, u32[]{:S(2)}, u32[]{:S(2)}) collective-permute-start(f32[512,256]{1,0:T(8,128)} %refs_0_.3), channel_id=1, source_target_pairs={{0,3},{1,2},{2,5},{3,4},{4,7},{5,6},{6,1},{7,0},{8,11},{9,10},{10,... | collective-permute-start | bytes 1572872 | tf_op jit(solution)/shard_map/ppermute | solution.py:40
  3.2 2.1 %collective-permute-start.2 = (f32[512,256]{1,0:T(8,128)}, f32[512,256]{1,0:T(8,128)S(1)}, u32[]{:S(2)}, u32[]{:S(2)}) collective-permute-start(f32[512,256]{1,0:T(8,128)} %refs_0_.3), channel_id=1, source_target_pairs={{0,7},{1,6},{2,1},{3,0},{4,3},{5,2},{6,5},{7,4},{8,15},{9,14},{10,... | collective-permute-start | bytes 1572872 | tf_op jit(solution)/shard_map/ppermute | solution.py:40
  5.4 1.1 %fusion = (f32[256,256]{1,0:T(8,128)S(1)}, f32[256,256]{1,0:T(8,128)S(1)}) fusion(f32[512,256]{1,0:T(8,128)} %refs_6_.1), kind=kLoop, calls=%fused_computation.6 | loop fusion | bytes 1048576 | tf_op jit(solution)/shard_map/slice | solution.py:44
  6.4 2.8 %collective-permute-start.11 = (f32[256,256]{1,0:T(8,128)S(1)}, f32[256,256]{1,0:T(8,128)S(1)}, u32[]{:S(2)}, u32[]{:S(2)}) collective-permute-start(f32[256,256]{1,0:T(8,128)S(1)} %get-tuple-element.20), channel_id=1, source_target_pairs={{0,16},{1,17},{2,18},{3,19},{4,20},{5,21},{6,22},{7,23},{8,24},{9,... | collective-permute-start | bytes 786440 | tf_op jit(solution)/shard_map/ppermute | solution.py:40
  10.0 12.3 %collective-permute-done.11.refs_11_ = f32[256,256]{1,0:T(8,128)S(1)} collective-permute-done((f32[256,256]{1,0:T(8,128)S(1)}, f32[256,256]{1,0:T(8,128)S(1)}, u32[]{:S(2)}, u32[]{:S(2)}) %collective-permute-start.11) | collective-permute-done | bytes 262176 | tf_op jit(solution)/shard_map/ppermute | solution.py:40
  22.4 1.6 %collective-permute-start.17 = (f32[512,256]{1,0:T(8,128)}, f32[512,256]{1,0:T(8,128)S(1)}, u32[]{:S(2)}, u32[]{:S(2)}) collective-permute-start(f32[512,256]{1,0:T(8,128)} %refs_6_.1), channel_id=1, source_target_pairs={{0,32},{1,33},{2,34},{3,35},{4,36},{5,37},{6,38},{7,39},{8,40},{9,... | collective-permute-start | bytes 1572872 | tf_op jit(solution)/shard_map/ppermute | solution.py:40
  23.9 4.0 %collective-permute-done.14.refs_12_ = f32[256,256]{1,0:T(8,128)S(1)} collective-permute-done((f32[256,256]{1,0:T(8,128)S(1)}, f32[256,256]{1,0:T(8,128)S(1)}, u32[]{:S(2)}, u32[]{:S(2)}) %collective-permute-start.14) | collective-permute-done | bytes 262176 | tf_op jit(solution)/shard_map/ppermute | solution.py:40
  28.0 3.0 %collective-permute-start.18 = (f32[512,256]{1,0:T(8,128)}, f32[512,256]{1,0:T(8,128)S(1)}, u32[]{:S(2)}, u32[]{:S(2)}) collective-permute-start(f32[512,256]{1,0:T(8,128)} %refs_6_.1), channel_id=1, source_target_pairs={{0,96},{1,97},{2,98},{3,99},{4,100},{5,101},{6,102},{7,103},{8,104... | collective-permute-start | bytes 1572872 | tf_op jit(solution)/shard_map/ppermute | solution.py:40
  31.0 2.0 %collective-permute-start.5 = (f32[512,256]{1,0:T(8,128)S(1)}, f32[512,256]{1,0:T(8,128)S(1)}, u32[]{:S(2)}, u32[]{:S(2)}) collective-permute-start(f32[512,256]{1,0:T(8,128)S(1)} %collective-permute-done.refs_1_), channel_id=1, source_target_pairs={{0,3},{1,2},{2,5},{3,4},{4,7},{5,6},{6,1},{7,0},{8,11},{9,10},{10,... | collective-permute-start | bytes 1572872 | tf_op jit(solution)/shard_map/ppermute | solution.py:40
  33.0 2.2 %collective-permute-start.6 = (f32[512,256]{1,0:T(8,128)S(1)}, f32[512,256]{1,0:T(8,128)S(1)}, u32[]{:S(2)}, u32[]{:S(2)}) collective-permute-start(f32[512,256]{1,0:T(8,128)S(1)} %collective-permute-done.refs_1_), channel_id=1, source_target_pairs={{0,7},{1,6},{2,1},{3,0},{4,3},{5,2},{6,5},{7,4},{8,15},{9,14},{10,... | collective-permute-start | bytes 1572872 | tf_op jit(solution)/shard_map/ppermute | solution.py:40
  35.3 2.4 %collective-permute-done.17.refs_7_ = f32[512,256]{1,0:T(8,128)S(1)} collective-permute-done((f32[512,256]{1,0:T(8,128)}, f32[512,256]{1,0:T(8,128)S(1)}, u32[]{:S(2)}, u32[]{:S(2)}) %collective-permute-start.17) | collective-permute-done | bytes 524320 | tf_op jit(solution)/shard_map/ppermute | solution.py:40
  37.8 5.0 %collective-permute-done.18.refs_8_ = f32[512,256]{1,0:T(8,128)S(1)} collective-permute-done((f32[512,256]{1,0:T(8,128)}, f32[512,256]{1,0:T(8,128)S(1)}, u32[]{:S(2)}, u32[]{:S(2)}) %collective-permute-start.18) | collective-permute-done | bytes 524320 | tf_op jit(solution)/shard_map/ppermute | solution.py:40
  43.7 2.7 %collective-permute-start.16 = (f32[256,256]{1,0:T(8,128)S(1)}, f32[256,256]{1,0:T(8,128)S(1)}, u32[]{:S(2)}, u32[]{:S(2)}) collective-permute-start(f32[256,256]{1,0:T(8,128)S(1)} %collective-permute-done.14.refs_12_), channel_id=1, source_target_pairs={{0,96},{1,97},{2,98},{3,99},{4,100},{5,101},{6,102},{7,103},{8,104... | collective-permute-start | bytes 786440 | tf_op jit(solution)/shard_map/ppermute | solution.py:40
  46.4 5.7 %collective-permute-done.12.refs_11_ = f32[256,256]{1,0:T(8,128)S(1)} collective-permute-done((f32[256,256]{1,0:T(8,128)S(1)}, f32[256,256]{1,0:T(8,128)S(1)}, u32[]{:S(2)}, u32[]{:S(2)}) %collective-permute-start.12) | collective-permute-done | bytes 262176 | tf_op jit(solution)/shard_map/ppermute | solution.py:40
  52.1 1.7 %collective-permute-start.13 = (f32[256,256]{1,0:T(8,128)S(1)}, f32[256,256]{1,0:T(8,128)S(1)}, u32[]{:S(2)}, u32[]{:S(2)}) collective-permute-start(f32[256,256]{1,0:T(8,128)S(1)} %collective-permute-done.11.refs_11_), channel_id=1, source_target_pairs={{0,96},{1,97},{2,98},{3,99},{4,100},{5,101},{6,102},{7,103},{8,104... | collective-permute-start | bytes 786440 | tf_op jit(solution)/shard_map/ppermute | solution.py:40
  54.3 2.1 %collective-permute-start.10 = (f32[1024,256]{1,0:T(8,128)S(1)}, f32[1024,256]{1,0:T(8,128)S(1)}, u32[]{:S(2)}, u32[]{:S(2)}) collective-permute-start(f32[1024,256]{1,0:T(8,128)S(1)} %pad_maximum_fusion.1), channel_id=1, source_target_pairs={{0,1},{1,0},{2,3},{3,2},{4,5},{5,4},{6,7},{7,6},{8,9},{9,8},{10,11... | collective-permute-start | bytes 3145736 | tf_op jit(solution)/shard_map/ppermute | solution.py:40
  56.4 2.5 %collective-permute-done.13.refs_12_ = f32[256,256]{1,0:T(8,128)S(1)} collective-permute-done((f32[256,256]{1,0:T(8,128)S(1)}, f32[256,256]{1,0:T(8,128)S(1)}, u32[]{:S(2)}, u32[]{:S(2)}) %collective-permute-start.13) | collective-permute-done | bytes 262176 | tf_op jit(solution)/shard_map/ppermute | solution.py:40
  58.9 1.5 %collective-permute-start.4 = (f32[256,256]{1,0:T(8,128)S(1)}, f32[256,256]{1,0:T(8,128)S(1)}, u32[]{:S(2)}, u32[]{:S(2)}) collective-permute-start(f32[256,256]{1,0:T(8,128)S(1)} %slice.33), channel_id=1, source_target_pairs={{0,7},{1,6},{2,1},{3,0},{4,3},{5,2},{6,5},{7,4},{8,15},{9,14},{10,... | collective-permute-start | bytes 786440 | tf_op jit(solution)/shard_map/ppermute | solution.py:40
  60.4 1.1 %collective-permute-done.15.refs_13_ = f32[256,256]{1,0:T(8,128)S(1)} collective-permute-done((f32[256,256]{1,0:T(8,128)S(1)}, f32[256,256]{1,0:T(8,128)S(1)}, u32[]{:S(2)}, u32[]{:S(2)}) %collective-permute-start.15) | collective-permute-done | bytes 262176 | tf_op jit(solution)/shard_map/ppermute | solution.py:40
  62.6 2.0 %collective-permute-start.22 = (f32[256,256]{1,0:T(8,128)S(1)}, f32[256,256]{1,0:T(8,128)S(1)}, u32[]{:S(2)}, u32[]{:S(2)}) collective-permute-start(f32[256,256]{1,0:T(8,128)S(1)} %slice.37), channel_id=1, source_target_pairs={{0,7},{1,6},{2,1},{3,0},{4,3},{5,2},{6,5},{7,4},{8,15},{9,14},{10,... | collective-permute-start | bytes 786440 | tf_op jit(solution)/shard_map/ppermute | solution.py:40
  64.6 2.4 %collective-permute-done.4 = f32[256,256]{1,0:T(8,128)S(1)} collective-permute-done((f32[256,256]{1,0:T(8,128)S(1)}, f32[256,256]{1,0:T(8,128)S(1)}, u32[]{:S(2)}, u32[]{:S(2)}) %collective-permute-start.4) | collective-permute-done | bytes 262176 | tf_op jit(solution)/shard_map/ppermute | solution.py:40
  67.1 2.3 %collective-permute-done.21 = f32[256,256]{1,0:T(8,128)S(1)} collective-permute-done((f32[256,256]{1,0:T(8,128)S(1)}, f32[256,256]{1,0:T(8,128)S(1)}, u32[]{:S(2)}, u32[]{:S(2)}) %collective-permute-start.21) | collective-permute-done | bytes 262176 | tf_op jit(solution)/shard_map/ppermute | solution.py:40
  69.4 1.7 %collective-permute-start.9 = (f32[512,256]{1,0:T(8,128)S(1)}, f32[512,256]{1,0:T(8,128)S(1)}, u32[]{:S(2)}, u32[]{:S(2)}) collective-permute-start(f32[512,256]{1,0:T(8,128)S(1)} %constant_dynamic-update-slice_fusion.refs_4_), channel_id=1, source_target_pairs={{0,1},{1,0},{2,3},{3,2},{4,5},{5,4},{6,7},{7,6},{8,9},{9,8},{10,11... | collective-permute-start | bytes 1572872 | tf_op jit(solution)/shard_map/ppermute | solution.py:40
  71.1 1.5 %collective-permute-done.22 = f32[256,256]{1,0:T(8,128)S(1)} collective-permute-done((f32[256,256]{1,0:T(8,128)S(1)}, f32[256,256]{1,0:T(8,128)S(1)}, u32[]{:S(2)}, u32[]{:S(2)}) %collective-permute-start.22) | collective-permute-done | bytes 262176 | tf_op jit(solution)/shard_map/ppermute | solution.py:40
  72.7 2.7 %collective-permute-start.20 = (f32[256,256]{1,0:T(8,128)S(1)}, f32[256,256]{1,0:T(8,128)S(1)}, u32[]{:S(2)}, u32[]{:S(2)}) collective-permute-start(f32[256,256]{1,0:T(8,128)S(1)} %slice.35), channel_id=1, source_target_pairs={{0,96},{1,97},{2,98},{3,99},{4,100},{5,101},{6,102},{7,103},{8,104... | collective-permute-start | bytes 786440 | tf_op jit(solution)/shard_map/ppermute | solution.py:40
  75.4 1.5 %collective-permute-done.19.refs_9_ = f32[256,256]{1,0:T(8,128)S(1)} collective-permute-done((f32[256,256]{1,0:T(8,128)S(1)}, f32[256,256]{1,0:T(8,128)S(1)}, u32[]{:S(2)}, u32[]{:S(2)}) %collective-permute-start.19) | collective-permute-done | bytes 262176 | tf_op jit(solution)/shard_map/ppermute | solution.py:40
  77.3 4.4 %collective-permute-done.20.refs_10_ = f32[256,256]{1,0:T(8,128)S(1)} collective-permute-done((f32[256,256]{1,0:T(8,128)S(1)}, f32[256,256]{1,0:T(8,128)S(1)}, u32[]{:S(2)}, u32[]{:S(2)}) %collective-permute-start.20) | collective-permute-done | bytes 262176 | tf_op jit(solution)/shard_map/ppermute | solution.py:40
  81.7 3.7 %collective-permute-start.25 = (f32[256,256]{1,0:T(8,128)S(1)}, f32[256,256]{1,0:T(8,128)S(1)}, u32[]{:S(2)}, u32[]{:S(2)}) collective-permute-start(f32[256,256]{1,0:T(8,128)S(1)} %collective-permute-done.16.refs_14_), channel_id=1, source_target_pairs={{0,96},{1,97},{2,98},{3,99},{4,100},{5,101},{6,102},{7,103},{8,104... | collective-permute-start | bytes 786440 | tf_op jit(solution)/shard_map/ppermute | solution.py:40
  85.4 2.1 %shard_map.28 = (f32[512,256]{1,0:T(8,128)S(1)}, bf16[16,256,256]{2,1,0:T(8,128)(2,1)S(1)}, bf16[16,256,256]{2,1,0:T(8,128)(2,1)S(1)}) custom-call(f32[512,256]{1,0:T(8,128)S(1)} %copy-done, f32[512,256]{1,0:T(8,128)S(1)} %collective-permute-done.refs_1_, f32[512,256]{1,0:T(8,128)S(1)} %collective-permute-done.1.refs_2_, ...), custom_call_target="tpu_custom_call" | custom-call | flops 805306368 | bytes 2097152 | tf_op jit(solution)/shard_map/pallas_call | solution.py:232
  87.5 2.2 %shard_map.29 = (f32[512,256]{1,0:T(8,128)S(1)}, bf16[16,256,256]{2,1,0:T(8,128)(2,1)S(1)}, bf16[16,256,256]{2,1,0:T(8,128)(2,1)S(1)}, f32[2,512,256]{2,1,0:T(8,...) custom-call(f32[512,256]{1,0:T(8,128)S(1)} %copy-done, ...), custom_call_target="tpu_custom_call", output_to_operand_aliasing={{0}: (15, {}), {1}: (16, {}), {2}: (17, {})} | custom-call | flops 2013265920 | bytes 5242880 | tf_op jit(solution)/shard_map/pallas_call | solution.py:241
  89.8 1.8 %collective-permute-done.24.b0 = f32[256,256]{1,0:T(8,128)S(1)} collective-permute-done((f32[256,256]{1,0:T(8,128)S(1)}, f32[256,256]{1,0:T(8,128)S(1)}, u32[]{:S(2)}, u32[]{:S(2)}) %collective-permute-start.24) | collective-permute-done | bytes 262176 | tf_op jit(solution)/shard_map/ppermute | solution.py:40
  91.6 1.9 %shard_map.30 = f32[512,256]{1,0:T(8,128)} custom-call(f32[512,256]{1,0:T(8,128)S(1)} %get-tuple-element.15.total, f32[2,512,256]{2,1,0:T(8,128)S(1)} %get-tuple-element.16.held_left, bf16[2,256,256]{2,1,0:T(8,128)(2,1)S(1)} %get-tuple-element.17.held_high, bf16[2,256,256]{2,1,0:T(8,128)(2,1)S(1)} %get-tuple-element.18.held_low, ...), custom_call_target="tpu_custom_call" | custom-call | flops 805306368 | bytes 2097152 | tf_op jit(solution)/shard_map/pallas_call | solution.py:258
  (40 shorter events, 5.0 us)
Async XLA Ops:
  0.0 31.0 %collective-permute-start = (f32[512,256]{1,0:T(8,128)}, f32[512,256]{1,0:T(8,128)S(1)}, u32[]{:S(2)}, u32[]{:S(2)}) collective-permute-start(f32[512,256]{1,0:T(8,128)} %refs_0_.3), channel_id=1, source_target_pairs={{0,9},{1,8},{2,11},{3,10},{4,13},{5,12},{6,15},{7,14},{8,1},{9,0},... | collective-permute-start | bytes 1572872 | tf_op jit(solution)/shard_map/ppermute | solution.py:40
  1.0 30.0 %collective-permute-start.1 = (f32[512,256]{1,0:T(8,128)}, f32[512,256]{1,0:T(8,128)S(1)}, u32[]{:S(2)}, u32[]{:S(2)}) collective-permute-start(f32[512,256]{1,0:T(8,128)} %refs_0_.3), channel_id=1, source_target_pairs={{0,3},{1,2},{2,5},{3,4},{4,7},{5,6},{6,1},{7,0},{8,11},{9,10},{10,... | collective-permute-start | bytes 1572872 | tf_op jit(solution)/shard_map/ppermute | solution.py:40
  3.2 29.8 %collective-permute-start.2 = (f32[512,256]{1,0:T(8,128)}, f32[512,256]{1,0:T(8,128)S(1)}, u32[]{:S(2)}, u32[]{:S(2)}) collective-permute-start(f32[512,256]{1,0:T(8,128)} %refs_0_.3), channel_id=1, source_target_pairs={{0,7},{1,6},{2,1},{3,0},{4,3},{5,2},{6,5},{7,4},{8,15},{9,14},{10,... | collective-permute-start | bytes 1572872 | tf_op jit(solution)/shard_map/ppermute | solution.py:40
  6.4 15.9 %collective-permute-start.11 = (f32[256,256]{1,0:T(8,128)S(1)}, f32[256,256]{1,0:T(8,128)S(1)}, u32[]{:S(2)}, u32[]{:S(2)}) collective-permute-start(f32[256,256]{1,0:T(8,128)S(1)} %get-tuple-element.20), channel_id=1, source_target_pairs={{0,16},{1,17},{2,18},{3,19},{4,20},{5,21},{6,22},{7,23},{8,24},{9,... | collective-permute-start | bytes 786440 | tf_op jit(solution)/shard_map/ppermute | solution.py:40
  9.2 18.7 %collective-permute-start.14 = (f32[256,256]{1,0:T(8,128)S(1)}, f32[256,256]{1,0:T(8,128)S(1)}, u32[]{:S(2)}, u32[]{:S(2)}) collective-permute-start(f32[256,256]{1,0:T(8,128)S(1)} %get-tuple-element.19), channel_id=1, source_target_pairs={{0,16},{1,17},{2,18},{3,19},{4,20},{5,21},{6,22},{7,23},{8,24},{9,... | collective-permute-start | bytes 786440 | tf_op jit(solution)/shard_map/ppermute | solution.py:40
  22.4 15.4 %collective-permute-start.17 = (f32[512,256]{1,0:T(8,128)}, f32[512,256]{1,0:T(8,128)S(1)}, u32[]{:S(2)}, u32[]{:S(2)}) collective-permute-start(f32[512,256]{1,0:T(8,128)} %refs_6_.1), channel_id=1, source_target_pairs={{0,32},{1,33},{2,34},{3,35},{4,36},{5,37},{6,38},{7,39},{8,40},{9,... | collective-permute-start | bytes 1572872 | tf_op jit(solution)/shard_map/ppermute | solution.py:40
  28.0 14.8 %collective-permute-start.18 = (f32[512,256]{1,0:T(8,128)}, f32[512,256]{1,0:T(8,128)S(1)}, u32[]{:S(2)}, u32[]{:S(2)}) collective-permute-start(f32[512,256]{1,0:T(8,128)} %refs_6_.1), channel_id=1, source_target_pairs={{0,96},{1,97},{2,98},{3,99},{4,100},{5,101},{6,102},{7,103},{8,104... | collective-permute-start | bytes 1572872 | tf_op jit(solution)/shard_map/ppermute | solution.py:40
  31.0 12.7 %collective-permute-start.7 = (f32[512,256]{1,0:T(8,128)}, f32[512,256]{1,0:T(8,128)S(1)}, u32[]{:S(2)}, u32[]{:S(2)}) collective-permute-start(f32[512,256]{1,0:T(8,128)} %refs_0_.3), channel_id=1, source_target_pairs={{0,1},{1,0},{2,3},{3,2},{4,5},{5,4},{6,7},{7,6},{8,9},{9,8},{10,11... | collective-permute-start | bytes 1572872 | tf_op jit(solution)/shard_map/ppermute | solution.py:40
  31.0 22.8 %collective-permute-start.5 = (f32[512,256]{1,0:T(8,128)S(1)}, f32[512,256]{1,0:T(8,128)S(1)}, u32[]{:S(2)}, u32[]{:S(2)}) collective-permute-start(f32[512,256]{1,0:T(8,128)S(1)} %collective-permute-done.refs_1_), channel_id=1, source_target_pairs={{0,3},{1,2},{2,5},{3,4},{4,7},{5,6},{6,1},{7,0},{8,11},{9,10},{10,... | collective-permute-start | bytes 1572872 | tf_op jit(solution)/shard_map/ppermute | solution.py:40
  33.0 21.1 %collective-permute-start.6 = (f32[512,256]{1,0:T(8,128)S(1)}, f32[512,256]{1,0:T(8,128)S(1)}, u32[]{:S(2)}, u32[]{:S(2)}) collective-permute-start(f32[512,256]{1,0:T(8,128)S(1)} %collective-permute-done.refs_1_), channel_id=1, source_target_pairs={{0,7},{1,6},{2,1},{3,0},{4,3},{5,2},{6,5},{7,4},{8,15},{9,14},{10,... | collective-permute-start | bytes 1572872 | tf_op jit(solution)/shard_map/ppermute | solution.py:40
  37.8 43.9 %collective-permute-start.8 = (f32[1536,256]{1,0:T(8,128)S(1)}, f32[1536,256]{1,0:T(8,128)S(1)}, u32[]{:S(2)}, u32[]{:S(2)}) collective-permute-start(f32[1536,256]{1,0:T(8,128)S(1)} %pad_maximum_fusion), channel_id=1, source_target_pairs={{0,1},{1,0},{2,3},{3,2},{4,5},{5,4},{6,7},{7,6},{8,9},{9,8},{10,11... | collective-permute-start | bytes 4718600 | tf_op jit(solution)/shard_map/ppermute | solution.py:40
  42.8 9.3 %collective-permute-start.12 = (f32[256,256]{1,0:T(8,128)S(1)}, f32[256,256]{1,0:T(8,128)S(1)}, u32[]{:S(2)}, u32[]{:S(2)}) collective-permute-start(f32[256,256]{1,0:T(8,128)S(1)} %collective-permute-done.11.refs_11_), channel_id=1, source_target_pairs={{0,32},{1,33},{2,34},{3,35},{4,36},{5,37},{6,38},{7,39},{8,40},{9,... | collective-permute-start | bytes 786440 | tf_op jit(solution)/shard_map/ppermute | solution.py:40
  43.7 10.6 %collective-permute-start.16 = (f32[256,256]{1,0:T(8,128)S(1)}, f32[256,256]{1,0:T(8,128)S(1)}, u32[]{:S(2)}, u32[]{:S(2)}) collective-permute-start(f32[256,256]{1,0:T(8,128)S(1)} %collective-permute-done.14.refs_12_), channel_id=1, source_target_pairs={{0,96},{1,97},{2,98},{3,99},{4,100},{5,101},{6,102},{7,103},{8,104... | collective-permute-start | bytes 786440 | tf_op jit(solution)/shard_map/ppermute | solution.py:40
  52.1 6.9 %collective-permute-start.13 = (f32[256,256]{1,0:T(8,128)S(1)}, f32[256,256]{1,0:T(8,128)S(1)}, u32[]{:S(2)}, u32[]{:S(2)}) collective-permute-start(f32[256,256]{1,0:T(8,128)S(1)} %collective-permute-done.11.refs_11_), channel_id=1, source_target_pairs={{0,96},{1,97},{2,98},{3,99},{4,100},{5,101},{6,102},{7,103},{8,104... | collective-permute-start | bytes 786440 | tf_op jit(solution)/shard_map/ppermute | solution.py:40
  53.8 7.7 %collective-permute-start.15 = (f32[256,256]{1,0:T(8,128)S(1)}, f32[256,256]{1,0:T(8,128)S(1)}, u32[]{:S(2)}, u32[]{:S(2)}) collective-permute-start(f32[256,256]{1,0:T(8,128)S(1)} %collective-permute-done.14.refs_12_), channel_id=1, source_target_pairs={{0,32},{1,33},{2,34},{3,35},{4,36},{5,37},{6,38},{7,39},{8,40},{9,... | collective-permute-start | bytes 786440 | tf_op jit(solution)/shard_map/ppermute | solution.py:40
  54.2 8.4 %collective-permute-start.3 = (f32[256,256]{1,0:T(8,128)S(1)}, f32[256,256]{1,0:T(8,128)S(1)}, u32[]{:S(2)}, u32[]{:S(2)}) collective-permute-start(f32[256,256]{1,0:T(8,128)S(1)} %slice.32), channel_id=1, source_target_pairs={{0,3},{1,2},{2,5},{3,4},{4,7},{5,6},{6,1},{7,0},{8,11},{9,10},{10,... | collective-permute-start | bytes 786440 | tf_op jit(solution)/shard_map/ppermute | solution.py:40
  54.3 33.2 %collective-permute-start.10 = (f32[1024,256]{1,0:T(8,128)S(1)}, f32[1024,256]{1,0:T(8,128)S(1)}, u32[]{:S(2)}, u32[]{:S(2)}) collective-permute-start(f32[1024,256]{1,0:T(8,128)S(1)} %pad_maximum_fusion.1), channel_id=1, source_target_pairs={{0,1},{1,0},{2,3},{3,2},{4,5},{5,4},{6,7},{7,6},{8,9},{9,8},{10,11... | collective-permute-start | bytes 3145736 | tf_op jit(solution)/shard_map/ppermute | solution.py:40
  58.9 8.1 %collective-permute-start.4 = (f32[256,256]{1,0:T(8,128)S(1)}, f32[256,256]{1,0:T(8,128)S(1)}, u32[]{:S(2)}, u32[]{:S(2)}) collective-permute-start(f32[256,256]{1,0:T(8,128)S(1)} %slice.33), channel_id=1, source_target_pairs={{0,7},{1,6},{2,1},{3,0},{4,3},{5,2},{6,5},{7,4},{8,15},{9,14},{10,... | collective-permute-start | bytes 786440 | tf_op jit(solution)/shard_map/ppermute | solution.py:40
  61.5 7.9 %collective-permute-start.21 = (f32[256,256]{1,0:T(8,128)S(1)}, f32[256,256]{1,0:T(8,128)S(1)}, u32[]{:S(2)}, u32[]{:S(2)}) collective-permute-start(f32[256,256]{1,0:T(8,128)S(1)} %slice.36), channel_id=1, source_target_pairs={{0,3},{1,2},{2,5},{3,4},{4,7},{5,6},{6,1},{7,0},{8,11},{9,10},{10,... | collective-permute-start | bytes 786440 | tf_op jit(solution)/shard_map/ppermute | solution.py:40
  61.5 23.9 %copy-start = (f32[512,256]{1,0:T(8,128)S(1)}, f32[512,256]{1,0:T(8,128)}, u32[]{:S(2)}) copy-start(f32[512,256]{1,0:T(8,128)} %refs_0_.3) | copy-start | bytes 1572868
  61.5 23.9 %copy-start.1 = (f32[512,256]{1,0:T(8,128)S(1)}, f32[512,256]{1,0:T(8,128)}, u32[]{:S(2)}) copy-start(f32[512,256]{1,0:T(8,128)} %refs_6_.1) | copy-start | bytes 1572868
  62.6 10.1 %collective-permute-start.22 = (f32[256,256]{1,0:T(8,128)S(1)}, f32[256,256]{1,0:T(8,128)S(1)}, u32[]{:S(2)}, u32[]{:S(2)}) collective-permute-start(f32[256,256]{1,0:T(8,128)S(1)} %slice.37), channel_id=1, source_target_pairs={{0,7},{1,6},{2,1},{3,0},{4,3},{5,2},{6,5},{7,4},{8,15},{9,14},{10,... | collective-permute-start | bytes 786440 | tf_op jit(solution)/shard_map/ppermute | solution.py:40
  67.1 9.8 %collective-permute-start.19 = (f32[256,256]{1,0:T(8,128)S(1)}, f32[256,256]{1,0:T(8,128)S(1)}, u32[]{:S(2)}, u32[]{:S(2)}) collective-permute-start(f32[256,256]{1,0:T(8,128)S(1)} %slice.34), channel_id=1, source_target_pairs={{0,32},{1,33},{2,34},{3,35},{4,36},{5,37},{6,38},{7,39},{8,40},{9,... | collective-permute-start | bytes 786440 | tf_op jit(solution)/shard_map/ppermute | solution.py:40
  69.4 18.1 %collective-permute-start.9 = (f32[512,256]{1,0:T(8,128)S(1)}, f32[512,256]{1,0:T(8,128)S(1)}, u32[]{:S(2)}, u32[]{:S(2)}) collective-permute-start(f32[512,256]{1,0:T(8,128)S(1)} %constant_dynamic-update-slice_fusion.refs_4_), channel_id=1, source_target_pairs={{0,1},{1,0},{2,3},{3,2},{4,5},{5,4},{6,7},{7,6},{8,9},{9,8},{10,11... | collective-permute-start | bytes 1572872 | tf_op jit(solution)/shard_map/ppermute | solution.py:40
  72.7 9.0 %collective-permute-start.20 = (f32[256,256]{1,0:T(8,128)S(1)}, f32[256,256]{1,0:T(8,128)S(1)}, u32[]{:S(2)}, u32[]{:S(2)}) collective-permute-start(f32[256,256]{1,0:T(8,128)S(1)} %slice.35), channel_id=1, source_target_pairs={{0,96},{1,97},{2,98},{3,99},{4,100},{5,101},{6,102},{7,103},{8,104... | collective-permute-start | bytes 786440 | tf_op jit(solution)/shard_map/ppermute | solution.py:40
  76.9 14.7 %collective-permute-start.23 = (f32[512,256]{1,0:T(8,128)S(1)}, f32[512,256]{1,0:T(8,128)S(1)}, u32[]{:S(2)}, u32[]{:S(2)}) collective-permute-start(f32[512,256]{1,0:T(8,128)S(1)} %constant_dynamic-update-slice_fusion.2.mine), channel_id=1, source_target_pairs={{0,1},{1,0},{2,3},{3,2},{4,5},{5,4},{6,7},{7,6},{8,9},{9,8},{10,11... | collective-permute-start | bytes 1572872 | tf_op jit(solution)/shard_map/ppermute | solution.py:40
  81.7 9.9 %collective-permute-start.24 = (f32[256,256]{1,0:T(8,128)S(1)}, f32[256,256]{1,0:T(8,128)S(1)}, u32[]{:S(2)}, u32[]{:S(2)}) collective-permute-start(f32[256,256]{1,0:T(8,128)S(1)} %collective-permute-done.12.refs_11_), channel_id=1, source_target_pairs={{0,32},{1,33},{2,34},{3,35},{4,36},{5,37},{6,38},{7,39},{8,40},{9,... | collective-permute-start | bytes 786440 | tf_op jit(solution)/shard_map/ppermute | solution.py:40
  81.7 9.9 %collective-permute-start.25 = (f32[256,256]{1,0:T(8,128)S(1)}, f32[256,256]{1,0:T(8,128)S(1)}, u32[]{:S(2)}, u32[]{:S(2)}) collective-permute-start(f32[256,256]{1,0:T(8,128)S(1)} %collective-permute-done.16.refs_14_), channel_id=1, source_target_pairs={{0,96},{1,97},{2,98},{3,99},{4,100},{5,101},{6,102},{7,103},{8,104... | collective-permute-start | bytes 786440 | tf_op jit(solution)/shard_map/ppermute | solution.py:40

commit v5 on v4

--- a/solution.py
+++ b/solution.py
@@ -72,10 +72,10 @@
 
 
 LEFTS = ((0, 0), (1, 0), (0, 3), (0, 1), (0, 2), (1, 3), (1, 1))
-ROWS, FAR = 64, 256
+ROWS, FAR, UPPER = 64, 256, 320
 RIGHTS = (
-    (0, 0, 0), (0, 3, 0), (0, 1, 0), (0, 2, 0), (0, 2, FAR), (1, 0, 0), (1, 0, 256),
-    (1, 3, 0), (1, 1, 0), (1, 3, 256), (1, 1, 256),
+    (0, 0, 0), (0, 3, 0), (0, 1, 0), (0, 2, 0), (0, 2, FAR), (1, 0, 0), (1, 0, UPPER),
+    (1, 3, 0), (1, 1, 0), (1, 3, UPPER), (1, 1, UPPER),
 )
 SOON, HELD = 4, 7
 
@@ -168,8 +168,10 @@
     last = right_of(1, 2)
     spare = left_of(1, 2)
     step = high.shape[1]
-    for index, ref in enumerate((b0, b1)):
-        high[index], low[index] = split(ref[...])
+    for ref, top in ((b0, 0), (b1, UPPER)):
+        for part in range(0, ref.shape[0], ROWS):
+            at, rows = (top + part) // step, pl.ds((top + part) % step, ROWS)
+            high[at, rows], low[at, rows] = split(ref[part : part + ROWS])
 
     @pl.when(last == spare)
     def _():
@@ -201,7 +203,7 @@
     a_lo = send(a, "lo")
     a_p, a_m = send(a, "z+"), send(a, "z-")
     b_p, b_m = send(b, "y+"), send(b, "y-")
-    b_hi = [send(cut(b, 0, half), "hi"), send(cut(b, half, half), "hi")]
+    b_hi = [send(cut(b, 0, UPPER), "hi"), send(cut(b, UPPER, deep - UPPER), "hi")]
     al_p, al_m = send(a_lo, "z+"), send(a_lo, "z-")
     a_pp = send(cut(a_p, 0, hill), "z+")
     a_mm = send(cut(a_m, hill, hill), "z-")

time: 93.8 us -> 98.1 us (1.046)
  waiting for transfers between devices: 48.2 us -> 53.8 us
  starting transfers between devices: 37.5 us -> 35.3 us
    ppermute x26, waiting for transfers between devices: 48.2 us -> 53.8 us  [send(): return lax.ppermute(array, BOTH, MOVES[move])]
    ppermute x26, starting transfers between devices: 37.5 us -> 35.3 us  [send(): return lax.ppermute(array, BOTH, MOVES[move])]
    slice x7 -> x8, local copies, waits for them, and re-layouts: 1.17 us -> 2.04 us  [cut(): return array[top:top + rows]]
  transfers between devices with their start and end apart: 26 -> 26, of which waited for: 14 -> 12; matrix products, arithmetic and copies ran while one was open for 2% -> 2% of each run, Pallas kernels for 5% -> 4%
where the time goes in v5:
time: 98.1 us; the launch traced here: 97.9 us
  waiting for transfers between devices  53.8 us (55%)
  starting transfers between devices  35.3 us (36%)
  Pallas kernels  6.2 us (6%)
  local copies, waits for them, and re-layouts  2.13 us (2%)
    ppermute x26, waiting for transfers between devices, send(): return lax.ppermute(array, BOTH, MOVES[move])  53.8 us
    ppermute x26, starting transfers between devices, send(): return lax.ppermute(array, BOTH, MOVES[move])  35.3 us
    pallas_call x1, Pallas kernels, product(): pl.pallas_call(main_kernel, out_shape=(whole, panel, panel, shape((2, tal...  2.25 us
    pallas_call x1, Pallas kernels, product(): pl.pallas_call(soon_kernel, out_shape=(whole, panel, panel), in_specs=[in...  2.09 us
    slice x8, local copies, waits for them, and re-layouts, cut(): return array[top:top + rows]  2.04 us
  transfers between devices with their start and end apart: 26, of which 12 were waited for; matrix products, arithmetic and copies ran while one was open for 2% of the time, Pallas kernels for 4%

profile of v5, /device:TPU:0, one launch (start us, length us, event | category | flops | bytes accessed | tf_op | source)
XLA Modules:
  0.0 97.9 jit_solution(8639390541076607723)
XLA Ops:
  0.0 1.0 %collective-permute-start = (f32[512,256]{1,0:T(8,128)}, f32[512,256]{1,0:T(8,128)S(1)}, u32[]{:S(2)}, u32[]{:S(2)}) collective-permute-start(f32[512,256]{1,0:T(8,128)} %refs_0_.3), channel_id=1, source_target_pairs={{0,9},{1,8},{2,11},{3,10},{4,13},{5,12},{6,15},{7,14},{8,1},{9,0},... | collective-permute-start | bytes 1572872 | tf_op jit(solution)/shard_map/ppermute | solution.py:40
  1.0 2.2 %collective-permute-start.1 = (f32[512,256]{1,0:T(8,128)}, f32[512,256]{1,0:T(8,128)S(1)}, u32[]{:S(2)}, u32[]{:S(2)}) collective-permute-start(f32[512,256]{1,0:T(8,128)} %refs_0_.3), channel_id=1, source_target_pairs={{0,3},{1,2},{2,5},{3,4},{4,7},{5,6},{6,1},{7,0},{8,11},{9,10},{10,... | collective-permute-start | bytes 1572872 | tf_op jit(solution)/shard_map/ppermute | solution.py:40
  3.2 2.1 %collective-permute-start.2 = (f32[512,256]{1,0:T(8,128)}, f32[512,256]{1,0:T(8,128)S(1)}, u32[]{:S(2)}, u32[]{:S(2)}) collective-permute-start(f32[512,256]{1,0:T(8,128)} %refs_0_.3), channel_id=1, source_target_pairs={{0,7},{1,6},{2,1},{3,0},{4,3},{5,2},{6,5},{7,4},{8,15},{9,14},{10,... | collective-permute-start | bytes 1572872 | tf_op jit(solution)/shard_map/ppermute | solution.py:40
  5.4 1.0 %slice.26 = f32[320,256]{1,0:T(8,128)S(1)} slice(f32[512,256]{1,0:T(8,128)} %refs_6_.1), slice={[0:320], [0:256]} | slice | bytes 655360 | tf_op jit(solution)/shard_map/slice | solution.py:44
  6.4 2.8 %collective-permute-start.11 = (f32[320,256]{1,0:T(8,128)S(1)}, f32[320,256]{1,0:T(8,128)S(1)}, u32[]{:S(2)}, u32[]{:S(2)}) collective-permute-start(f32[320,256]{1,0:T(8,128)S(1)} %slice.26), channel_id=1, source_target_pairs={{0,16},{1,17},{2,18},{3,19},{4,20},{5,21},{6,22},{7,23},{8,24},{9,... | collective-permute-start | bytes 983048 | tf_op jit(solution)/shard_map/ppermute | solution.py:40
  9.2 0.9 slice.27
  10.1 0.9 collective-permute-start.14
  11.0 17.0 %collective-permute-done.14.refs_12_ = f32[192,256]{1,0:T(8,128)S(1)} collective-permute-done((f32[192,256]{1,0:T(8,128)S(1)}, f32[192,256]{1,0:T(8,128)S(1)}, u32[]{:S(2)}, u32[]{:S(2)}) %collective-permute-start.14) | collective-permute-done | bytes 196640 | tf_op jit(solution)/shard_map/ppermute | solution.py:40
  28.0 3.0 %collective-permute-start.16 = (f32[192,256]{1,0:T(8,128)S(1)}, f32[192,256]{1,0:T(8,128)S(1)}, u32[]{:S(2)}, u32[]{:S(2)}) collective-permute-start(f32[192,256]{1,0:T(8,128)S(1)} %collective-permute-done.14.refs_12_), channel_id=1, source_target_pairs={{0,96},{1,97},{2,98},{3,99},{4,100},{5,101},{6,102},{7,103},{8,104... | collective-permute-start | bytes 589832 | tf_op jit(solution)/shard_map/ppermute | solution.py:40
  31.0 4.4 %collective-permute-done.16.refs_14_ = f32[192,256]{1,0:T(8,128)S(1)} collective-permute-done((f32[192,256]{1,0:T(8,128)S(1)}, f32[192,256]{1,0:T(8,128)S(1)}, u32[]{:S(2)}, u32[]{:S(2)}) %collective-permute-start.16) | collective-permute-done | bytes 196640 | tf_op jit(solution)/shard_map/ppermute | solution.py:40
  35.4 3.7 %collective-permute-start.18 = (f32[512,256]{1,0:T(8,128)}, f32[512,256]{1,0:T(8,128)S(1)}, u32[]{:S(2)}, u32[]{:S(2)}) collective-permute-start(f32[512,256]{1,0:T(8,128)} %refs_6_.1), channel_id=1, source_target_pairs={{0,96},{1,97},{2,98},{3,99},{4,100},{5,101},{6,102},{7,103},{8,104... | collective-permute-start | bytes 1572872 | tf_op jit(solution)/shard_map/ppermute | solution.py:40
  39.1 0.6 collective-permute-start.5
  39.7 2.5 %collective-permute-start.6 = (f32[512,256]{1,0:T(8,128)S(1)}, f32[512,256]{1,0:T(8,128)S(1)}, u32[]{:S(2)}, u32[]{:S(2)}) collective-permute-start(f32[512,256]{1,0:T(8,128)S(1)} %collective-permute-done.refs_1_), channel_id=1, source_target_pairs={{0,7},{1,6},{2,1},{3,0},{4,3},{5,2},{6,5},{7,4},{8,15},{9,14},{10,... | collective-permute-start | bytes 1572872 | tf_op jit(solution)/shard_map/ppermute | solution.py:40
  42.3 8.0 %collective-permute-done.15.refs_13_ = f32[192,256]{1,0:T(8,128)S(1)} collective-permute-done((f32[192,256]{1,0:T(8,128)S(1)}, f32[192,256]{1,0:T(8,128)S(1)}, u32[]{:S(2)}, u32[]{:S(2)}) %collective-permute-start.15) | collective-permute-done | bytes 196640 | tf_op jit(solution)/shard_map/ppermute | solution.py:40
  50.8 2.4 %collective-permute-done.5.refs_5_ = f32[512,256]{1,0:T(8,128)S(1)} collective-permute-done((f32[512,256]{1,0:T(8,128)S(1)}, f32[512,256]{1,0:T(8,128)S(1)}, u32[]{:S(2)}, u32[]{:S(2)}) %collective-permute-start.5) | collective-permute-done | bytes 524320 | tf_op jit(solution)/shard_map/ppermute | solution.py:40
  53.2 3.2 %collective-permute-start.13 = (f32[320,256]{1,0:T(8,128)S(1)}, f32[320,256]{1,0:T(8,128)S(1)}, u32[]{:S(2)}, u32[]{:S(2)}) collective-permute-start(f32[320,256]{1,0:T(8,128)S(1)} %collective-permute-done.11.refs_11_), channel_id=1, source_target_pairs={{0,96},{1,97},{2,98},{3,99},{4,100},{5,101},{6,102},{7,103},{8,104... | collective-permute-start | bytes 983048 | tf_op jit(solution)/shard_map/ppermute | solution.py:40
  56.5 1.1 %collective-permute-start.10 = (f32[1024,256]{1,0:T(8,128)S(1)}, f32[1024,256]{1,0:T(8,128)S(1)}, u32[]{:S(2)}, u32[]{:S(2)}) collective-permute-start(f32[1024,256]{1,0:T(8,128)S(1)} %pad_maximum_fusion.1), channel_id=1, source_target_pairs={{0,1},{1,0},{2,3},{3,2},{4,5},{5,4},{6,7},{7,6},{8,9},{9,8},{10,11... | collective-permute-start | bytes 3145736 | tf_op jit(solution)/shard_map/ppermute | solution.py:40
  57.7 4.0 %collective-permute-done.12.refs_11_ = f32[320,256]{1,0:T(8,128)S(1)} collective-permute-done((f32[320,256]{1,0:T(8,128)S(1)}, f32[320,256]{1,0:T(8,128)S(1)}, u32[]{:S(2)}, u32[]{:S(2)}) %collective-permute-start.12) | collective-permute-done | bytes 327712 | tf_op jit(solution)/shard_map/ppermute | solution.py:40
  61.7 2.9 %collective-permute-start.4 = (f32[256,256]{1,0:T(8,128)S(1)}, f32[256,256]{1,0:T(8,128)S(1)}, u32[]{:S(2)}, u32[]{:S(2)}) collective-permute-start(f32[256,256]{1,0:T(8,128)S(1)} %slice.33), channel_id=1, source_target_pairs={{0,7},{1,6},{2,1},{3,0},{4,3},{5,2},{6,5},{7,4},{8,15},{9,14},{10,... | collective-permute-start | bytes 786440 | tf_op jit(solution)/shard_map/ppermute | solution.py:40
  65.1 2.7 %collective-permute-start.22 = (f32[256,256]{1,0:T(8,128)S(1)}, f32[256,256]{1,0:T(8,128)S(1)}, u32[]{:S(2)}, u32[]{:S(2)}) collective-permute-start(f32[256,256]{1,0:T(8,128)S(1)} %slice.37), channel_id=1, source_target_pairs={{0,7},{1,6},{2,1},{3,0},{4,3},{5,2},{6,5},{7,4},{8,15},{9,14},{10,... | collective-permute-start | bytes 786440 | tf_op jit(solution)/shard_map/ppermute | solution.py:40
  67.8 2.9 %collective-permute-done.4 = f32[256,256]{1,0:T(8,128)S(1)} collective-permute-done((f32[256,256]{1,0:T(8,128)S(1)}, f32[256,256]{1,0:T(8,128)S(1)}, u32[]{:S(2)}, u32[]{:S(2)}) %collective-permute-start.4) | collective-permute-done | bytes 262176 | tf_op jit(solution)/shard_map/ppermute | solution.py:40
  70.7 2.3 %collective-permute-done.21 = f32[256,256]{1,0:T(8,128)S(1)} collective-permute-done((f32[256,256]{1,0:T(8,128)S(1)}, f32[256,256]{1,0:T(8,128)S(1)}, u32[]{:S(2)}, u32[]{:S(2)}) %collective-permute-start.21) | collective-permute-done | bytes 262176 | tf_op jit(solution)/shard_map/ppermute | solution.py:40
  73.0 1.3 %collective-permute-start.9 = (f32[512,256]{1,0:T(8,128)S(1)}, f32[512,256]{1,0:T(8,128)S(1)}, u32[]{:S(2)}, u32[]{:S(2)}) collective-permute-start(f32[512,256]{1,0:T(8,128)S(1)} %constant_dynamic-update-slice_fusion.refs_4_), channel_id=1, source_target_pairs={{0,1},{1,0},{2,3},{3,2},{4,5},{5,4},{6,7},{7,6},{8,9},{9,8},{10,11... | collective-permute-start | bytes 1572872 | tf_op jit(solution)/shard_map/ppermute | solution.py:40
  74.3 2.0 %collective-permute-done.22 = f32[256,256]{1,0:T(8,128)S(1)} collective-permute-done((f32[256,256]{1,0:T(8,128)S(1)}, f32[256,256]{1,0:T(8,128)S(1)}, u32[]{:S(2)}, u32[]{:S(2)}) %collective-permute-start.22) | collective-permute-done | bytes 262176 | tf_op jit(solution)/shard_map/ppermute | solution.py:40
  76.3 1.4 %collective-permute-start.20 = (f32[256,256]{1,0:T(8,128)S(1)}, f32[256,256]{1,0:T(8,128)S(1)}, u32[]{:S(2)}, u32[]{:S(2)}) collective-permute-start(f32[256,256]{1,0:T(8,128)S(1)} %slice.35), channel_id=1, source_target_pairs={{0,96},{1,97},{2,98},{3,99},{4,100},{5,101},{6,102},{7,103},{8,104... | collective-permute-start | bytes 786440 | tf_op jit(solution)/shard_map/ppermute | solution.py:40
  77.7 3.0 %collective-permute-done.19.refs_9_ = f32[256,256]{1,0:T(8,128)S(1)} collective-permute-done((f32[256,256]{1,0:T(8,128)S(1)}, f32[256,256]{1,0:T(8,128)S(1)}, u32[]{:S(2)}, u32[]{:S(2)}) %collective-permute-start.19) | collective-permute-done | bytes 262176 | tf_op jit(solution)/shard_map/ppermute | solution.py:40
  80.9 4.3 %collective-permute-done.20.refs_10_ = f32[256,256]{1,0:T(8,128)S(1)} collective-permute-done((f32[256,256]{1,0:T(8,128)S(1)}, f32[256,256]{1,0:T(8,128)S(1)}, u32[]{:S(2)}, u32[]{:S(2)}) %collective-permute-start.20) | collective-permute-done | bytes 262176 | tf_op jit(solution)/shard_map/ppermute | solution.py:40
  85.2 3.2 %collective-permute-start.25 = (f32[192,256]{1,0:T(8,128)S(1)}, f32[192,256]{1,0:T(8,128)S(1)}, u32[]{:S(2)}, u32[]{:S(2)}) collective-permute-start(f32[192,256]{1,0:T(8,128)S(1)} %collective-permute-done.16.refs_14_), channel_id=1, source_target_pairs={{0,96},{1,97},{2,98},{3,99},{4,100},{5,101},{6,102},{7,103},{8,104... | collective-permute-start | bytes 589832 | tf_op jit(solution)/shard_map/ppermute | solution.py:40
  88.5 2.1 %shard_map.28 = (f32[512,256]{1,0:T(8,128)S(1)}, bf16[16,256,256]{2,1,0:T(8,128)(2,1)S(1)}, bf16[16,256,256]{2,1,0:T(8,128)(2,1)S(1)}) custom-call(f32[512,256]{1,0:T(8,128)S(1)} %copy-done, f32[512,256]{1,0:T(8,128)S(1)} %collective-permute-done.refs_1_, f32[512,256]{1,0:T(8,128)S(1)} %collective-permute-done.1.refs_2_, ...), custom_call_target="tpu_custom_call" | custom-call | flops 805306368 | bytes 2097152 | tf_op jit(solution)/shard_map/pallas_call | solution.py:234
  90.6 2.2 %shard_map.29 = (f32[512,256]{1,0:T(8,128)S(1)}, bf16[16,256,256]{2,1,0:T(8,128)(2,1)S(1)}, bf16[16,256,256]{2,1,0:T(8,128)(2,1)S(1)}, f32[2,512,256]{2,1,0:T(8,...) custom-call(f32[512,256]{1,0:T(8,128)S(1)} %copy-done, ...), custom_call_target="tpu_custom_call", output_to_operand_aliasing={{0}: (15, {}), {1}: (16, {}), {2}: (17, {})} | custom-call | flops 2013265920 | bytes 5242880 | tf_op jit(solution)/shard_map/pallas_call | solution.py:243
  92.9 3.1 %collective-permute-done.24.b0 = f32[320,256]{1,0:T(8,128)S(1)} collective-permute-done((f32[320,256]{1,0:T(8,128)S(1)}, f32[320,256]{1,0:T(8,128)S(1)}, u32[]{:S(2)}, u32[]{:S(2)}) %collective-permute-start.24) | collective-permute-done | bytes 327712 | tf_op jit(solution)/shard_map/ppermute | solution.py:40
  95.9 1.9 %shard_map.30 = f32[512,256]{1,0:T(8,128)} custom-call(f32[512,256]{1,0:T(8,128)S(1)} %get-tuple-element.15.total, f32[2,512,256]{2,1,0:T(8,128)S(1)} %get-tuple-element.16.held_left, bf16[2,256,256]{2,1,0:T(8,128)(2,1)S(1)} %get-tuple-element.17.held_high, bf16[2,256,256]{2,1,0:T(8,128)(2,1)S(1)} %get-tuple-element.18.held_low, ...), custom_call_target="tpu_custom_call" | custom-call | flops 805306368 | bytes 2097152 | tf_op jit(solution)/shard_map/pallas_call | solution.py:260
  (41 shorter events, 1.5 us)
Async XLA Ops:
  0.0 39.1 %collective-permute-start = (f32[512,256]{1,0:T(8,128)}, f32[512,256]{1,0:T(8,128)S(1)}, u32[]{:S(2)}, u32[]{:S(2)}) collective-permute-start(f32[512,256]{1,0:T(8,128)} %refs_0_.3), channel_id=1, source_target_pairs={{0,9},{1,8},{2,11},{3,10},{4,13},{5,12},{6,15},{7,14},{8,1},{9,0},... | collective-permute-start | bytes 1572872 | tf_op jit(solution)/shard_map/ppermute | solution.py:40
  1.0 38.1 %collective-permute-start.1 = (f32[512,256]{1,0:T(8,128)}, f32[512,256]{1,0:T(8,128)S(1)}, u32[]{:S(2)}, u32[]{:S(2)}) collective-permute-start(f32[512,256]{1,0:T(8,128)} %refs_0_.3), channel_id=1, source_target_pairs={{0,3},{1,2},{2,5},{3,4},{4,7},{5,6},{6,1},{7,0},{8,11},{9,10},{10,... | collective-permute-start | bytes 1572872 | tf_op jit(solution)/shard_map/ppermute | solution.py:40
  3.2 36.4 %collective-permute-start.2 = (f32[512,256]{1,0:T(8,128)}, f32[512,256]{1,0:T(8,128)S(1)}, u32[]{:S(2)}, u32[]{:S(2)}) collective-permute-start(f32[512,256]{1,0:T(8,128)} %refs_0_.3), channel_id=1, source_target_pairs={{0,7},{1,6},{2,1},{3,0},{4,3},{5,2},{6,5},{7,4},{8,15},{9,14},{10,... | collective-permute-start | bytes 1572872 | tf_op jit(solution)/shard_map/ppermute | solution.py:40
  6.4 24.6 %collective-permute-start.11 = (f32[320,256]{1,0:T(8,128)S(1)}, f32[320,256]{1,0:T(8,128)S(1)}, u32[]{:S(2)}, u32[]{:S(2)}) collective-permute-start(f32[320,256]{1,0:T(8,128)S(1)} %slice.26), channel_id=1, source_target_pairs={{0,16},{1,17},{2,18},{3,19},{4,20},{5,21},{6,22},{7,23},{8,24},{9,... | collective-permute-start | bytes 983048 | tf_op jit(solution)/shard_map/ppermute | solution.py:40
  10.1 40.2 %copy-start = (f32[512,256]{1,0:T(8,128)S(1)}, f32[512,256]{1,0:T(8,128)}, u32[]{:S(2)}) copy-start(f32[512,256]{1,0:T(8,128)} %refs_0_.3) | copy-start | bytes 1572868
  10.1 17.9 %collective-permute-start.14 = (f32[192,256]{1,0:T(8,128)S(1)}, f32[192,256]{1,0:T(8,128)S(1)}, u32[]{:S(2)}, u32[]{:S(2)}) collective-permute-start(f32[192,256]{1,0:T(8,128)S(1)} %slice.27), channel_id=1, source_target_pairs={{0,16},{1,17},{2,18},{3,19},{4,20},{5,21},{6,22},{7,23},{8,24},{9,... | collective-permute-start | bytes 589832 | tf_op jit(solution)/shard_map/ppermute | solution.py:40
  28.0 7.4 %collective-permute-start.16 = (f32[192,256]{1,0:T(8,128)S(1)}, f32[192,256]{1,0:T(8,128)S(1)}, u32[]{:S(2)}, u32[]{:S(2)}) collective-permute-start(f32[192,256]{1,0:T(8,128)S(1)} %collective-permute-done.14.refs_12_), channel_id=1, source_target_pairs={{0,96},{1,97},{2,98},{3,99},{4,100},{5,101},{6,102},{7,103},{8,104... | collective-permute-start | bytes 589832 | tf_op jit(solution)/shard_map/ppermute | solution.py:40
  31.0 19.3 %collective-permute-start.17 = (f32[512,256]{1,0:T(8,128)}, f32[512,256]{1,0:T(8,128)S(1)}, u32[]{:S(2)}, u32[]{:S(2)}) collective-permute-start(f32[512,256]{1,0:T(8,128)} %refs_6_.1), channel_id=1, source_target_pairs={{0,32},{1,33},{2,34},{3,35},{4,36},{5,37},{6,38},{7,39},{8,40},{9,... | collective-permute-start | bytes 1572872 | tf_op jit(solution)/shard_map/ppermute | solution.py:40
  35.4 15.4 %collective-permute-start.18 = (f32[512,256]{1,0:T(8,128)}, f32[512,256]{1,0:T(8,128)S(1)}, u32[]{:S(2)}, u32[]{:S(2)}) collective-permute-start(f32[512,256]{1,0:T(8,128)} %refs_6_.1), channel_id=1, source_target_pairs={{0,96},{1,97},{2,98},{3,99},{4,100},{5,101},{6,102},{7,103},{8,104... | collective-permute-start | bytes 1572872 | tf_op jit(solution)/shard_map/ppermute | solution.py:40
  39.1 11.2 %collective-permute-start.15 = (f32[192,256]{1,0:T(8,128)S(1)}, f32[192,256]{1,0:T(8,128)S(1)}, u32[]{:S(2)}, u32[]{:S(2)}) collective-permute-start(f32[192,256]{1,0:T(8,128)S(1)} %collective-permute-done.14.refs_12_), channel_id=1, source_target_pairs={{0,32},{1,33},{2,34},{3,35},{4,36},{5,37},{6,38},{7,39},{8,40},{9,... | collective-permute-start | bytes 589832 | tf_op jit(solution)/shard_map/ppermute | solution.py:40
  39.1 14.1 %collective-permute-start.5 = (f32[512,256]{1,0:T(8,128)S(1)}, f32[512,256]{1,0:T(8,128)S(1)}, u32[]{:S(2)}, u32[]{:S(2)}) collective-permute-start(f32[512,256]{1,0:T(8,128)S(1)} %collective-permute-done.refs_1_), channel_id=1, source_target_pairs={{0,3},{1,2},{2,5},{3,4},{4,7},{5,6},{6,1},{7,0},{8,11},{9,10},{10,... | collective-permute-start | bytes 1572872 | tf_op jit(solution)/shard_map/ppermute | solution.py:40
  39.7 16.7 %collective-permute-start.6 = (f32[512,256]{1,0:T(8,128)S(1)}, f32[512,256]{1,0:T(8,128)S(1)}, u32[]{:S(2)}, u32[]{:S(2)}) collective-permute-start(f32[512,256]{1,0:T(8,128)S(1)} %collective-permute-done.refs_1_), channel_id=1, source_target_pairs={{0,7},{1,6},{2,1},{3,0},{4,3},{5,2},{6,5},{7,4},{8,15},{9,14},{10,... | collective-permute-start | bytes 1572872 | tf_op jit(solution)/shard_map/ppermute | solution.py:40
  50.3 35.0 %collective-permute-start.8 = (f32[1536,256]{1,0:T(8,128)S(1)}, f32[1536,256]{1,0:T(8,128)S(1)}, u32[]{:S(2)}, u32[]{:S(2)}) collective-permute-start(f32[1536,256]{1,0:T(8,128)S(1)} %pad_maximum_fusion), channel_id=1, source_target_pairs={{0,1},{1,0},{2,3},{3,2},{4,5},{5,4},{6,7},{7,6},{8,9},{9,8},{10,11... | collective-permute-start | bytes 4718600 | tf_op jit(solution)/shard_map/ppermute | solution.py:40
  50.3 6.2 %collective-permute-start.7 = (f32[512,256]{1,0:T(8,128)S(1)}, f32[512,256]{1,0:T(8,128)S(1)}, u32[]{:S(2)}, u32[]{:S(2)}) collective-permute-start(f32[512,256]{1,0:T(8,128)S(1)} %copy-done), channel_id=1, source_target_pairs={{0,1},{1,0},{2,3},{3,2},{4,5},{5,4},{6,7},{7,6},{8,9},{9,8},{10,11... | collective-permute-start | bytes 1572872 | tf_op jit(solution)/shard_map/ppermute | solution.py:40
  50.8 10.9 %collective-permute-start.12 = (f32[320,256]{1,0:T(8,128)S(1)}, f32[320,256]{1,0:T(8,128)S(1)}, u32[]{:S(2)}, u32[]{:S(2)}) collective-permute-start(f32[320,256]{1,0:T(8,128)S(1)} %collective-permute-done.11.refs_11_), channel_id=1, source_target_pairs={{0,32},{1,33},{2,34},{3,35},{4,36},{5,37},{6,38},{7,39},{8,40},{9,... | collective-permute-start | bytes 983048 | tf_op jit(solution)/shard_map/ppermute | solution.py:40
  53.2 11.4 %collective-permute-start.13 = (f32[320,256]{1,0:T(8,128)S(1)}, f32[320,256]{1,0:T(8,128)S(1)}, u32[]{:S(2)}, u32[]{:S(2)}) collective-permute-start(f32[320,256]{1,0:T(8,128)S(1)} %collective-permute-done.11.refs_11_), channel_id=1, source_target_pairs={{0,96},{1,97},{2,98},{3,99},{4,100},{5,101},{6,102},{7,103},{8,104... | collective-permute-start | bytes 983048 | tf_op jit(solution)/shard_map/ppermute | solution.py:40
  56.4 8.7 %collective-permute-start.3 = (f32[256,256]{1,0:T(8,128)S(1)}, f32[256,256]{1,0:T(8,128)S(1)}, u32[]{:S(2)}, u32[]{:S(2)}) collective-permute-start(f32[256,256]{1,0:T(8,128)S(1)} %slice.32), channel_id=1, source_target_pairs={{0,3},{1,2},{2,5},{3,4},{4,7},{5,6},{6,1},{7,0},{8,11},{9,10},{10,... | collective-permute-start | bytes 786440 | tf_op jit(solution)/shard_map/ppermute | solution.py:40
  56.5 34.1 %collective-permute-start.10 = (f32[1024,256]{1,0:T(8,128)S(1)}, f32[1024,256]{1,0:T(8,128)S(1)}, u32[]{:S(2)}, u32[]{:S(2)}) collective-permute-start(f32[1024,256]{1,0:T(8,128)S(1)} %pad_maximum_fusion.1), channel_id=1, source_target_pairs={{0,1},{1,0},{2,3},{3,2},{4,5},{5,4},{6,7},{7,6},{8,9},{9,8},{10,11... | collective-permute-start | bytes 3145736 | tf_op jit(solution)/shard_map/ppermute | solution.py:40
  61.7 9.0 %collective-permute-start.4 = (f32[256,256]{1,0:T(8,128)S(1)}, f32[256,256]{1,0:T(8,128)S(1)}, u32[]{:S(2)}, u32[]{:S(2)}) collective-permute-start(f32[256,256]{1,0:T(8,128)S(1)} %slice.33), channel_id=1, source_target_pairs={{0,7},{1,6},{2,1},{3,0},{4,3},{5,2},{6,5},{7,4},{8,15},{9,14},{10,... | collective-permute-start | bytes 786440 | tf_op jit(solution)/shard_map/ppermute | solution.py:40
  64.6 8.4 %collective-permute-start.21 = (f32[256,256]{1,0:T(8,128)S(1)}, f32[256,256]{1,0:T(8,128)S(1)}, u32[]{:S(2)}, u32[]{:S(2)}) collective-permute-start(f32[256,256]{1,0:T(8,128)S(1)} %slice.36), channel_id=1, source_target_pairs={{0,3},{1,2},{2,5},{3,4},{4,7},{5,6},{6,1},{7,0},{8,11},{9,10},{10,... | collective-permute-start | bytes 786440 | tf_op jit(solution)/shard_map/ppermute | solution.py:40
  64.7 23.7 %copy-start.1 = (f32[512,256]{1,0:T(8,128)S(1)}, f32[512,256]{1,0:T(8,128)}, u32[]{:S(2)}) copy-start(f32[512,256]{1,0:T(8,128)} %refs_6_.1) | copy-start | bytes 1572868
  65.1 11.2 %collective-permute-start.22 = (f32[256,256]{1,0:T(8,128)S(1)}, f32[256,256]{1,0:T(8,128)S(1)}, u32[]{:S(2)}, u32[]{:S(2)}) collective-permute-start(f32[256,256]{1,0:T(8,128)S(1)} %slice.37), channel_id=1, source_target_pairs={{0,7},{1,6},{2,1},{3,0},{4,3},{5,2},{6,5},{7,4},{8,15},{9,14},{10,... | collective-permute-start | bytes 786440 | tf_op jit(solution)/shard_map/ppermute | solution.py:40
  70.7 10.1 %collective-permute-start.19 = (f32[256,256]{1,0:T(8,128)S(1)}, f32[256,256]{1,0:T(8,128)S(1)}, u32[]{:S(2)}, u32[]{:S(2)}) collective-permute-start(f32[256,256]{1,0:T(8,128)S(1)} %slice.34), channel_id=1, source_target_pairs={{0,32},{1,33},{2,34},{3,35},{4,36},{5,37},{6,38},{7,39},{8,40},{9,... | collective-permute-start | bytes 786440 | tf_op jit(solution)/shard_map/ppermute | solution.py:40
  73.0 17.5 %collective-permute-start.9 = (f32[512,256]{1,0:T(8,128)S(1)}, f32[512,256]{1,0:T(8,128)S(1)}, u32[]{:S(2)}, u32[]{:S(2)}) collective-permute-start(f32[512,256]{1,0:T(8,128)S(1)} %constant_dynamic-update-slice_fusion.refs_4_), channel_id=1, source_target_pairs={{0,1},{1,0},{2,3},{3,2},{4,5},{5,4},{6,7},{7,6},{8,9},{9,8},{10,11... | collective-permute-start | bytes 1572872 | tf_op jit(solution)/shard_map/ppermute | solution.py:40
  76.3 8.9 %collective-permute-start.20 = (f32[256,256]{1,0:T(8,128)S(1)}, f32[256,256]{1,0:T(8,128)S(1)}, u32[]{:S(2)}, u32[]{:S(2)}) collective-permute-start(f32[256,256]{1,0:T(8,128)S(1)} %slice.35), channel_id=1, source_target_pairs={{0,96},{1,97},{2,98},{3,99},{4,100},{5,101},{6,102},{7,103},{8,104... | collective-permute-start | bytes 786440 | tf_op jit(solution)/shard_map/ppermute | solution.py:40
  80.7 15.2 %collective-permute-start.23 = (f32[512,256]{1,0:T(8,128)S(1)}, f32[512,256]{1,0:T(8,128)S(1)}, u32[]{:S(2)}, u32[]{:S(2)}) collective-permute-start(f32[512,256]{1,0:T(8,128)S(1)} %constant_dynamic-update-slice_fusion.2.mine), channel_id=1, source_target_pairs={{0,1},{1,0},{2,3},{3,2},{4,5},{5,4},{6,7},{7,6},{8,9},{9,8},{10,11... | collective-permute-start | bytes 1572872 | tf_op jit(solution)/shard_map/ppermute | solution.py:40
  85.2 10.7 %collective-permute-start.24 = (f32[320,256]{1,0:T(8,128)S(1)}, f32[320,256]{1,0:T(8,128)S(1)}, u32[]{:S(2)}, u32[]{:S(2)}) collective-permute-start(f32[320,256]{1,0:T(8,128)S(1)} %collective-permute-done.12.refs_11_), channel_id=1, source_target_pairs={{0,32},{1,33},{2,34},{3,35},{4,36},{5,37},{6,38},{7,39},{8,40},{9,... | collective-permute-start | bytes 983048 | tf_op jit(solution)/shard_map/ppermute | solution.py:40
  85.2 7.6 %collective-permute-start.25 = (f32[192,256]{1,0:T(8,128)S(1)}, f32[192,256]{1,0:T(8,128)S(1)}, u32[]{:S(2)}, u32[]{:S(2)}) collective-permute-start(f32[192,256]{1,0:T(8,128)S(1)} %collective-permute-done.16.refs_14_), channel_id=1, source_target_pairs={{0,96},{1,97},{2,98},{3,99},{4,100},{5,101},{6,102},{7,103},{8,104... | collective-permute-start | bytes 589832 | tf_op jit(solution)/shard_map/ppermute | solution.py:40
